TPU v7x, 512 devices: a whole 4x8x8 slice. The times are simulated.
512 devices in a mesh: row: 32 (over y, x), col: 16 (over z, core).
Axes of the slice: x: 4, y: 8, z: 8, core: 2. Of those that a mesh axis runs over, the one named last changes fastest.
Arguments:
- ancestor: float32 [9, 9, 128, 2048], P(None, None, 'row', 'col'), may hold values from -1 to 4, as said below
- inverse_first: float32 [2, 2, 128, 2048], P(None, None, 'row', 'col'), may hold values from -1 to 2, as said below
- panel_first: float32 [1536, 2, 512], P('row', None, 'col'), may hold values from -0.15625 to 0.15625
- structure_first: int32 [1536], replicated, may hold values from 0 to 4607, as said below
- inverse_second: float32 [1, 1, 128, 2048], P(None, None, 'row', 'col'), may hold values from -1 to 2, as said below
- panel_second: float32 [1536, 1, 512], P('row', None, 'col'), may hold values from -0.15625 to 0.15625
- structure_second: int32 [1536], replicated, may hold values from 0 to 5631, as said below
Outputs:
- row_first: float32 [2, 11, 128, 2048], P(None, None, 'row', 'col')
- row_second: float32 [1, 12, 128, 2048], P(None, None, 'row', 'col')
Inputs may be any that keep to these rules, and one draw needn't show every extreme that they name: `ancestor`: symmetric and positive definite as a matrix. `inverse_first`: symmetric and positive definite as a matrix. `inverse_second`: symmetric and positive definite as a matrix. `structure_first`: entries are distinct; every aligned group of 16 ancestor rows holds at most 6 entries, and some group holds exactly 6. `structure_second`: entries are distinct; every aligned group of 16 ancestor rows holds at most 6 entries, and some group holds exactly 6.
All inputs are finite; a program needn't handle non-finite values.
Results may differ from a plain program's by a relative error of at most 0.000075.
Values sent between devices are 32-bit elements; how exact they have to be, the bound alone decides.
No kernel may reach another device: no remote copies, remote signals or barrier semaphores. Data moves between devices by JAX's collectives and lax.ppermute only.
A program may use at most 64 MiB of HBM per device.

v0:
```python
import jax
import jax.numpy as jnp
import numpy as np
from jax import lax
from jax.experimental import pallas as pl
from jax.experimental.pallas import tpu as pltpu
from jax.sharding import PartitionSpec as P

F32 = jnp.float32
BF16 = jnp.bfloat16
LINES = 40
TALL = 4 * LINES
SLOTS = 128
EXT = 16 * 2 * SLOTS

Y_GROUPS = [[4 * y + x for y in range(8)] for x in range(4)]
X_GROUPS = [[4 * y + x for x in range(4)] for y in range(8)]
Z_GROUPS = [[2 * z + k for z in range(8)] for k in range(2)]


def column_choice():
    table = np.zeros((96, 128), np.float32)
    for h in range(2):
        for m in range(32):
            al, k, q = m // 8, (m % 8) // 4, m % 4
            table[h * 48 + m, k * 32 + h * 16 + 4 * q + al] = 1
        for m in range(16):
            al, q = m // 4, m % 4
            table[h * 48 + 32 + m, 64 + h * 16 + 4 * q + al] = 1
    return table


def lane_order():
    table = np.zeros((512, 512), np.float32)
    for g in range(2):
        for al in range(4):
            for i in range(9):
                for q in range(4):
                    table[g * 256 + al * LINES + i * 4 + q, i * 32 + g * 16 + 4 * q + al] = 1
            for k in range(2):
                for q in range(4):
                    table[g * 256 + TALL + al * 8 + k * 4 + q, 384 + k * 32 + g * 16 + 4 * q + al] = 1
    return table


def dot(left, right):
    return jnp.dot(left, right, preferred_element_type=F32)


def halves(x):
    high = x.astype(BF16)
    return high, (x - high.astype(F32)).astype(BF16)


def thirds(x):
    high = x.astype(BF16)
    rest = x - high.astype(F32)
    mid = rest.astype(BF16)
    return high, mid, (rest - mid.astype(F32)).astype(BF16)


def product_terms(left, right):
    return dot(jnp.concatenate(halves(left), 0), jnp.concatenate(halves(right), 1))


def folded(terms):
    m, n = terms.shape[0] // 2, terms.shape[1] // 2
    return terms[:m, :n] + (terms[:m, n:] + terms[m:, :n])


def chosen(x, table):
    m = x.shape[0]
    out = dot(jnp.concatenate(thirds(x), 0), table)
    return out[:m] + (out[m : 2 * m] + out[2 * m :])


def lanes_of(shape):
    return lax.broadcasted_iota(jnp.int32, shape, len(shape) - 1)


def rank_body(where, s1, s2, tiles, packed, slot1, slot2, table, lhs, rhs, stage):
    col = where[1]
    upper = (
        lax.broadcasted_iota(jnp.int32, (128, 128), 0) < lax.broadcasted_iota(jnp.int32, (128, 128), 1)
    ).astype(BF16)
    groups = lax.broadcasted_iota(jnp.int32, (16, 128), 0)
    ranks = []
    for which, (source, target) in enumerate(((s1, slot1), (s2, slot2))):
        carry = jnp.zeros((16, 1), F32)
        rank = []
        for m in range(12):
            row = source[m : m + 1, :]
            group = jnp.bitwise_and(lax.shift_right_logical(row, 5), 15)
            inside = row < 4608
            mark = ((group == groups) & inside).astype(F32)
            before = dot(mark.astype(BF16), upper) + carry
            t = jnp.sum(mark * before, axis=0, keepdims=True)
            carry = carry + jnp.sum(mark, axis=1, keepdims=True)
            rank.append(t + 1.0)
            place = group * (2 * SLOTS) + which * SLOTS + t.astype(jnp.int32)
            if which:
                high = lax.shift_right_logical(row - 4608, 9)
                other = EXT + group * 64 + high * 32 + jnp.bitwise_and(row, 31)
                place = jnp.where(inside, place, other)
            target[m : m + 1, :] = place
        ranks.append(rank)
    slots = lanes_of((32, 128)).astype(F32)
    table[288:, :] = jnp.zeros((96, 256), BF16)
    for j in range(9):
        spots = lax.broadcasted_iota(jnp.int32, (32, 128), 0) + (j * 512 + col * 32)
        both = []
        for source, rank in ((s1, ranks[0]), (s2, ranks[1])):
            total = jnp.zeros((32, 128), F32)
            for m in range(12):
                total = total + jnp.where(source[m : m + 1, :] == spots, rank[m], 0.0)
            slot = jnp.sum(total, axis=1, keepdims=True) - 1.0
            both.append((slot == slots).astype(BF16))
        pair = jnp.concatenate(both, 1)
        table[j * 32 : (j + 1) * 32, :] = pair
        for al in range(4):
            rhs[j * 128 + al * 32 : j * 128 + (al + 1) * 32, :] = pair
        stage[...] = jnp.zeros((LINES, 128), F32)
        for i in range(9):
            stage[i * 4 : (i + 1) * 4, :] = tiles[i, j]
        x = stage[...]
        quarter = lanes_of((LINES, 128)) // 32
        x = jnp.concatenate([jnp.where(quarter == al, x, 0.0) for al in range(4)], 0)
        for part, value in enumerate(thirds(x)):
            lhs[part * TALL : (part + 1) * TALL, j * 128 : (j + 1) * 128] = value
    out = dot(lhs[...], rhs[...])
    packed[...] = out[:TALL] + (out[TALL : 2 * TALL] + out[2 * TALL :])


def second_body(slot2, panels, mixed, spread, fold, extra):
    spread[...] = jnp.zeros(spread.shape, F32)

    def place(step, _):
        x, y = step // 8, step % 8
        base = (y * 4 + x) * 48
        for u in range(48):
            spread[pl.ds(slot2[base + u], 1), :] = panels[x, y, u : u + 1, :]
        return 0

    lax.fori_loop(0, 32, place, 0)
    lane = lanes_of((40, 128))
    lane_r = lanes_of((64, 128))
    total = jnp.zeros((160, 256), F32)
    for c in range(16):
        x = mixed[c]
        left = jnp.concatenate([jnp.where(lane < 64, x, 0.0), jnp.where(lane >= 64, x, 0.0)], 0)
        right = spread[EXT + c * 64 : EXT + (c + 1) * 64, :]
        right = jnp.where((lane_r >= 64) & (lane_r < 96), right, 0.0)
        total = total + product_terms(left, jnp.concatenate([right, right], 0))
    out = folded(total)
    lane_f = lanes_of((16, 128))
    value = jnp.zeros((16, 128), F32)
    for h in range(3):
        moved = pltpu.roll(out[16 * h : 16 * (h + 1), :], (32 * h - 64) % 128, 1)
        value = jnp.where(lane_f // 32 == h, moved, value)
    fold[...] = value
    extra[...] = out[48:80, :]


def image_body(where, slot1, panels, fold, spread, blocks, extra, choice, right, send, comb):
    lane = lanes_of((16, 128))

    def join(step, _):
        x, y = step // 8, step % 8
        base = pl.multiple_of((y * 4 + x) * 48, 16)
        q = -fold[x, y]
        for h in range(3):
            moved = pltpu.roll(q, (64 - 32 * h) % 128, 1)
            value = jnp.where(lane < 64, panels[x, y, 16 * h : 16 * (h + 1), :], jnp.where(lane < 96, moved, 0.0))
            comb[pl.ds(base + 16 * h, 16), :] = value
        return 0

    lax.fori_loop(0, 32, join, 0)
    lane_r = lanes_of((SLOTS, 128))
    for c in range(16):
        low = c * 2 * SLOTS
        right[low : low + SLOTS, :] = jnp.zeros((SLOTS, 128), F32)
        value = spread[low + SLOTS : low + 2 * SLOTS, :]
        right[low + SLOTS : low + 2 * SLOTS, :] = jnp.where((lane_r >= 64) & (lane_r < 96), value, 0.0)

    def place(step, _):
        base = pl.multiple_of(step * 48, 16)
        for u in range(48):
            right[pl.ds(slot1[base + u], 1), :] = comb[pl.ds(base + u, 1), :]
        return 0

    lax.fori_loop(0, 32, place, 0)
    total = jnp.zeros((2 * TALL, 256), F32)
    for c in range(16):
        total = total + product_terms(blocks[c], right[c * 256 : (c + 1) * 256, :])
    image = jnp.concatenate([folded(total), extra[...]], 0)
    sent = jnp.zeros((96, TALL + 32), F32)
    for part in thirds(image):
        sent = sent + lax.dot_general(choice[...], part, (((1,), (1,)), ((), ())), preferred_element_type=F32)
    sent = jnp.concatenate([sent, jnp.zeros((96, 256 - TALL - 32), F32)], 1)
    parity = where[0] % 2
    for h in range(2):
        send[pl.ds((h + parity) % 2, 1)] = sent[h * 48 : (h + 1) * 48][None]


def cross_body(where, got0, got1, order, table, first, second, share, own):
    parity = where[0] % 2
    a, b = got0[...], got1[...]
    even = jnp.where(parity == 0, a, b)
    odd = jnp.where(parity == 0, b, a)
    y = chosen(jnp.concatenate([even, odd], 1), order[...])
    close = chosen(y[:, :384], table[...])
    share[0:48, :] = close[:, :128]
    share[48:64, :] = close[32:48, 128:]
    e = y[32:48, 384:512]
    own[...] = e
    lane = lanes_of((8, 128))
    share[64:72, :] = jnp.where(lane < 64, e[:8], pltpu.roll(e[8:], 64, 1))
    lane2 = lanes_of((4, 128))
    for i in range(9):
        chunk = (i // 4) * 128
        one = jnp.zeros((8, 128), F32)
        two = jnp.zeros((4, 128), F32)
        for al in range(4):
            shift = ((al - i % 4) * 32) % 128
            moved = pltpu.roll(y[al * 8 : (al + 1) * 8, chunk : chunk + 128], shift, 1) if shift else y[al * 8 : (al + 1) * 8, chunk : chunk + 128]
            one = jnp.where(lane // 32 == al, moved, one)
            low = y[32 + al * 4 : 36 + al * 4, chunk : chunk + 128]
            moved = pltpu.roll(low, shift, 1) if shift else low
            two = jnp.where(lane2 // 32 == al, moved, two)
        first[0, i] = -one[0:4]
        first[1, i] = -one[4:8]
        second[0, i] = -two


def diagonal_body(shares, right, spread, own, d1, d2, first, second):
    lane_r = lanes_of((64, 128))
    lane_e = lanes_of((8, 128))
    total = jnp.zeros((128, 256), F32)
    also = jnp.zeros((32, 256), F32)
    for c in range(16):
        x = shares[c]
        zero = jnp.zeros((48, 128), F32)
        left = jnp.concatenate(
            [jnp.concatenate([x[:48], zero], 1), jnp.concatenate([zero[:16], x[48:64]], 1)], 0
        )
        total = total + product_terms(left, right[c * 256 : (c + 1) * 256, :])
        e = x[64:72]
        left = jnp.concatenate([jnp.where(lane_e < 64, e, 0.0), jnp.where(lane_e >= 64, e, 0.0)], 0)
        v = spread[EXT + c * 64 : EXT + (c + 1) * 64, :]
        v = jnp.where((lane_r >= 64) & (lane_r < 96), v, 0.0)
        also = also + product_terms(left, jnp.concatenate([v, v], 0))
    out = folded(total)
    g1 = out[:32]
    bottom = own[...] - out[32:48]
    g2 = out[32:48] + out[48:64] + folded(also)
    lane = lanes_of((8, 128))
    lane2 = lanes_of((4, 128))
    for k in range(2):
        one = jnp.zeros((8, 128), F32)
        two = jnp.zeros((4, 128), F32)
        for al in range(4):
            shift = ((al - k) * 32) % 128
            one = jnp.where(lane // 32 == al, pltpu.roll(g1[al * 8 : (al + 1) * 8], shift, 1), one)
            two = jnp.where(lane2 // 32 == al, pltpu.roll(bottom[al * 4 : (al + 1) * 4], shift, 1), two)
        first[0, k] = d1[0, k] + one[0:4]
        first[1, k] = d1[1, k] + one[4:8]
        second[0, k] = -two
    two = jnp.zeros((4, 128), F32)
    for al in range(4):
        shift = ((al - 2) * 32) % 128
        two = jnp.where(lane2 // 32 == al, pltpu.roll(g2[al * 4 : (al + 1) * 4], shift, 1), two)
    second[0, 2] = d2[0, 0] + two


VMEM = pl.BlockSpec(memory_space=pltpu.VMEM)
SMEM = pl.BlockSpec(memory_space=pltpu.SMEM)


def kernel(body, specs, outs, scratch=()):
    return pl.pallas_call(
        body,
        in_specs=list(specs),
        out_specs=[VMEM] * len(outs),
        out_shape=[jax.ShapeDtypeStruct(shape, dtype) for shape, dtype in outs],
        scratch_shapes=list(scratch),
    )


def from_all(x, axis, count, groups=None):
    copies = jnp.broadcast_to(x, (count, *x.shape))
    return lax.all_to_all(copies, axis, 0, 0, axis_index_groups=groups, tiled=True)


def along_rows(x):
    return from_all(from_all(x, "row", 8, Y_GROUPS), "row", 4, X_GROUPS)


def along_cols(x):
    return from_all(x, "col", 16)


def transposed(x, turn):
    pairs = [(r * 16 + c, (2 * c + (r + turn) % 2) * 16 + r // 2) for r in range(32) for c in range(16)]
    return lax.ppermute(x, ("row", "col"), pairs)


def on_device(ancestor, inverse_first, panel_first, structure_first, inverse_second, panel_second, structure_second):
    where = jnp.stack([lax.axis_index("row"), lax.axis_index("col")]).astype(jnp.int32)
    p1 = panel_first.reshape(48, 64)
    p2 = panel_second.reshape(48, 32)
    panel = jnp.concatenate([p1, p2, jnp.zeros((48, 32), F32)], 1)
    d1 = inverse_first.reshape(2, 2, 4, 4, 32).transpose(3, 0, 2, 1, 4).reshape(32, 64)
    stacked = jnp.concatenate([p1, d1], 0)
    mixed = jnp.concatenate([stacked[:40], stacked[40:]], 1)

    packed, slot1, slot2, table = kernel(
        rank_body,
        (SMEM, VMEM, VMEM, VMEM),
        (((TALL, 256), F32), ((12, 128), jnp.int32), ((12, 128), jnp.int32), ((384, 256), BF16)),
        (pltpu.VMEM((3 * TALL, 1152), BF16), pltpu.VMEM((1152, 256), BF16), pltpu.VMEM((LINES, 128), F32)),
    )(where, structure_first.reshape(12, 128), structure_second.reshape(12, 128), ancestor)
    blocks = lax.all_gather(packed, "col")
    panels = along_rows(panel)
    mixes = along_cols(mixed)
    slot1, slot2 = slot1.reshape(1536), slot2.reshape(1536)
    spread, fold, extra = kernel(
        second_body,
        (SMEM, VMEM, VMEM),
        (((EXT + 1024, 128), F32), ((16, 128), F32), ((32, 128), F32)),
    )(slot2, panels, mixes)
    folds = along_rows(fold)
    right, send = kernel(
        image_body,
        (SMEM, SMEM, VMEM, VMEM, VMEM, VMEM, VMEM, VMEM),
        (((EXT, 128), F32), ((2, 48, 256), F32)),
        (pltpu.VMEM((1536, 128), F32),),
    )(where, slot1, panels, folds, spread, blocks, extra, jnp.asarray(column_choice(), BF16))
    got0, got1 = transposed(send[0], 0), transposed(send[1], 1)
    first_left, second_left, share, own = kernel(
        cross_body,
        (SMEM, VMEM, VMEM, VMEM, VMEM),
        (((2, 9, 4, 128), F32), ((1, 9, 4, 128), F32), ((72, 128), F32), ((16, 128), F32)),
    )(where, got0, got1, jnp.asarray(lane_order(), BF16), table)
    shares = along_cols(share)
    first_right, second_right = kernel(
        diagonal_body,
        (VMEM,) * 6,
        (((2, 2, 4, 128), F32), ((1, 3, 4, 128), F32)),
    )(shares, right, spread, own, inverse_first, inverse_second)
    return (
        jnp.concatenate([first_left, first_right], 1),
        jnp.concatenate([second_left, second_right], 1),
    )


def solution(mesh):
    tiles = P(None, None, "row", "col")
    panels = P("row", None, "col")
    return jax.shard_map(
        on_device,
        mesh=mesh,
        in_specs=(tiles, tiles, panels, P(), tiles, panels, P()),
        out_specs=(tiles, tiles),
        check_vma=False,
    )
```

profile of v0, /device:TPU:1, one launch (start us, length us, event | category | flops | bytes accessed | tf_op | source)
XLA Modules:
  0.0 172.1 jit_solution(15946011164500332949)
XLA Ops:
  7.2 0.0 all-gather.3.cloned.1.call-start
  7.2 0.6 pad_add_fusion.where
  7.8 2.9 %shard_map.104 = (f32[160,256]{1,0:T(8,128)}, s32[12,128]{1,0:T(8,128)}, s32[12,128]{1,0:T(8,128)}, bf16[384,256]{1,0:T(8,128)(2,1)}) custom-call(s32[2]{0:T(128)} %pad_add_fusion.where, s32[12,128]{1,0:T(8,128)} %bitcast.26, s32[12,128]{1,0:T(8,128)} %bitcast.27, f32[9,9,4,128]{3,2,1,0:T(4,128)} %tiles.1), custom_call_target="tpu_custom_call" | custom-call | tf_op jit(solution)/shard_map/pallas_call | solution.py:316
  10.7 0.0 all-gather.3.cloned.1.call-update
  10.7 0.8 copy.28
  11.5 0.8 copy.29
  12.3 0.1 pad.10.clone
  12.4 0.1 maximum_maximum_fusion
  12.5 0.7 broadcast_in_dim.22
  13.2 7.6 %all-to-all-start = ((f32[8,48,128]{2,1,0:T(8,128)}), f32[8,48,128]{2,1,0:T(8,128)S(1)}, u32[]{:S(2)}, u32[]{:S(2)}) async-start(f32[8,48,128]{2,1,0:T(8,128)} %broadcast_in_dim.22), calls=%async_computation | async-start | bytes 393216 | tf_op jit(solution)/shard_map/all_to_all | solution.py:291
  20.8 0.8 copy.32
  21.7 0.8 reshape.35
  22.5 0.1 reshape.36
  22.6 0.1 copy.31
  22.7 0.8 pad_maximum_fusion.1
  23.5 0.1 copy.33
  23.6 0.1 pad_maximum_fusion.3
  23.7 5.9 %all-to-all-done = f32[8,48,128]{2,1,0:T(8,128)S(1)} async-done(((f32[8,48,128]{2,1,0:T(8,128)}), f32[8,48,128]{2,1,0:T(8,128)S(1)}, u32[]{:S(2)}, u32[]{:S(2)}) %all-to-all-start) | async-done | bytes 196640 | tf_op jit(solution)/shard_map/all_to_all | solution.py:291
  29.6 27.7 %all_to_all.30.mixed = f32[16,40,128]{2,1,0:T(8,128)} all-to-all(f32[16,40,128]{2,1,0:T(8,128)S(1)} %broadcast_in_dim.24), channel_id=1, replica_groups=mesh['row'=32,'col'=16] {'col'}, dimensions={0} | all-to-all | bytes 655360 | tf_op jit(solution)/shard_map/all_to_all | solution.py:291
  57.3 0.1 broadcast_in_dim.23
  57.4 16.2 %all_to_all.31.panels = f32[4,8,48,128]{3,2,1,0:T(8,128)} all-to-all(f32[4,8,48,128]{3,2,1,0:T(8,128)S(1)} %broadcast_in_dim.23), channel_id=1, replica_groups={{0,16,32,48},{64,80,96,112},{128,144,160,176},{192,208,224,240},{256,27..., dimensions={0} | all-to-all | bytes 1572864 | tf_op jit(solution)/shard_map/all_to_all | solution.py:291
  73.6 4.4 %shard_map.105 = (f32[5120,128]{1,0:T(8,128)}, f32[16,128]{1,0:T(8,128)}, f32[32,128]{1,0:T(8,128)}) custom-call(s32[1536]{0:T(1024)} %bitcast.25, f32[4,8,48,128]{3,2,1,0:T(8,128)} %all_to_all.31.panels, f32[16,40,128]{2,1,0:T(8,128)} %all_to_all.30.mixed), custom_call_target="tpu_custom_call" | custom-call | tf_op jit(solution)/shard_map/pallas_call | solution.py:326
  78.0 0.7 broadcast_in_dim.25
  78.7 9.7 %all_to_all.32 = f32[8,16,128]{2,1,0:T(8,128)S(1)} all-to-all(f32[8,16,128]{2,1,0:T(8,128)S(1)} %broadcast_in_dim.25), channel_id=1, replica_groups={{0,64,128,192,256,320,384,448},{16,80,144,208,272,336,400,464},{32,96,1..., dimensions={0} | all-to-all | bytes 131072 | tf_op jit(solution)/shard_map/all_to_all | solution.py:291
  88.5 8.6 %all_to_all.33.fold = f32[4,8,16,128]{3,2,1,0:T(8,128)} all-to-all(f32[4,8,16,128]{3,2,1,0:T(8,128)S(1)} %broadcast_in_dim.26), channel_id=1, replica_groups={{0,16,32,48},{64,80,96,112},{128,144,160,176},{192,208,224,240},{256,27..., dimensions={0} | all-to-all | bytes 524288 | tf_op jit(solution)/shard_map/all_to_all | solution.py:291
  97.1 0.0 all-gather.3.cloned.1.call-done
  97.1 8.7 %shard_map.106 = (f32[4096,128]{1,0:T(8,128)}, f32[2,48,256]{2,1,0:T(8,128)}) custom-call(s32[2]{0:T(128)} %pad_add_fusion.where, s32[1536]{0:T(1024)} %bitcast.24, f32[4,8,48,128]{3,2,1,0:T(8,128)} %all_to_all.31.panels, f32[4,8,16,128]{3,2,1,0:T(8,128)} %all_to_all.33.fold, f32[5120,128]{1,0:T(8,128)} %get-tuple-element.20.spread, ...), custom_call_target="tpu_custom_call" | custom-call | tf_op jit(solution)/shard_map/pallas_call | solution.py:332
  105.8 0.8 slice_bitcast_fusion
  106.6 6.4 %collective-permute-start.1 = (f32[48,256]{1,0:T(8,128)S(1)}, f32[48,256]{1,0:T(8,128)S(1)}, u32[]{:S(2)}, u32[]{:S(2)}) collective-permute-start(f32[48,256]{1,0:T(8,128)S(1)} %get-tuple-element.32), channel_id=1, source_target_pairs={{0,16},{1,48},{2,80},{3,112},{4,144},{5,176},{6,208},{7,240},{8,27... | collective-permute-start | bytes 147464 | tf_op jit(solution)/shard_map/ppermute | solution.py:304
  113.1 1.9 %collective-permute-start = (f32[48,256]{1,0:T(8,128)S(1)}, f32[48,256]{1,0:T(8,128)S(1)}, u32[]{:S(2)}, u32[]{:S(2)}) collective-permute-start(f32[48,256]{1,0:T(8,128)S(1)} %get-tuple-element.33), channel_id=1, source_target_pairs={{0,0},{1,32},{2,64},{3,96},{4,128},{5,160},{6,192},{7,224},{8,256}... | collective-permute-start | bytes 147464 | tf_op jit(solution)/shard_map/ppermute | solution.py:304
  115.0 0.0 collective-permute-done.1.got1
  115.0 0.0 copy-start
  115.0 5.0 %collective-permute-done.got0 = f32[48,256]{1,0:T(8,128)S(1)} collective-permute-done((f32[48,256]{1,0:T(8,128)S(1)}, f32[48,256]{1,0:T(8,128)S(1)}, u32[]{:S(2)}, u32[]{:S(2)}) %collective-permute-start) | collective-permute-done | bytes 49184 | tf_op jit(solution)/shard_map/ppermute | solution.py:304
  120.0 0.0 copy-start.1
  120.0 0.0 copy-done
  120.0 0.6 copy-done.1
  120.6 2.2 %shard_map.107 = (f32[2,9,4,128]{3,2,1,0:T(4,128)}, f32[1,9,4,128]{3,2,1,0:T(4,128)}, f32[72,128]{1,0:T(8,128)}, f32[16,128]{1,0:T(8,128)}) custom-call(s32[2]{0:T(128)} %pad_add_fusion.where, f32[48,256]{1,0:T(8,128)} %copy-done.1, f32[48,256]{1,0:T(8,128)} %copy-done, bf16[512,512]{1,0:T(8,128)(2,1)} %constant.16.clone.order, ...), custom_call_target="tpu_custom_call" | custom-call | tf_op jit(solution)/shard_map/pallas_call | solution.py:339
  122.8 0.8 broadcast_in_dim.27
  123.6 35.1 %all_to_all.34.shares = f32[16,72,128]{2,1,0:T(8,128)} all-to-all(f32[16,72,128]{2,1,0:T(8,128)S(1)} %broadcast_in_dim.27), channel_id=1, replica_groups=mesh['row'=32,'col'=16] {'col'}, dimensions={0} | all-to-all | bytes 1179648 | tf_op jit(solution)/shard_map/all_to_all | solution.py:291
  158.7 0.0 copy-start.2
  158.7 0.0 copy-start.3
  158.7 3.9 %shard_map.108 = (f32[2,2,4,128]{3,2,1,0:T(4,128)}, f32[1,3,4,128]{3,2,1,0:T(4,128)}) custom-call(f32[16,72,128]{2,1,0:T(8,128)} %all_to_all.34.shares, f32[4096,128]{1,0:T(8,128)} %get-tuple-element.27.right, f32[5120,128]{1,0:T(8,128)} %get-tuple-element.20.spread, f32[16,128]{1,0:T(8,128)} %get-tuple-element.28.own, f32[2,2,4,128]{3,2,1,0:T(4,128)} %d1.1, ...), custom_call_target="tpu_custom_call" | custom-call | tf_op jit(solution)/shard_map/pallas_call | solution.py:345
  162.6 0.0 copy-done.2
  162.6 1.3 pad_maximum_fusion
  163.9 0.0 copy-done.3
  163.9 1.3 pad_maximum_fusion.2
  (4 shorter events, 0.1 us)
Async XLA Ops:
  7.2 89.9 %all-gather.3.cloned.1.call-start = ((), (), s32[]{:S(2)}) async-start(), calls=%async_computation.6 | async-start | bytes 2785280 | tf_op jit(solution)/shard_map/all_gather | solution.py:322
  13.2 16.4 %all-to-all-start = ((f32[8,48,128]{2,1,0:T(8,128)}), f32[8,48,128]{2,1,0:T(8,128)S(1)}, u32[]{:S(2)}, u32[]{:S(2)}) async-start(f32[8,48,128]{2,1,0:T(8,128)} %broadcast_in_dim.22), calls=%async_computation | async-start | bytes 393216 | tf_op jit(solution)/shard_map/all_to_all | solution.py:291
  106.6 8.4 %collective-permute-start.1 = (f32[48,256]{1,0:T(8,128)S(1)}, f32[48,256]{1,0:T(8,128)S(1)}, u32[]{:S(2)}, u32[]{:S(2)}) collective-permute-start(f32[48,256]{1,0:T(8,128)S(1)} %get-tuple-element.32), channel_id=1, source_target_pairs={{0,16},{1,48},{2,80},{3,112},{4,144},{5,176},{6,208},{7,240},{8,27... | collective-permute-start | bytes 147464 | tf_op jit(solution)/shard_map/ppermute | solution.py:304
  113.1 6.9 %collective-permute-start = (f32[48,256]{1,0:T(8,128)S(1)}, f32[48,256]{1,0:T(8,128)S(1)}, u32[]{:S(2)}, u32[]{:S(2)}) collective-permute-start(f32[48,256]{1,0:T(8,128)S(1)} %get-tuple-element.33), channel_id=1, source_target_pairs={{0,0},{1,32},{2,64},{3,96},{4,128},{5,160},{6,192},{7,224},{8,256}... | collective-permute-start | bytes 147464 | tf_op jit(solution)/shard_map/ppermute | solution.py:304
  115.0 5.0 %copy-start = (f32[48,256]{1,0:T(8,128)}, f32[48,256]{1,0:T(8,128)S(1)}, u32[]{:S(2)}) copy-start(f32[48,256]{1,0:T(8,128)S(1)} %collective-permute-done.1.got1) | copy-start | bytes 147460
  120.0 0.6 copy-start.1
  158.7 3.9 %copy-start.2 = (f32[2,9,4,128]{3,2,1,0:T(4,128)S(1)}, f32[2,9,4,128]{3,2,1,0:T(4,128)}, u32[]{:S(2)}) copy-start(f32[2,9,4,128]{3,2,1,0:T(4,128)} %get-tuple-element.25) | copy-start | bytes 110596
  158.7 5.2 %copy-start.3 = (f32[1,9,4,128]{3,2,1,0:T(4,128)S(1)}, f32[1,9,4,128]{3,2,1,0:T(4,128)}, u32[]{:S(2)}) copy-start(f32[1,9,4,128]{3,2,1,0:T(4,128)} %get-tuple-element.30) | copy-start | bytes 55300
Sparse Core Ops, SparseCore 0:
  10.8 53.6 all-gather.2
where the time goes:
time: 173 us; the launch traced here: 172 us
  blocking collectives  97.4 us (56%)
  Pallas kernels  22.1 us (13%)
  starting transfers between devices  16 us (9%)
  between operations  14.1 us (8%)
  waiting for transfers between devices  10.9 us (6%)
  local copies, waits for them, and re-layouts  7.33 us (4%)
  other arithmetic  4.24 us (2%)
    all_to_all x5, blocking collectives, from_all(): lax.all_to_all(copies, axis, 0, 0, axis_index_groups=groups, tiled=True)  97.4 us
    pallas_call x1, Pallas kernels, on_device(): kernel(image_body, (SMEM, SMEM, VMEM, VMEM, VMEM, VMEM, VMEM, VMEM), (((E...  8.71 us
    ppermute x2, starting transfers between devices, transposed(): return lax.ppermute(x, ('row', 'col'), pairs)  8.37 us
    all_to_all x1, starting transfers between devices, from_all(): lax.all_to_all(copies, axis, 0, 0, axis_index_groups=groups, tiled=True)  7.64 us
    all_to_all x1, waiting for transfers between devices, from_all(): lax.all_to_all(copies, axis, 0, 0, axis_index_groups=groups, tiled=True)  5.92 us
    ppermute x2, waiting for transfers between devices, transposed(): return lax.ppermute(x, ('row', 'col'), pairs)  4.97 us
    pallas_call x1, Pallas kernels, on_device(): kernel(second_body, (SMEM, VMEM, VMEM), (((EXT + 1024, 128), F32), ((16,...  4.43 us
    pallas_call x1, Pallas kernels, on_device(): kernel(diagonal_body, (VMEM,) * 6, (((2, 2, 4, 128), F32), ((1, 3, 4, 128...  3.86 us
  transfers between devices with their start and end apart: 4, of which 2 were waited for; matrix products, arithmetic and copies ran while one was open for 4% of the time, Pallas kernels for 3%

commit v1 on v0

--- a/solution.py
+++ b/solution.py
@@ -11,7 +11,7 @@
 LINES = 40
 TALL = 4 * LINES
 SLOTS = 128
-EXT = 16 * 2 * SLOTS
+EXT = 16 * SLOTS
 
 Y_GROUPS = [[4 * y + x for y in range(8)] for x in range(4)]
 X_GROUPS = [[4 * y + x for x in range(4)] for y in range(8)]
@@ -97,7 +97,7 @@
             t = jnp.sum(mark * before, axis=0, keepdims=True)
             carry = carry + jnp.sum(mark, axis=1, keepdims=True)
             rank.append(t + 1.0)
-            place = group * (2 * SLOTS) + which * SLOTS + t.astype(jnp.int32)
+            place = group * SLOTS + t.astype(jnp.int32)
             if which:
                 high = lax.shift_right_logical(row - 4608, 9)
                 other = EXT + group * 64 + high * 32 + jnp.bitwise_and(row, 31)
@@ -131,67 +131,109 @@
     packed[...] = out[:TALL] + (out[TALL : 2 * TALL] + out[2 * TALL :])
 
 
-def second_body(slot2, panels, mixed, spread, fold, extra):
+def lay_body(p1, p2, d1, panel, mixed, tall):
+    tall[...] = jnp.zeros((128, 128), F32)
+    tall[0:32, 0:48] = p1[0]
+    tall[32:64, 0:48] = p1[1]
+    tall[64:96, 0:48] = p2[0]
+    both = tall[...].T[:48]
+    for n in range(8):
+        panel[n] = both
+    lane = lanes_of((4, 128))
+    tall[0:48, :] = both
+    for al in range(4):
+        for k in range(2):
+            value = jnp.zeros((4, 128), F32)
+            for m in range(2):
+                value = jnp.where(lane // 32 == m, pltpu.roll(d1[k, m], ((m - al) * 32) % 128, 1), value)
+            tall[48 + al * 8 + k * 4 : 52 + al * 8 + k * 4, :] = value
+    half = lanes_of((40, 128)) < 64
+    value = jnp.where(half, tall[0:40, :], pltpu.roll(tall[40:80, :], 64, 1))
+    for n in range(8):
+        mixed[n] = value
+
+
+def scatter_rows(slots, source, target):
+    def place(step, _):
+        base = pl.multiple_of(step * 48, 16)
+        for u in range(48):
+            target[pl.ds(slots[base + u], 1), :] = source[pl.ds(base + u, 1), :]
+        return 0
+
+    lax.fori_loop(0, 32, place, 0)
+
+
+def in_order(step):
+    return pl.multiple_of(((step % 8) * 4 + step // 8) * 48, 16)
+
+
+def second_body(where, slot2, panels, mine, other, spread, fold, extra, rows):
+    lane = lanes_of((48, 128))
+    keep = (lane >= 64) & (lane < 96)
+
+    def copy(step, _):
+        rows[pl.ds(in_order(step), 48), :] = jnp.where(keep, panels[step // 8, step % 8], 0.0)
+        return 0
+
+    lax.fori_loop(0, 32, copy, 0)
     spread[...] = jnp.zeros(spread.shape, F32)
-
-    def place(step, _):
-        x, y = step // 8, step % 8
-        base = (y * 4 + x) * 48
-        for u in range(48):
-            spread[pl.ds(slot2[base + u], 1), :] = panels[x, y, u : u + 1, :]
-        return 0
-
-    lax.fori_loop(0, 32, place, 0)
-    lane = lanes_of((40, 128))
-    lane_r = lanes_of((64, 128))
+    scatter_rows(slot2, rows, spread)
+    core = where[1] % 2
+    half = lanes_of((40, 128)) < 64
     total = jnp.zeros((160, 256), F32)
-    for c in range(16):
-        x = mixed[c]
-        left = jnp.concatenate([jnp.where(lane < 64, x, 0.0), jnp.where(lane >= 64, x, 0.0)], 0)
-        right = spread[EXT + c * 64 : EXT + (c + 1) * 64, :]
-        right = jnp.where((lane_r >= 64) & (lane_r < 96), right, 0.0)
-        total = total + product_terms(left, jnp.concatenate([right, right], 0))
+    for z in range(8):
+        for source, k in ((mine, core), (other, 1 - core)):
+            x = source[z]
+            left = jnp.concatenate([jnp.where(half, x, 0.0), jnp.where(half, 0.0, x)], 0)
+            right = spread[pl.ds(pl.multiple_of(EXT + (2 * z + k) * 64, 64), 64), :]
+            total = total + product_terms(left, jnp.concatenate([right, right], 0))
     out = folded(total)
     lane_f = lanes_of((16, 128))
     value = jnp.zeros((16, 128), F32)
     for h in range(3):
         moved = pltpu.roll(out[16 * h : 16 * (h + 1), :], (32 * h - 64) % 128, 1)
         value = jnp.where(lane_f // 32 == h, moved, value)
-    fold[...] = value
+    for n in range(8):
+        fold[n] = value
     extra[...] = out[48:80, :]
 
 
-def image_body(where, slot1, panels, fold, spread, blocks, extra, choice, right, send, comb):
-    lane = lanes_of((16, 128))
+def first_body(slot1, panels, spread, rows):
+    keep = lanes_of((48, 128)) < 64
+
+    def copy(step, _):
+        rows[pl.ds(in_order(step), 48), :] = jnp.where(keep, panels[step // 8, step % 8], 0.0)
+        return 0
+
+    lax.fori_loop(0, 32, copy, 0)
+    spread[...] = jnp.zeros(spread.shape, F32)
+    scatter_rows(slot1, rows, spread)
+
+
+def image_body(where, slot1, fold, own, second, blocks, extra, choice, right, send0, send1, rows, held, done):
+    send = (send0, send1)
+    arrival = pltpu.make_async_copy(blocks, held, done)
+    arrival.start()
+    keep = lanes_of((16, 128))
+    keep = (keep >= 64) & (keep < 96)
 
     def join(step, _):
-        x, y = step // 8, step % 8
-        base = pl.multiple_of((y * 4 + x) * 48, 16)
-        q = -fold[x, y]
+        q = -fold[step // 8, step % 8]
+        base = in_order(step)
         for h in range(3):
             moved = pltpu.roll(q, (64 - 32 * h) % 128, 1)
-            value = jnp.where(lane < 64, panels[x, y, 16 * h : 16 * (h + 1), :], jnp.where(lane < 96, moved, 0.0))
-            comb[pl.ds(base + 16 * h, 16), :] = value
+            rows[pl.ds(base + 16 * h, 16), :] = jnp.where(keep, moved, 0.0)
         return 0
 
     lax.fori_loop(0, 32, join, 0)
-    lane_r = lanes_of((SLOTS, 128))
-    for c in range(16):
-        low = c * 2 * SLOTS
-        right[low : low + SLOTS, :] = jnp.zeros((SLOTS, 128), F32)
-        value = spread[low + SLOTS : low + 2 * SLOTS, :]
-        right[low + SLOTS : low + 2 * SLOTS, :] = jnp.where((lane_r >= 64) & (lane_r < 96), value, 0.0)
-
-    def place(step, _):
-        base = pl.multiple_of(step * 48, 16)
-        for u in range(48):
-            right[pl.ds(slot1[base + u], 1), :] = comb[pl.ds(base + u, 1), :]
-        return 0
-
-    lax.fori_loop(0, 32, place, 0)
+    right[...] = jnp.zeros(right.shape, F32)
+    scatter_rows(slot1, rows, right)
+    right[...] = right[...] + own[...]
+    arrival.wait()
     total = jnp.zeros((2 * TALL, 256), F32)
     for c in range(16):
-        total = total + product_terms(blocks[c], right[c * 256 : (c + 1) * 256, :])
+        part = slice(c * SLOTS, (c + 1) * SLOTS)
+        total = total + product_terms(held[c], jnp.concatenate([right[part, :], second[part, :]], 0))
     image = jnp.concatenate([folded(total), extra[...]], 0)
     sent = jnp.zeros((96, TALL + 32), F32)
     for part in thirds(image):
@@ -199,7 +241,11 @@
     sent = jnp.concatenate([sent, jnp.zeros((96, 256 - TALL - 32), F32)], 1)
     parity = where[0] % 2
     for h in range(2):
-        send[pl.ds((h + parity) % 2, 1)] = sent[h * 48 : (h + 1) * 48][None]
+
+        @pl.when(parity == h)
+        def _(h=h):
+            send[0][...] = sent[h * 48 : (h + 1) * 48]
+            send[1][...] = sent[(1 - h) * 48 : (2 - h) * 48]
 
 
 def cross_body(where, got0, got1, order, table, first, second, share, own):
@@ -209,12 +255,13 @@
     odd = jnp.where(parity == 0, b, a)
     y = chosen(jnp.concatenate([even, odd], 1), order[...])
     close = chosen(y[:, :384], table[...])
-    share[0:48, :] = close[:, :128]
-    share[48:64, :] = close[32:48, 128:]
     e = y[32:48, 384:512]
     own[...] = e
     lane = lanes_of((8, 128))
-    share[64:72, :] = jnp.where(lane < 64, e[:8], pltpu.roll(e[8:], 64, 1))
+    e = jnp.where(lane < 64, e[:8], pltpu.roll(e[8:], 64, 1))
+    e = jnp.concatenate([close[:, :128], close[32:48, 128:], e], 0)
+    for n in range(8):
+        share[n] = e
     lane2 = lanes_of((4, 128))
     for i in range(9):
         chunk = (i // 4) * 128
@@ -232,23 +279,27 @@
         second[0, i] = -two
 
 
-def diagonal_body(shares, right, spread, own, d1, d2, first, second):
-    lane_r = lanes_of((64, 128))
+def diagonal_body(where, mine, other, right, spread, own, d1, d2, left1, left2, first, second):
+    first[:, 0:9] = left1[...]
+    second[:, 0:9] = left2[...]
+    core = where[1] % 2
     lane_e = lanes_of((8, 128))
     total = jnp.zeros((128, 256), F32)
     also = jnp.zeros((32, 256), F32)
-    for c in range(16):
-        x = shares[c]
-        zero = jnp.zeros((48, 128), F32)
-        left = jnp.concatenate(
-            [jnp.concatenate([x[:48], zero], 1), jnp.concatenate([zero[:16], x[48:64]], 1)], 0
-        )
-        total = total + product_terms(left, right[c * 256 : (c + 1) * 256, :])
-        e = x[64:72]
-        left = jnp.concatenate([jnp.where(lane_e < 64, e, 0.0), jnp.where(lane_e >= 64, e, 0.0)], 0)
-        v = spread[EXT + c * 64 : EXT + (c + 1) * 64, :]
-        v = jnp.where((lane_r >= 64) & (lane_r < 96), v, 0.0)
-        also = also + product_terms(left, jnp.concatenate([v, v], 0))
+    for z in range(8):
+        for source, k in ((mine, core), (other, 1 - core)):
+            c = 2 * z + k
+            x = source[z]
+            part = pl.ds(pl.multiple_of(c * SLOTS, SLOTS), SLOTS)
+            zero = jnp.zeros((48, 128), F32)
+            left = jnp.concatenate(
+                [jnp.concatenate([x[:48], zero], 1), jnp.concatenate([zero[:16], x[48:64]], 1)], 0
+            )
+            total = total + product_terms(left, jnp.concatenate([right[part, :], spread[part, :]], 0))
+            e = x[64:72]
+            left = jnp.concatenate([jnp.where(lane_e < 64, e, 0.0), jnp.where(lane_e >= 64, e, 0.0)], 0)
+            v = spread[pl.ds(pl.multiple_of(EXT + c * 64, 64), 64), :]
+            also = also + product_terms(left, jnp.concatenate([v, v], 0))
     out = folded(total)
     g1 = out[:32]
     bottom = own[...] - out[32:48]
@@ -262,18 +313,19 @@
             shift = ((al - k) * 32) % 128
             one = jnp.where(lane // 32 == al, pltpu.roll(g1[al * 8 : (al + 1) * 8], shift, 1), one)
             two = jnp.where(lane2 // 32 == al, pltpu.roll(bottom[al * 4 : (al + 1) * 4], shift, 1), two)
-        first[0, k] = d1[0, k] + one[0:4]
-        first[1, k] = d1[1, k] + one[4:8]
-        second[0, k] = -two
+        first[0, 9 + k] = d1[0, k] + one[0:4]
+        first[1, 9 + k] = d1[1, k] + one[4:8]
+        second[0, 9 + k] = -two
     two = jnp.zeros((4, 128), F32)
     for al in range(4):
         shift = ((al - 2) * 32) % 128
         two = jnp.where(lane2 // 32 == al, pltpu.roll(g2[al * 4 : (al + 1) * 4], shift, 1), two)
-    second[0, 2] = d2[0, 0] + two
+    second[0, 11] = d2[0, 0] + two
 
 
 VMEM = pl.BlockSpec(memory_space=pltpu.VMEM)
 SMEM = pl.BlockSpec(memory_space=pltpu.SMEM)
+ANY = pl.BlockSpec(memory_space=pl.ANY)
 
 
 def kernel(body, specs, outs, scratch=()):
@@ -286,17 +338,18 @@
     )
 
 
-def from_all(x, axis, count, groups=None):
-    copies = jnp.broadcast_to(x, (count, *x.shape))
-    return lax.all_to_all(copies, axis, 0, 0, axis_index_groups=groups, tiled=True)
+def exchanged(x, axis, groups):
+    return lax.all_to_all(x, axis, 0, 0, axis_index_groups=groups, tiled=True)
 
 
 def along_rows(x):
-    return from_all(from_all(x, "row", 8, Y_GROUPS), "row", 4, X_GROUPS)
+    near = exchanged(x, "row", Y_GROUPS)
+    return exchanged(jnp.broadcast_to(near, (4, *near.shape)), "row", X_GROUPS)
 
 
 def along_cols(x):
-    return from_all(x, "col", 16)
+    mine = exchanged(x, "col", Z_GROUPS)
+    return mine, lax.ppermute(mine, "col", [(c, c ^ 1) for c in range(16)])
 
 
 def transposed(x, turn):
@@ -306,13 +359,12 @@
 
 def on_device(ancestor, inverse_first, panel_first, structure_first, inverse_second, panel_second, structure_second):
     where = jnp.stack([lax.axis_index("row"), lax.axis_index("col")]).astype(jnp.int32)
-    p1 = panel_first.reshape(48, 64)
-    p2 = panel_second.reshape(48, 32)
-    panel = jnp.concatenate([p1, p2, jnp.zeros((48, 32), F32)], 1)
-    d1 = inverse_first.reshape(2, 2, 4, 4, 32).transpose(3, 0, 2, 1, 4).reshape(32, 64)
-    stacked = jnp.concatenate([p1, d1], 0)
-    mixed = jnp.concatenate([stacked[:40], stacked[40:]], 1)
-
+    panel, mixed = kernel(
+        lay_body,
+        (VMEM, VMEM, VMEM),
+        (((8, 48, 128), F32), ((8, 40, 128), F32)),
+        (pltpu.VMEM((128, 128), F32),),
+    )(panel_first.transpose(1, 2, 0), panel_second.transpose(1, 2, 0), inverse_first)
     packed, slot1, slot2, table = kernel(
         rank_body,
         (SMEM, VMEM, VMEM, VMEM),
@@ -321,36 +373,35 @@
     )(where, structure_first.reshape(12, 128), structure_second.reshape(12, 128), ancestor)
     blocks = lax.all_gather(packed, "col")
     panels = along_rows(panel)
-    mixes = along_cols(mixed)
+    mine, other = along_cols(mixed)
     slot1, slot2 = slot1.reshape(1536), slot2.reshape(1536)
+    rows = pltpu.VMEM((1536, 128), F32)
     spread, fold, extra = kernel(
         second_body,
-        (SMEM, VMEM, VMEM),
-        (((EXT + 1024, 128), F32), ((16, 128), F32), ((32, 128), F32)),
-    )(slot2, panels, mixes)
+        (SMEM, SMEM, VMEM, VMEM, VMEM),
+        (((EXT + 1024, 128), F32), ((8, 16, 128), F32), ((32, 128), F32)),
+        (rows,),
+    )(where, slot2, panels, mine, other)
     folds = along_rows(fold)
-    right, send = kernel(
+    (own,) = kernel(first_body, (SMEM, VMEM), (((EXT, 128), F32),), (rows,))(slot1, panels)
+    right, send0, send1 = kernel(
         image_body,
-        (SMEM, SMEM, VMEM, VMEM, VMEM, VMEM, VMEM, VMEM),
-        (((EXT, 128), F32), ((2, 48, 256), F32)),
-        (pltpu.VMEM((1536, 128), F32),),
-    )(where, slot1, panels, folds, spread, blocks, extra, jnp.asarray(column_choice(), BF16))
-    got0, got1 = transposed(send[0], 0), transposed(send[1], 1)
-    first_left, second_left, share, own = kernel(
+        (SMEM, SMEM, VMEM, VMEM, VMEM, ANY, VMEM, VMEM),
+        (((EXT, 128), F32), ((48, 256), F32), ((48, 256), F32)),
+        (rows, pltpu.VMEM((16, TALL, 256), F32), pltpu.SemaphoreType.DMA),
+    )(where, slot1, folds, own, spread, blocks, extra, jnp.asarray(column_choice(), BF16))
+    got0, got1 = transposed(send0, 0), transposed(send1, 1)
+    left1, left2, share, own = kernel(
         cross_body,
         (SMEM, VMEM, VMEM, VMEM, VMEM),
-        (((2, 9, 4, 128), F32), ((1, 9, 4, 128), F32), ((72, 128), F32), ((16, 128), F32)),
+        (((2, 9, 4, 128), F32), ((1, 9, 4, 128), F32), ((8, 72, 128), F32), ((16, 128), F32)),
     )(where, got0, got1, jnp.asarray(lane_order(), BF16), table)
-    shares = along_cols(share)
-    first_right, second_right = kernel(
+    mine, other = along_cols(share)
+    return kernel(
         diagonal_body,
-        (VMEM,) * 6,
-        (((2, 2, 4, 128), F32), ((1, 3, 4, 128), F32)),
-    )(shares, right, spread, own, inverse_first, inverse_second)
-    return (
-        jnp.concatenate([first_left, first_right], 1),
-        jnp.concatenate([second_left, second_right], 1),
-    )
+        (SMEM,) + (VMEM,) * 9,
+        (((2, 11, 4, 128), F32), ((1, 12, 4, 128), F32)),
+    )(where, mine, other, right, spread, own, inverse_first, inverse_second, left1, left2)
 
 
 def solution(mesh):

time: 173 us -> 158 us (0.913)
  blocking collectives: 97.4 us -> 74.1 us
  starting transfers between devices: 16 us -> 27.9 us
  Pallas kernels: 22.1 us -> 26.5 us
  other arithmetic: 4.24 us -> 0.65 us
  local copies, waits for them, and re-layouts: 7.33 us -> 4.64 us
    all_to_all x5 -> x4, blocking collectives: 97.4 us -> 74.1 us  [exchanged(): return lax.all_to_all(x, axis, 0, 0, axis_index_groups=groups, tiled=True)]
    ppermute x0 -> x2, starting transfers between devices: none -> 8.33 us  [along_cols(): return (mine, lax.ppermute(mine, 'col', [(c, c ^ 1) for c in range(16)]))]
    pallas_call x3 -> x5, Pallas kernels: 17 us -> 21.3 us  [the longest x1 8.1 us: on_device(): kernel(image_body, (SMEM, SMEM, VMEM, VMEM, VMEM, ANY, VMEM, VMEM), (((EX...]
    ppermute x2, starting transfers between devices: 8.37 us -> 12.2 us  [transposed(): return lax.ppermute(x, ('row', 'col'), pairs)]
    concatenate x5 -> x0, other arithmetic: 3.63 us -> none  [the longest x1 1.33 us: on_device(): jnp.concatenate([first_left, first_right], 1)]
    all_to_all x1 -> x2, waiting for transfers between devices: 5.92 us -> 2.91 us  [exchanged(): return lax.all_to_all(x, axis, 0, 0, axis_index_groups=groups, tiled=True)]
    ppermute x0 -> x2, waiting for transfers between devices: none -> 2.19 us  [along_cols(): return (mine, lax.ppermute(mine, 'col', [(c, c ^ 1) for c in range(16)]))]
    reshape x5 -> x0, local copies, waits for them, and re-layouts: 1.81 us -> none  [the longest x4 0.98 us: on_device(): inverse_first.reshape(2, 2, 4, 4, 32).transpose(3, 0, 2, 1, 4)]
  transfers between devices with their start and end apart: 4 -> 7, of which waited for: 2 -> 5; matrix products, arithmetic and copies ran while one was open for 4% -> 1% of each run, Pallas kernels for 3% -> 6%
where the time goes in v1:
time: 158 us; the launch traced here: 157 us
  blocking collectives  74.1 us (47%)
  starting transfers between devices  27.9 us (18%)
  Pallas kernels  26.5 us (17%)
  between operations  14.1 us (9%)
  waiting for transfers between devices  9.58 us (6%)
  local copies, waits for them, and re-layouts  4.64 us (3%)
    all_to_all x4, blocking collectives, exchanged(): return lax.all_to_all(x, axis, 0, 0, axis_index_groups=groups, tiled=True)  74.1 us
    ppermute x2, starting transfers between devices, transposed(): return lax.ppermute(x, ('row', 'col'), pairs)  12.2 us
    ppermute x2, starting transfers between devices, along_cols(): return (mine, lax.ppermute(mine, 'col', [(c, c ^ 1) for c in range(16)]))  8.33 us
    pallas_call x1, Pallas kernels, on_device(): kernel(image_body, (SMEM, SMEM, VMEM, VMEM, VMEM, ANY, VMEM, VMEM), (((EX...  8.1 us
    all_to_all x2, starting transfers between devices, exchanged(): return lax.all_to_all(x, axis, 0, 0, axis_index_groups=groups, tiled=True)  7.42 us
    ppermute x2, waiting for transfers between devices, transposed(): return lax.ppermute(x, ('row', 'col'), pairs)  4.46 us
    pallas_call x1, Pallas kernels, on_device(): kernel(second_body, (SMEM, SMEM, VMEM, VMEM, VMEM), (((EXT + 1024, 128),...  4.44 us
    pallas_call x1, Pallas kernels, on_device(): kernel(first_body, (SMEM, VMEM), (((EXT, 128), F32),), (rows,))  3.9 us
  transfers between devices with their start and end apart: 7, of which 5 were waited for; matrix products, arithmetic and copies ran while one was open for 1% of the time, Pallas kernels for 6%

profile of v1, /device:TPU:1, one launch (start us, length us, event | category | flops | bytes accessed | tf_op | source)
XLA Modules:
  0.0 157.5 jit_solution(2562931210584867468)
XLA Ops:
  7.2 0.0 all-gather.3.cloned.1.call-start
  7.2 0.6 pad_add_fusion.where
  7.9 2.9 %shard_map.104 = (f32[160,256]{1,0:T(8,128)}, s32[12,128]{1,0:T(8,128)}, s32[12,128]{1,0:T(8,128)}, bf16[384,256]{1,0:T(8,128)(2,1)}) custom-call(s32[2]{0:T(128)} %pad_add_fusion.where, s32[12,128]{1,0:T(8,128)} %bitcast.15, s32[12,128]{1,0:T(8,128)} %bitcast.16, f32[9,9,4,128]{3,2,1,0:T(4,128)} %tiles.1), custom_call_target="tpu_custom_call" | custom-call | tf_op jit(solution)/shard_map/pallas_call | solution.py:368
  10.7 0.0 all-gather.3.cloned.1.call-update
  10.7 1.6 %shard_map.105 = (f32[8,48,128]{2,1,0:T(8,128)}, f32[8,40,128]{2,1,0:T(8,128)}) custom-call(f32[2,32,48]{2,1,0:T(8,128)} %bitcast.12, f32[1,32,48]{2,1,0:T(8,128)} %bitcast.13, f32[2,2,4,128]{3,2,1,0:T(4,128)} %d1.3), custom_call_target="tpu_custom_call" | custom-call | tf_op jit(solution)/shard_map/pallas_call | solution.py:362
  12.4 19.1 %all_to_all.30.mine = f32[8,40,128]{2,1,0:T(8,128)S(1)} all-to-all(f32[8,40,128]{2,1,0:T(8,128)} %get-tuple-element.21), channel_id=1, replica_groups={{0,2,4,6,8,10,12,14},{1,3,5,7,9,11,13,15},{16,18,20,22,24,26,28,30},{17..., dimensions={0} | all-to-all | bytes 327680 | tf_op jit(solution)/shard_map/all_to_all | solution.py:342
  31.4 0.0 copy-start.3
  31.4 15.6 %all_to_all.31 = f32[8,48,128]{2,1,0:T(8,128)S(1)} all-to-all(f32[8,48,128]{2,1,0:T(8,128)} %get-tuple-element.20), channel_id=1, replica_groups={{0,64,128,192,256,320,384,448},{16,80,144,208,272,336,400,464},{32,96,1..., dimensions={0} | all-to-all | bytes 393216 | tf_op jit(solution)/shard_map/all_to_all | solution.py:342
  47.0 1.0 broadcast_in_dim.6
  48.0 4.0 %all-to-all-start.1 = ((f32[4,8,48,128]{3,2,1,0:T(8,128)}), f32[4,8,48,128]{3,2,1,0:T(8,128)S(1)}, u32[]{:S(2)}, u32[]{:S(2)}) async-start(f32[4,8,48,128]{3,2,1,0:T(8,128)} %broadcast_in_dim.6), calls=%async_computation.1 | async-start | bytes 1572864 | tf_op jit(solution)/shard_map/all_to_all | solution.py:342
  52.0 6.0 %collective-permute-start = (f32[8,40,128]{2,1,0:T(8,128)S(1)}, f32[8,40,128]{2,1,0:T(8,128)S(1)}, u32[]{:S(2)}, u32[]{:S(2)}) collective-permute-start(f32[8,40,128]{2,1,0:T(8,128)S(1)} %all_to_all.30.mine), channel_id=1, source_target_pairs={{0,1},{1,0},{2,3},{3,2},{4,5},{5,4},{6,7},{7,6},{8,9},{9,8},{10,11... | collective-permute-start | bytes 491528 | tf_op jit(solution)/shard_map/ppermute | solution.py:352
  58.0 1.0 collective-permute-done.other
  59.0 0.0 copy-start.5
  59.0 1.3 all-to-all-done.1.panels
  60.3 0.0 copy-start
  60.3 0.0 copy-done.3
  60.3 0.0 copy-done.5
  60.3 0.9 copy-done
  61.2 4.4 %shard_map.106 = (f32[3072,128]{1,0:T(8,128)}, f32[8,16,128]{2,1,0:T(8,128)}, f32[32,128]{1,0:T(8,128)}) custom-call(s32[2]{0:T(128)} %pad_add_fusion.where, s32[1536]{0:T(1024)} %bitcast.14, f32[4,8,48,128]{3,2,1,0:T(8,128)} %copy-done, f32[8,40,128]{2,1,0:T(8,128)} %copy-done.3, f32[8,40,128]{2,1,0:T(8,128)} %copy-done.5), custom_call_target="tpu_custom_call" | custom-call | tf_op jit(solution)/shard_map/pallas_call | solution.py:379
  65.7 10.5 %all_to_all.32 = f32[8,16,128]{2,1,0:T(8,128)S(1)} all-to-all(f32[8,16,128]{2,1,0:T(8,128)} %get-tuple-element.22), channel_id=1, replica_groups={{0,64,128,192,256,320,384,448},{16,80,144,208,272,336,400,464},{32,96,1..., dimensions={0} | all-to-all | bytes 131072 | tf_op jit(solution)/shard_map/all_to_all | solution.py:342
  76.1 0.7 broadcast_in_dim.7
  76.9 3.4 %all-to-all-start.4 = ((f32[4,8,16,128]{3,2,1,0:T(8,128)}), f32[4,8,16,128]{3,2,1,0:T(8,128)S(1)}, u32[]{:S(2)}, u32[]{:S(2)}) async-start(f32[4,8,16,128]{3,2,1,0:T(8,128)} %broadcast_in_dim.7), calls=%async_computation.4 | async-start | bytes 524288 | tf_op jit(solution)/shard_map/all_to_all | solution.py:342
  80.3 3.9 %shard_map.107.own = f32[2048,128]{1,0:T(8,128)} custom-call(s32[1536]{0:T(1024)} %bitcast.10, f32[4,8,48,128]{3,2,1,0:T(8,128)} %copy-done), custom_call_target="tpu_custom_call" | custom-call | tf_op jit(solution)/shard_map/pallas_call | solution.py:386
  84.2 1.6 %all-to-all-done.4.fold = f32[4,8,16,128]{3,2,1,0:T(8,128)S(1)} async-done(((f32[4,8,16,128]{3,2,1,0:T(8,128)}), f32[4,8,16,128]{3,2,1,0:T(8,128)S(1)}, u32[]{:S(2)}, u32[]{:S(2)}) %all-to-all-start.4) | async-done | bytes 262176 | tf_op jit(solution)/shard_map/all_to_all | solution.py:342
  85.8 0.0 copy-start.2
  85.8 0.0 all-gather.3.cloned.1.call-done
  85.8 0.7 copy-done.2
  86.5 8.1 %shard_map.108 = (f32[2048,128]{1,0:T(8,128)}, f32[48,256]{1,0:T(8,128)}, f32[48,256]{1,0:T(8,128)}) custom-call(s32[2]{0:T(128)} %pad_add_fusion.where, s32[1536]{0:T(1024)} %bitcast.11, f32[4,8,16,128]{3,2,1,0:T(8,128)} %copy-done.2, f32[2048,128]{1,0:T(8,128)} %shard_map.107.own, f32[3072,128]{1,0:T(8,128)} %get-tuple-element.23.second.spread, ...), custom_call_target="tpu_custom_call" | custom-call | tf_op jit(solution)/shard_map/pallas_call | solution.py:387
  94.6 9.8 %collective-permute-start.1 = (f32[48,256]{1,0:T(8,128)}, f32[48,256]{1,0:T(8,128)S(1)}, u32[]{:S(2)}, u32[]{:S(2)}) collective-permute-start(f32[48,256]{1,0:T(8,128)} %get-tuple-element.26), channel_id=1, source_target_pairs={{0,0},{1,32},{2,64},{3,96},{4,128},{5,160},{6,192},{7,224},{8,256}... | collective-permute-start | bytes 147464 | tf_op jit(solution)/shard_map/ppermute | solution.py:357
  104.4 2.3 %collective-permute-start.2 = (f32[48,256]{1,0:T(8,128)}, f32[48,256]{1,0:T(8,128)S(1)}, u32[]{:S(2)}, u32[]{:S(2)}) collective-permute-start(f32[48,256]{1,0:T(8,128)} %get-tuple-element.27), channel_id=1, source_target_pairs={{0,16},{1,48},{2,80},{3,112},{4,144},{5,176},{6,208},{7,240},{8,27... | collective-permute-start | bytes 147464 | tf_op jit(solution)/shard_map/ppermute | solution.py:357
  106.8 0.0 collective-permute-done.1.got0
  106.8 0.0 copy-start.6
  106.8 4.5 %collective-permute-done.2.got1 = f32[48,256]{1,0:T(8,128)S(1)} collective-permute-done((f32[48,256]{1,0:T(8,128)}, f32[48,256]{1,0:T(8,128)S(1)}, u32[]{:S(2)}, u32[]{:S(2)}) %collective-permute-start.2) | collective-permute-done | bytes 49184 | tf_op jit(solution)/shard_map/ppermute | solution.py:357
  111.3 0.0 copy-start.7
  111.3 0.0 copy-done.6
  111.3 0.6 copy-done.7
  111.9 2.3 %shard_map.109 = (f32[2,9,4,128]{3,2,1,0:T(4,128)}, f32[1,9,4,128]{3,2,1,0:T(4,128)}, f32[8,72,128]{2,1,0:T(8,128)}, f32[16,128]{1,0:T(8,128)}) custom-call(s32[2]{0:T(128)} %pad_add_fusion.where, f32[48,256]{1,0:T(8,128)} %copy-done.6, f32[48,256]{1,0:T(8,128)} %copy-done.7, bf16[512,512]{1,0:T(8,128)(2,1)} %constant.14.clone.order, ...), custom_call_target="tpu_custom_call" | custom-call | tf_op jit(solution)/shard_map/pallas_call | solution.py:394
  114.2 29.0 %all_to_all.33.mine = f32[8,72,128]{2,1,0:T(8,128)S(1)} all-to-all(f32[8,72,128]{2,1,0:T(8,128)} %get-tuple-element.29), channel_id=1, replica_groups={{0,2,4,6,8,10,12,14},{1,3,5,7,9,11,13,15},{16,18,20,22,24,26,28,30},{17..., dimensions={0} | all-to-all | bytes 589824 | tf_op jit(solution)/shard_map/all_to_all | solution.py:342
  143.2 0.0 copy-start.1
  143.2 2.3 %collective-permute-start.3 = (f32[8,72,128]{2,1,0:T(8,128)S(1)}, f32[8,72,128]{2,1,0:T(8,128)S(1)}, u32[]{:S(2)}, u32[]{:S(2)}) collective-permute-start(f32[8,72,128]{2,1,0:T(8,128)S(1)} %all_to_all.33.mine), channel_id=1, source_target_pairs={{0,1},{1,0},{2,3},{3,2},{4,5},{5,4},{6,7},{7,6},{8,9},{9,8},{10,11... | collective-permute-start | bytes 884744 | tf_op jit(solution)/shard_map/ppermute | solution.py:352
  145.5 1.2 collective-permute-done.3.other
  146.7 0.0 copy-start.4
  146.7 0.0 copy-done.1
  146.7 0.7 copy-done.4
  147.4 3.2 %shard_map.110 = (f32[2,11,4,128]{3,2,1,0:T(4,128)}, f32[1,12,4,128]{3,2,1,0:T(4,128)}) custom-call(s32[2]{0:T(128)} %pad_add_fusion.where, f32[8,72,128]{2,1,0:T(8,128)} %copy-done.1, f32[8,72,128]{2,1,0:T(8,128)} %copy-done.4, f32[2048,128]{1,0:T(8,128)} %get-tuple-element.30.right, f32[3072,128]{1,0:T(8,128)} %get-tuple-element.23.second.spread, ...), custom_call_target="tpu_custom_call" | custom-call | tf_op jit(solution)/shard_map/pallas_call | solution.py:400
Async XLA Ops:
  7.2 78.6 %all-gather.3.cloned.1.call-start = ((), (), s32[]{:S(2)}) async-start(), calls=%async_computation.6 | async-start | bytes 2785280 | tf_op jit(solution)/shard_map/all_gather | solution.py:374
  31.4 28.9 %copy-start.3 = (f32[8,40,128]{2,1,0:T(8,128)}, f32[8,40,128]{2,1,0:T(8,128)S(1)}, u32[]{:S(2)}) copy-start(f32[8,40,128]{2,1,0:T(8,128)S(1)} %all_to_all.30.mine) | copy-start | bytes 491524
  48.0 12.4 %all-to-all-start.1 = ((f32[4,8,48,128]{3,2,1,0:T(8,128)}), f32[4,8,48,128]{3,2,1,0:T(8,128)S(1)}, u32[]{:S(2)}, u32[]{:S(2)}) async-start(f32[4,8,48,128]{3,2,1,0:T(8,128)} %broadcast_in_dim.6), calls=%async_computation.1 | async-start | bytes 1572864 | tf_op jit(solution)/shard_map/all_to_all | solution.py:342
  52.0 7.0 %collective-permute-start = (f32[8,40,128]{2,1,0:T(8,128)S(1)}, f32[8,40,128]{2,1,0:T(8,128)S(1)}, u32[]{:S(2)}, u32[]{:S(2)}) collective-permute-start(f32[8,40,128]{2,1,0:T(8,128)S(1)} %all_to_all.30.mine), channel_id=1, source_target_pairs={{0,1},{1,0},{2,3},{3,2},{4,5},{5,4},{6,7},{7,6},{8,9},{9,8},{10,11... | collective-permute-start | bytes 491528 | tf_op jit(solution)/shard_map/ppermute | solution.py:352
  59.0 1.3 copy-start.5
  60.3 0.9 copy-start
  76.9 8.9 %all-to-all-start.4 = ((f32[4,8,16,128]{3,2,1,0:T(8,128)}), f32[4,8,16,128]{3,2,1,0:T(8,128)S(1)}, u32[]{:S(2)}, u32[]{:S(2)}) async-start(f32[4,8,16,128]{3,2,1,0:T(8,128)} %broadcast_in_dim.7), calls=%async_computation.4 | async-start | bytes 524288 | tf_op jit(solution)/shard_map/all_to_all | solution.py:342
  85.8 0.7 copy-start.2
  94.6 12.2 %collective-permute-start.1 = (f32[48,256]{1,0:T(8,128)}, f32[48,256]{1,0:T(8,128)S(1)}, u32[]{:S(2)}, u32[]{:S(2)}) collective-permute-start(f32[48,256]{1,0:T(8,128)} %get-tuple-element.26), channel_id=1, source_target_pairs={{0,0},{1,32},{2,64},{3,96},{4,128},{5,160},{6,192},{7,224},{8,256}... | collective-permute-start | bytes 147464 | tf_op jit(solution)/shard_map/ppermute | solution.py:357
  104.4 6.8 %collective-permute-start.2 = (f32[48,256]{1,0:T(8,128)}, f32[48,256]{1,0:T(8,128)S(1)}, u32[]{:S(2)}, u32[]{:S(2)}) collective-permute-start(f32[48,256]{1,0:T(8,128)} %get-tuple-element.27), channel_id=1, source_target_pairs={{0,16},{1,48},{2,80},{3,112},{4,144},{5,176},{6,208},{7,240},{8,27... | collective-permute-start | bytes 147464 | tf_op jit(solution)/shard_map/ppermute | solution.py:357
  106.8 4.5 %copy-start.6 = (f32[48,256]{1,0:T(8,128)}, f32[48,256]{1,0:T(8,128)S(1)}, u32[]{:S(2)}) copy-start(f32[48,256]{1,0:T(8,128)S(1)} %collective-permute-done.1.got0) | copy-start | bytes 147460
  111.3 0.6 copy-start.7
  143.2 3.5 %copy-start.1 = (f32[8,72,128]{2,1,0:T(8,128)}, f32[8,72,128]{2,1,0:T(8,128)S(1)}, u32[]{:S(2)}) copy-start(f32[8,72,128]{2,1,0:T(8,128)S(1)} %all_to_all.33.mine) | copy-start | bytes 884740
  143.2 3.5 %collective-permute-start.3 = (f32[8,72,128]{2,1,0:T(8,128)S(1)}, f32[8,72,128]{2,1,0:T(8,128)S(1)}, u32[]{:S(2)}, u32[]{:S(2)}) collective-permute-start(f32[8,72,128]{2,1,0:T(8,128)S(1)} %all_to_all.33.mine), channel_id=1, source_target_pairs={{0,1},{1,0},{2,3},{3,2},{4,5},{5,4},{6,7},{7,6},{8,9},{9,8},{10,11... | collective-permute-start | bytes 884744 | tf_op jit(solution)/shard_map/ppermute | solution.py:352
  146.7 0.7 copy-start.4
Sparse Core Ops, SparseCore 0:
  10.9 49.1 all-gather.2

commit v2 on v1

--- a/solution.py
+++ b/solution.py
@@ -8,8 +8,7 @@
 
 F32 = jnp.float32
 BF16 = jnp.bfloat16
-LINES = 40
-TALL = 4 * LINES
+TALL = 144
 SLOTS = 128
 EXT = 16 * SLOTS
 
@@ -36,7 +35,7 @@
         for al in range(4):
             for i in range(9):
                 for q in range(4):
-                    table[g * 256 + al * LINES + i * 4 + q, i * 32 + g * 16 + 4 * q + al] = 1
+                    table[g * 256 + i * 16 + al * 4 + q, i * 32 + g * 16 + 4 * q + al] = 1
             for k in range(2):
                 for q in range(4):
                     table[g * 256 + TALL + al * 8 + k * 4 + q, 384 + k * 32 + g * 16 + 4 * q + al] = 1
@@ -119,13 +118,11 @@
         table[j * 32 : (j + 1) * 32, :] = pair
         for al in range(4):
             rhs[j * 128 + al * 32 : j * 128 + (al + 1) * 32, :] = pair
-        stage[...] = jnp.zeros((LINES, 128), F32)
+        quarter = lanes_of((4, 128)) // 32
         for i in range(9):
-            stage[i * 4 : (i + 1) * 4, :] = tiles[i, j]
-        x = stage[...]
-        quarter = lanes_of((LINES, 128)) // 32
-        x = jnp.concatenate([jnp.where(quarter == al, x, 0.0) for al in range(4)], 0)
-        for part, value in enumerate(thirds(x)):
+            for al in range(4):
+                stage[i * 16 + al * 4 : i * 16 + (al + 1) * 4, :] = jnp.where(quarter == al, tiles[i, j], 0.0)
+        for part, value in enumerate(thirds(stage[...])):
             lhs[part * TALL : (part + 1) * TALL, j * 128 : (j + 1) * 128] = value
     out = dot(lhs[...], rhs[...])
     packed[...] = out[:TALL] + (out[TALL : 2 * TALL] + out[2 * TALL :])
@@ -193,7 +190,7 @@
     for h in range(3):
         moved = pltpu.roll(out[16 * h : 16 * (h + 1), :], (32 * h - 64) % 128, 1)
         value = jnp.where(lane_f // 32 == h, moved, value)
-    for n in range(8):
+    for n in range(32):
         fold[n] = value
     extra[...] = out[48:80, :]
 
@@ -218,8 +215,8 @@
     keep = (keep >= 64) & (keep < 96)
 
     def join(step, _):
-        q = -fold[step // 8, step % 8]
-        base = in_order(step)
+        q = -fold[step]
+        base = pl.multiple_of(step * 48, 16)
         for h in range(3):
             moved = pltpu.roll(q, (64 - 32 * h) % 128, 1)
             rows[pl.ds(base + 16 * h, 16), :] = jnp.where(keep, moved, 0.0)
@@ -238,14 +235,20 @@
     sent = jnp.zeros((96, TALL + 32), F32)
     for part in thirds(image):
         sent = sent + lax.dot_general(choice[...], part, (((1,), (1,)), ((), ())), preferred_element_type=F32)
-    sent = jnp.concatenate([sent, jnp.zeros((96, 256 - TALL - 32), F32)], 1)
+    lane = lanes_of((16, 128))
+    pieces = []
+    for h in range(2):
+        rest = jnp.concatenate([sent[h * 48 : (h + 1) * 48, 128:], jnp.zeros((48, 80), F32)], 1)
+        tail = jnp.where(lane < 16, rest[0:16], pltpu.roll(rest[16:32], 16, 1))
+        tail = jnp.where(lane < 32, tail, pltpu.roll(rest[32:48], 32, 1))
+        pieces.append(jnp.concatenate([sent[h * 48 : (h + 1) * 48, :128], tail], 0))
     parity = where[0] % 2
     for h in range(2):
 
         @pl.when(parity == h)
         def _(h=h):
-            send[0][...] = sent[h * 48 : (h + 1) * 48]
-            send[1][...] = sent[(1 - h) * 48 : (2 - h) * 48]
+            send[0][...] = pieces[h]
+            send[1][...] = pieces[1 - h]
 
 
 def cross_body(where, got0, got1, order, table, first, second, share, own):
@@ -253,7 +256,12 @@
     a, b = got0[...], got1[...]
     even = jnp.where(parity == 0, a, b)
     odd = jnp.where(parity == 0, b, a)
-    y = chosen(jnp.concatenate([even, odd], 1), order[...])
+    parts = []
+    for got in (even, odd):
+        tail = got[48:64]
+        parts.append(got[:48])
+        parts.append(jnp.concatenate([tail, pltpu.roll(tail, 112, 1), pltpu.roll(tail, 96, 1)], 0))
+    y = chosen(jnp.concatenate(parts, 1), order[...])
     close = chosen(y[:, :384], table[...])
     e = y[32:48, 384:512]
     own[...] = e
@@ -369,7 +377,7 @@
         rank_body,
         (SMEM, VMEM, VMEM, VMEM),
         (((TALL, 256), F32), ((12, 128), jnp.int32), ((12, 128), jnp.int32), ((384, 256), BF16)),
-        (pltpu.VMEM((3 * TALL, 1152), BF16), pltpu.VMEM((1152, 256), BF16), pltpu.VMEM((LINES, 128), F32)),
+        (pltpu.VMEM((3 * TALL, 1152), BF16), pltpu.VMEM((1152, 256), BF16), pltpu.VMEM((TALL, 128), F32)),
     )(where, structure_first.reshape(12, 128), structure_second.reshape(12, 128), ancestor)
     blocks = lax.all_gather(packed, "col")
     panels = along_rows(panel)
@@ -379,15 +387,15 @@
     spread, fold, extra = kernel(
         second_body,
         (SMEM, SMEM, VMEM, VMEM, VMEM),
-        (((EXT + 1024, 128), F32), ((8, 16, 128), F32), ((32, 128), F32)),
+        (((EXT + 1024, 128), F32), ((32, 16, 128), F32), ((32, 128), F32)),
         (rows,),
     )(where, slot2, panels, mine, other)
-    folds = along_rows(fold)
+    folds = lax.all_to_all(fold, "row", 0, 0, tiled=True)
     (own,) = kernel(first_body, (SMEM, VMEM), (((EXT, 128), F32),), (rows,))(slot1, panels)
     right, send0, send1 = kernel(
         image_body,
         (SMEM, SMEM, VMEM, VMEM, VMEM, ANY, VMEM, VMEM),
-        (((EXT, 128), F32), ((48, 256), F32), ((48, 256), F32)),
+        (((EXT, 128), F32), ((64, 128), F32), ((64, 128), F32)),
         (rows, pltpu.VMEM((16, TALL, 256), F32), pltpu.SemaphoreType.DMA),
     )(where, slot1, folds, own, spread, blocks, extra, jnp.asarray(column_choice(), BF16))
     got0, got1 = transposed(send0, 0), transposed(send1, 1)

time: 158 us -> 152 us (0.962)
  blocking collectives: 74.1 us -> 63.6 us
  waiting for transfers between devices: 9.58 us -> 14.9 us
    all_to_all x4 -> x3, blocking collectives: 74.1 us -> 63.6 us  [exchanged(): return lax.all_to_all(x, axis, 0, 0, axis_index_groups=groups, tiled=True)]
    all_to_all x0 -> x1, waiting for transfers between devices: none -> 6.67 us  [on_device(): folds = lax.all_to_all(fold, 'row', 0, 0, tiled=True)]
    all_to_all x0 -> x1, starting transfers between devices: none -> 3.87 us  [on_device(): folds = lax.all_to_all(fold, 'row', 0, 0, tiled=True)]
    all_to_all x2 -> x1, starting transfers between devices: 7.42 us -> 4.01 us  [exchanged(): return lax.all_to_all(x, axis, 0, 0, axis_index_groups=groups, tiled=True)]
    all_to_all x2 -> x1, waiting for transfers between devices: 2.91 us -> 1.31 us  [exchanged(): return lax.all_to_all(x, axis, 0, 0, axis_index_groups=groups, tiled=True)]
  transfers between devices with their start and end apart: 7 -> 7, of which waited for: 5 -> 5; matrix products, arithmetic and copies ran while one was open for 1% -> 1% of each run, Pallas kernels for 6% -> 7%
where the time goes in v2:
time: 152 us; the launch traced here: 151 us
  blocking collectives  63.6 us (42%)
  starting transfers between devices  27.4 us (18%)
  Pallas kernels  26.4 us (17%)
  waiting for transfers between devices  14.9 us (10%)
  between operations  14.1 us (9%)
  local copies, waits for them, and re-layouts  3.86 us (3%)
    all_to_all x3, blocking collectives, exchanged(): return lax.all_to_all(x, axis, 0, 0, axis_index_groups=groups, tiled=True)  63.6 us
    ppermute x2, starting transfers between devices, transposed(): return lax.ppermute(x, ('row', 'col'), pairs)  11.2 us
    ppermute x2, starting transfers between devices, along_cols(): return (mine, lax.ppermute(mine, 'col', [(c, c ^ 1) for c in range(16)]))  8.3 us
    pallas_call x1, Pallas kernels, on_device(): kernel(image_body, (SMEM, SMEM, VMEM, VMEM, VMEM, ANY, VMEM, VMEM), (((EX...  7.81 us
    all_to_all x1, waiting for transfers between devices, on_device(): folds = lax.all_to_all(fold, 'row', 0, 0, tiled=True)  6.67 us
    ppermute x2, waiting for transfers between devices, transposed(): return lax.ppermute(x, ('row', 'col'), pairs)  4.71 us
    pallas_call x1, Pallas kernels, on_device(): kernel(second_body, (SMEM, SMEM, VMEM, VMEM, VMEM), (((EXT + 1024, 128),...  4.5 us
    all_to_all x1, starting transfers between devices, exchanged(): return lax.all_to_all(x, axis, 0, 0, axis_index_groups=groups, tiled=True)  4.01 us
  transfers between devices with their start and end apart: 7, of which 5 were waited for; matrix products, arithmetic and copies ran while one was open for 1% of the time, Pallas kernels for 7%

profile of v2, /device:TPU:1, one launch (start us, length us, event | category | flops | bytes accessed | tf_op | source)
XLA Modules:
  0.0 150.9 jit_solution(1111597738191424500)
XLA Ops:
  7.2 0.0 all-gather.3.cloned.1.call-start
  7.2 0.6 pad_add_fusion.where
  7.9 3.0 %shard_map.104 = (f32[144,256]{1,0:T(8,128)}, s32[12,128]{1,0:T(8,128)}, s32[12,128]{1,0:T(8,128)}, bf16[384,256]{1,0:T(8,128)(2,1)}) custom-call(s32[2]{0:T(128)} %pad_add_fusion.where, s32[12,128]{1,0:T(8,128)} %bitcast.15, s32[12,128]{1,0:T(8,128)} %bitcast.16, f32[9,9,4,128]{3,2,1,0:T(4,128)} %tiles.1), custom_call_target="tpu_custom_call" | custom-call | tf_op jit(solution)/shard_map/pallas_call | solution.py:376
  10.8 0.0 all-gather.3.cloned.1.call-update
  10.8 1.6 %shard_map.105 = (f32[8,48,128]{2,1,0:T(8,128)}, f32[8,40,128]{2,1,0:T(8,128)}) custom-call(f32[2,32,48]{2,1,0:T(8,128)} %bitcast.12, f32[1,32,48]{2,1,0:T(8,128)} %bitcast.13, f32[2,2,4,128]{3,2,1,0:T(4,128)} %d1.3), custom_call_target="tpu_custom_call" | custom-call | tf_op jit(solution)/shard_map/pallas_call | solution.py:370
  12.5 19.1 %all_to_all.25.mine = f32[8,40,128]{2,1,0:T(8,128)S(1)} all-to-all(f32[8,40,128]{2,1,0:T(8,128)} %get-tuple-element.21), channel_id=1, replica_groups={{0,2,4,6,8,10,12,14},{1,3,5,7,9,11,13,15},{16,18,20,22,24,26,28,30},{17..., dimensions={0} | all-to-all | bytes 327680 | tf_op jit(solution)/shard_map/all_to_all | solution.py:350
  31.6 0.0 copy-start.3
  31.6 15.5 %all_to_all.26 = f32[8,48,128]{2,1,0:T(8,128)S(1)} all-to-all(f32[8,48,128]{2,1,0:T(8,128)} %get-tuple-element.20), channel_id=1, replica_groups={{0,64,128,192,256,320,384,448},{16,80,144,208,272,336,400,464},{32,96,1..., dimensions={0} | all-to-all | bytes 393216 | tf_op jit(solution)/shard_map/all_to_all | solution.py:350
  47.1 0.9 broadcast_in_dim.3
  48.1 4.0 %all-to-all-start.1 = ((f32[4,8,48,128]{3,2,1,0:T(8,128)}), f32[4,8,48,128]{3,2,1,0:T(8,128)S(1)}, u32[]{:S(2)}, u32[]{:S(2)}) async-start(f32[4,8,48,128]{3,2,1,0:T(8,128)} %broadcast_in_dim.3), calls=%async_computation.1 | async-start | bytes 1572864 | tf_op jit(solution)/shard_map/all_to_all | solution.py:350
  52.1 6.0 %collective-permute-start = (f32[8,40,128]{2,1,0:T(8,128)S(1)}, f32[8,40,128]{2,1,0:T(8,128)S(1)}, u32[]{:S(2)}, u32[]{:S(2)}) collective-permute-start(f32[8,40,128]{2,1,0:T(8,128)S(1)} %all_to_all.25.mine), channel_id=1, source_target_pairs={{0,1},{1,0},{2,3},{3,2},{4,5},{5,4},{6,7},{7,6},{8,9},{9,8},{10,11... | collective-permute-start | bytes 491528 | tf_op jit(solution)/shard_map/ppermute | solution.py:360
  58.1 1.0 collective-permute-done.other
  59.1 0.0 copy-start.5
  59.1 1.3 all-to-all-done.1.panels
  60.4 0.0 copy-start
  60.4 0.0 copy-done.3
  60.4 0.0 copy-done.5
  60.4 0.9 copy-done
  61.3 4.5 %shard_map.106 = (f32[3072,128]{1,0:T(8,128)}, f32[32,16,128]{2,1,0:T(8,128)}, f32[32,128]{1,0:T(8,128)}) custom-call(s32[2]{0:T(128)} %pad_add_fusion.where, s32[1536]{0:T(1024)} %bitcast.14, f32[4,8,48,128]{3,2,1,0:T(8,128)} %copy-done, f32[8,40,128]{2,1,0:T(8,128)} %copy-done.3, f32[8,40,128]{2,1,0:T(8,128)} %copy-done.5), custom_call_target="tpu_custom_call" | custom-call | tf_op jit(solution)/shard_map/pallas_call | solution.py:387
  65.8 3.9 %all-to-all-start.3 = ((f32[32,16,128]{2,1,0:T(8,128)}), f32[32,16,128]{2,1,0:T(8,128)S(1)}, u32[]{:S(2)}, u32[]{:S(2)}) async-start(f32[32,16,128]{2,1,0:T(8,128)} %get-tuple-element.22), calls=%async_computation.3 | async-start | bytes 524288 | tf_op jit(solution)/shard_map/all_to_all | solution.py:393
  69.7 3.9 %shard_map.107.own = f32[2048,128]{1,0:T(8,128)} custom-call(s32[1536]{0:T(1024)} %bitcast.10, f32[4,8,48,128]{3,2,1,0:T(8,128)} %copy-done), custom_call_target="tpu_custom_call" | custom-call | tf_op jit(solution)/shard_map/pallas_call | solution.py:394
  73.6 6.7 %all-to-all-done.3.fold = f32[32,16,128]{2,1,0:T(8,128)S(1)} async-done(((f32[32,16,128]{2,1,0:T(8,128)}), f32[32,16,128]{2,1,0:T(8,128)S(1)}, u32[]{:S(2)}, u32[]{:S(2)}) %all-to-all-start.3) | async-done | bytes 262176 | tf_op jit(solution)/shard_map/all_to_all | solution.py:393
  80.3 0.0 copy-start.2
  80.3 0.0 all-gather.3.cloned.1.call-done
  80.3 0.7 copy-done.2
  80.9 7.8 %shard_map.108 = (f32[2048,128]{1,0:T(8,128)}, f32[64,128]{1,0:T(8,128)}, f32[64,128]{1,0:T(8,128)}) custom-call(s32[2]{0:T(128)} %pad_add_fusion.where, s32[1536]{0:T(1024)} %bitcast.11, f32[32,16,128]{2,1,0:T(8,128)} %copy-done.2, f32[2048,128]{1,0:T(8,128)} %shard_map.107.own, f32[3072,128]{1,0:T(8,128)} %get-tuple-element.23.second.spread, ...), custom_call_target="tpu_custom_call" | custom-call | tf_op jit(solution)/shard_map/pallas_call | solution.py:395
  88.8 9.3 %collective-permute-start.1 = (f32[64,128]{1,0:T(8,128)}, f32[64,128]{1,0:T(8,128)S(1)}, u32[]{:S(2)}, u32[]{:S(2)}) collective-permute-start(f32[64,128]{1,0:T(8,128)} %get-tuple-element.26), channel_id=1, source_target_pairs={{0,0},{1,32},{2,64},{3,96},{4,128},{5,160},{6,192},{7,224},{8,256}... | collective-permute-start | bytes 98312 | tf_op jit(solution)/shard_map/ppermute | solution.py:365
  98.1 1.9 %collective-permute-start.2 = (f32[64,128]{1,0:T(8,128)}, f32[64,128]{1,0:T(8,128)S(1)}, u32[]{:S(2)}, u32[]{:S(2)}) collective-permute-start(f32[64,128]{1,0:T(8,128)} %get-tuple-element.27), channel_id=1, source_target_pairs={{0,16},{1,48},{2,80},{3,112},{4,144},{5,176},{6,208},{7,240},{8,27... | collective-permute-start | bytes 98312 | tf_op jit(solution)/shard_map/ppermute | solution.py:365
  100.0 0.0 collective-permute-done.1.got0
  100.0 0.0 copy-start.6
  100.0 4.7 %collective-permute-done.2.got1 = f32[64,128]{1,0:T(8,128)S(1)} collective-permute-done((f32[64,128]{1,0:T(8,128)}, f32[64,128]{1,0:T(8,128)S(1)}, u32[]{:S(2)}, u32[]{:S(2)}) %collective-permute-start.2) | collective-permute-done | bytes 32800 | tf_op jit(solution)/shard_map/ppermute | solution.py:365
  104.7 0.0 copy-start.7
  104.7 0.0 copy-done.6
  104.7 0.6 copy-done.7
  105.3 2.3 %shard_map.109 = (f32[2,9,4,128]{3,2,1,0:T(4,128)}, f32[1,9,4,128]{3,2,1,0:T(4,128)}, f32[8,72,128]{2,1,0:T(8,128)}, f32[16,128]{1,0:T(8,128)}) custom-call(s32[2]{0:T(128)} %pad_add_fusion.where, f32[64,128]{1,0:T(8,128)} %copy-done.6, f32[64,128]{1,0:T(8,128)} %copy-done.7, bf16[512,512]{1,0:T(8,128)(2,1)} %constant.14.clone.order, ...), custom_call_target="tpu_custom_call" | custom-call | tf_op jit(solution)/shard_map/pallas_call | solution.py:402
  107.6 29.0 %all_to_all.27.mine = f32[8,72,128]{2,1,0:T(8,128)S(1)} all-to-all(f32[8,72,128]{2,1,0:T(8,128)} %get-tuple-element.29), channel_id=1, replica_groups={{0,2,4,6,8,10,12,14},{1,3,5,7,9,11,13,15},{16,18,20,22,24,26,28,30},{17..., dimensions={0} | all-to-all | bytes 589824 | tf_op jit(solution)/shard_map/all_to_all | solution.py:350
  136.6 0.0 copy-start.1
  136.6 2.3 %collective-permute-start.3 = (f32[8,72,128]{2,1,0:T(8,128)S(1)}, f32[8,72,128]{2,1,0:T(8,128)S(1)}, u32[]{:S(2)}, u32[]{:S(2)}) collective-permute-start(f32[8,72,128]{2,1,0:T(8,128)S(1)} %all_to_all.27.mine), channel_id=1, source_target_pairs={{0,1},{1,0},{2,3},{3,2},{4,5},{5,4},{6,7},{7,6},{8,9},{9,8},{10,11... | collective-permute-start | bytes 884744 | tf_op jit(solution)/shard_map/ppermute | solution.py:360
  138.9 1.2 collective-permute-done.3.other
  140.1 0.0 copy-start.4
  140.1 0.0 copy-done.1
  140.1 0.7 copy-done.4
  140.8 3.2 %shard_map.110 = (f32[2,11,4,128]{3,2,1,0:T(4,128)}, f32[1,12,4,128]{3,2,1,0:T(4,128)}) custom-call(s32[2]{0:T(128)} %pad_add_fusion.where, f32[8,72,128]{2,1,0:T(8,128)} %copy-done.1, f32[8,72,128]{2,1,0:T(8,128)} %copy-done.4, f32[2048,128]{1,0:T(8,128)} %get-tuple-element.30.right, f32[3072,128]{1,0:T(8,128)} %get-tuple-element.23.second.spread, ...), custom_call_target="tpu_custom_call" | custom-call | tf_op jit(solution)/shard_map/pallas_call | solution.py:408
Async XLA Ops:
  7.2 73.1 %all-gather.3.cloned.1.call-start = ((), (), s32[]{:S(2)}) async-start(), calls=%async_computation.5 | async-start | bytes 2506752 | tf_op jit(solution)/shard_map/all_gather | solution.py:382
  31.6 28.9 %copy-start.3 = (f32[8,40,128]{2,1,0:T(8,128)}, f32[8,40,128]{2,1,0:T(8,128)S(1)}, u32[]{:S(2)}) copy-start(f32[8,40,128]{2,1,0:T(8,128)S(1)} %all_to_all.25.mine) | copy-start | bytes 491524
  48.1 12.4 %all-to-all-start.1 = ((f32[4,8,48,128]{3,2,1,0:T(8,128)}), f32[4,8,48,128]{3,2,1,0:T(8,128)S(1)}, u32[]{:S(2)}, u32[]{:S(2)}) async-start(f32[4,8,48,128]{3,2,1,0:T(8,128)} %broadcast_in_dim.3), calls=%async_computation.1 | async-start | bytes 1572864 | tf_op jit(solution)/shard_map/all_to_all | solution.py:350
  52.1 7.0 %collective-permute-start = (f32[8,40,128]{2,1,0:T(8,128)S(1)}, f32[8,40,128]{2,1,0:T(8,128)S(1)}, u32[]{:S(2)}, u32[]{:S(2)}) collective-permute-start(f32[8,40,128]{2,1,0:T(8,128)S(1)} %all_to_all.25.mine), channel_id=1, source_target_pairs={{0,1},{1,0},{2,3},{3,2},{4,5},{5,4},{6,7},{7,6},{8,9},{9,8},{10,11... | collective-permute-start | bytes 491528 | tf_op jit(solution)/shard_map/ppermute | solution.py:360
  59.1 1.3 copy-start.5
  60.4 0.9 copy-start
  65.8 14.5 %all-to-all-start.3 = ((f32[32,16,128]{2,1,0:T(8,128)}), f32[32,16,128]{2,1,0:T(8,128)S(1)}, u32[]{:S(2)}, u32[]{:S(2)}) async-start(f32[32,16,128]{2,1,0:T(8,128)} %get-tuple-element.22), calls=%async_computation.3 | async-start | bytes 524288 | tf_op jit(solution)/shard_map/all_to_all | solution.py:393
  80.3 0.7 copy-start.2
  88.8 11.2 %collective-permute-start.1 = (f32[64,128]{1,0:T(8,128)}, f32[64,128]{1,0:T(8,128)S(1)}, u32[]{:S(2)}, u32[]{:S(2)}) collective-permute-start(f32[64,128]{1,0:T(8,128)} %get-tuple-element.26), channel_id=1, source_target_pairs={{0,0},{1,32},{2,64},{3,96},{4,128},{5,160},{6,192},{7,224},{8,256}... | collective-permute-start | bytes 98312 | tf_op jit(solution)/shard_map/ppermute | solution.py:365
  98.1 6.7 %collective-permute-start.2 = (f32[64,128]{1,0:T(8,128)}, f32[64,128]{1,0:T(8,128)S(1)}, u32[]{:S(2)}, u32[]{:S(2)}) collective-permute-start(f32[64,128]{1,0:T(8,128)} %get-tuple-element.27), channel_id=1, source_target_pairs={{0,16},{1,48},{2,80},{3,112},{4,144},{5,176},{6,208},{7,240},{8,27... | collective-permute-start | bytes 98312 | tf_op jit(solution)/shard_map/ppermute | solution.py:365
  100.0 4.7 %copy-start.6 = (f32[64,128]{1,0:T(8,128)}, f32[64,128]{1,0:T(8,128)S(1)}, u32[]{:S(2)}) copy-start(f32[64,128]{1,0:T(8,128)S(1)} %collective-permute-done.1.got0) | copy-start | bytes 98308
  104.7 0.6 copy-start.7
  136.6 3.5 %copy-start.1 = (f32[8,72,128]{2,1,0:T(8,128)}, f32[8,72,128]{2,1,0:T(8,128)S(1)}, u32[]{:S(2)}) copy-start(f32[8,72,128]{2,1,0:T(8,128)S(1)} %all_to_all.27.mine) | copy-start | bytes 884740
  136.6 3.5 %collective-permute-start.3 = (f32[8,72,128]{2,1,0:T(8,128)S(1)}, f32[8,72,128]{2,1,0:T(8,128)S(1)}, u32[]{:S(2)}, u32[]{:S(2)}) collective-permute-start(f32[8,72,128]{2,1,0:T(8,128)S(1)} %all_to_all.27.mine), channel_id=1, source_target_pairs={{0,1},{1,0},{2,3},{3,2},{4,5},{5,4},{6,7},{7,6},{8,9},{9,8},{10,11... | collective-permute-start | bytes 884744 | tf_op jit(solution)/shard_map/ppermute | solution.py:360
  140.1 0.7 copy-start.4
Sparse Core Ops, SparseCore 0:
  11.0 48.9 all-gather.2

commit v3 on v2

--- a/solution.py
+++ b/solution.py
@@ -5,6 +5,7 @@
 from jax.experimental import pallas as pl
 from jax.experimental.pallas import tpu as pltpu
 from jax.sharding import PartitionSpec as P
+
 
 F32 = jnp.float32
 BF16 = jnp.bfloat16
@@ -77,13 +78,17 @@
     return lax.broadcasted_iota(jnp.int32, shape, len(shape) - 1)
 
 
-def rank_body(where, s1, s2, tiles, packed, slot1, slot2, table, lhs, rhs, stage):
-    col = where[1]
+def rank_body(s1, s2, tiles, packed, slot1, slot2, table, later, lhs, rhs, stage):
+    col = lax.axis_index("col")
     upper = (
         lax.broadcasted_iota(jnp.int32, (128, 128), 0) < lax.broadcasted_iota(jnp.int32, (128, 128), 1)
     ).astype(BF16)
     groups = lax.broadcasted_iota(jnp.int32, (16, 128), 0)
     ranks = []
+    count = jnp.zeros((8, 1), F32)
+    listed = jnp.zeros((8, 384), F32)
+    spot = lax.broadcasted_iota(jnp.int32, (384, 128), 0).astype(F32)
+    kind = lax.broadcasted_iota(jnp.int32, (8, 128), 0)
     for which, (source, target) in enumerate(((s1, slot1), (s2, slot2))):
         carry = jnp.zeros((16, 1), F32)
         rank = []
@@ -99,10 +104,26 @@
             place = group * SLOTS + t.astype(jnp.int32)
             if which:
                 high = lax.shift_right_logical(row - 4608, 9)
-                other = EXT + group * 64 + high * 32 + jnp.bitwise_and(row, 31)
-                place = jnp.where(inside, place, other)
+                other = group * 64 + high * 32 + jnp.bitwise_and(row, 31)
+                place = jnp.where(inside, place, EXT)
+                mark = jnp.broadcast_to(jnp.where(inside, 0.0, 1.0), (8, 128))
+                order = dot(mark.astype(BF16), upper) + count
+                count = count + jnp.sum(mark, axis=1, keepdims=True)
+                order = jnp.where(mark[0:1] > 0, order[0:1], -1.0)
+                index = lanes_of((1, 128)) + m * 128
+                value = jnp.where(kind == 0, lax.shift_right_logical(index, 6), jnp.bitwise_and(index, 63))
+                value = jnp.where(kind == 2, lax.shift_right_logical(other, 6), value)
+                value = jnp.where(kind == 3, jnp.bitwise_and(other, 63), value)
+                value = jnp.where(kind == 4, 1, value)
+                match = (order == spot).astype(BF16)
+                listed = listed + lax.dot_general(
+                    value.astype(F32).astype(BF16), match, (((1,), (1,)), ((), ())), preferred_element_type=F32
+                )
             target[m : m + 1, :] = place
         ranks.append(rank)
+    source_row = listed[0:1] * 64.0 + listed[1:2]
+    target_row = jnp.where(listed[4:5] > 0.5, listed[2:3] * 64.0 + listed[3:4], 1024.0)
+    later[...] = jnp.concatenate([source_row, target_row], 0).astype(jnp.int32)
     slots = lanes_of((32, 128)).astype(F32)
     table[288:, :] = jnp.zeros((96, 256), BF16)
     for j in range(9):
@@ -134,8 +155,12 @@
     tall[32:64, 0:48] = p1[1]
     tall[64:96, 0:48] = p2[0]
     both = tall[...].T[:48]
+    lane = lanes_of((8, 128))
+    spare = [jnp.where(lane < 96, 0.0, pltpu.roll(both[40:48], 96 - 32 * g, 1)) for g in range(3)]
+    lane = lanes_of((40, 128))
+    value = jnp.where(lane < 96, both[:40], jnp.concatenate([*spare, jnp.zeros((16, 128), F32)], 0))
     for n in range(8):
-        panel[n] = both
+        panel[n] = value
     lane = lanes_of((4, 128))
     tall[0:48, :] = both
     for al in range(4):
@@ -161,28 +186,45 @@
 
 
 def in_order(step):
-    return pl.multiple_of(((step % 8) * 4 + step // 8) * 48, 16)
-
-
-def second_body(where, slot2, panels, mine, other, spread, fold, extra, rows):
+    return ((step % 8) * 4 + step // 8) * 48
+
+
+def opened(panels, step):
+    piece = panels[step // 8, step % 8]
+    lane = lanes_of((8, 128))
+    tail = pltpu.roll(piece[16:24], 96, 1)
+    tail = jnp.where(lane < 64, pltpu.roll(piece[8:16], 64, 1), tail)
+    tail = jnp.where(lane < 32, pltpu.roll(piece[0:8], 32, 1), tail)
+    return jnp.concatenate([piece, tail], 0)
+
+
+def second_body(later, panels, mine, other, spread, fold, extra, rows):
     lane = lanes_of((48, 128))
     keep = (lane >= 64) & (lane < 96)
 
-    def copy(step, _):
-        rows[pl.ds(in_order(step), 48), :] = jnp.where(keep, panels[step // 8, step % 8], 0.0)
-        return 0
-
-    lax.fori_loop(0, 32, copy, 0)
+    def copy(step):
+        rows[pl.ds(in_order(step), 48), :] = jnp.where(keep, opened(panels, step), 0.0)
+        return 0
+
+    for step in range(32):
+        copy(step)
     spread[...] = jnp.zeros(spread.shape, F32)
-    scatter_rows(slot2, rows, spread)
-    core = where[1] % 2
+
+    def place(step, _):
+        for u in range(48):
+            n = step * 48 + u
+            spread[pl.ds(later[1, n], 1), :] = rows[pl.ds(later[0, n], 1), :]
+        return 0
+
+    lax.fori_loop(0, 8, place, 0)
+    core = lax.axis_index("col") % 2
     half = lanes_of((40, 128)) < 64
     total = jnp.zeros((160, 256), F32)
     for z in range(8):
         for source, k in ((mine, core), (other, 1 - core)):
             x = source[z]
             left = jnp.concatenate([jnp.where(half, x, 0.0), jnp.where(half, 0.0, x)], 0)
-            right = spread[pl.ds(pl.multiple_of(EXT + (2 * z + k) * 64, 64), 64), :]
+            right = spread[pl.ds(pl.multiple_of((2 * z + k) * 64, 64), 64), :]
             total = total + product_terms(left, jnp.concatenate([right, right], 0))
     out = folded(total)
     lane_f = lanes_of((16, 128))
@@ -195,34 +237,47 @@
     extra[...] = out[48:80, :]
 
 
-def first_body(slot1, panels, spread, rows):
-    keep = lanes_of((48, 128)) < 64
-
-    def copy(step, _):
-        rows[pl.ds(in_order(step), 48), :] = jnp.where(keep, panels[step // 8, step % 8], 0.0)
-        return 0
-
-    lax.fori_loop(0, 32, copy, 0)
+def first_body(slot1, slot2, panels, own, spread, rows1, rows2):
+    lane = lanes_of((48, 128))
+
+    def copy(step):
+        value = opened(panels, step)
+        rows1[pl.ds(in_order(step), 48), :] = jnp.where(lane < 64, value, 0.0)
+        rows2[pl.ds(in_order(step), 48), :] = jnp.where((lane >= 64) & (lane < 96), value, 0.0)
+        return 0
+
+    for step in range(32):
+        copy(step)
+    own[...] = jnp.zeros(own.shape, F32)
     spread[...] = jnp.zeros(spread.shape, F32)
-    scatter_rows(slot1, rows, spread)
-
-
-def image_body(where, slot1, fold, own, second, blocks, extra, choice, right, send0, send1, rows, held, done):
+
+    def place(step, _):
+        base = pl.multiple_of(step * 48, 16)
+        for u in range(48):
+            own[pl.ds(slot1[base + u], 1), :] = rows1[pl.ds(base + u, 1), :]
+            spread[pl.ds(slot2[base + u], 1), :] = rows2[pl.ds(base + u, 1), :]
+        return 0
+
+    lax.fori_loop(0, 32, place, 0)
+
+
+def image_body(slot1, fold, own, second, blocks, extra, choice, right, send0, send1, rows, held, done):
     send = (send0, send1)
     arrival = pltpu.make_async_copy(blocks, held, done)
     arrival.start()
     keep = lanes_of((16, 128))
     keep = (keep >= 64) & (keep < 96)
 
-    def join(step, _):
+    def join(step):
         q = -fold[step]
-        base = pl.multiple_of(step * 48, 16)
+        base = step * 48
         for h in range(3):
             moved = pltpu.roll(q, (64 - 32 * h) % 128, 1)
             rows[pl.ds(base + 16 * h, 16), :] = jnp.where(keep, moved, 0.0)
         return 0
 
-    lax.fori_loop(0, 32, join, 0)
+    for step in range(32):
+        join(step)
     right[...] = jnp.zeros(right.shape, F32)
     scatter_rows(slot1, rows, right)
     right[...] = right[...] + own[...]
@@ -242,7 +297,7 @@
         tail = jnp.where(lane < 16, rest[0:16], pltpu.roll(rest[16:32], 16, 1))
         tail = jnp.where(lane < 32, tail, pltpu.roll(rest[32:48], 32, 1))
         pieces.append(jnp.concatenate([sent[h * 48 : (h + 1) * 48, :128], tail], 0))
-    parity = where[0] % 2
+    parity = lax.axis_index("row") % 2
     for h in range(2):
 
         @pl.when(parity == h)
@@ -251,8 +306,8 @@
             send[1][...] = pieces[1 - h]
 
 
-def cross_body(where, got0, got1, order, table, first, second, share, own):
-    parity = where[0] % 2
+def cross_body(got0, got1, order, table, first, second, share, own):
+    parity = lax.axis_index("row") % 2
     a, b = got0[...], got1[...]
     even = jnp.where(parity == 0, a, b)
     odd = jnp.where(parity == 0, b, a)
@@ -287,10 +342,10 @@
         second[0, i] = -two
 
 
-def diagonal_body(where, mine, other, right, spread, own, d1, d2, left1, left2, first, second):
+def diagonal_body(mine, other, right, spread, later, own, d1, d2, left1, left2, first, second):
     first[:, 0:9] = left1[...]
     second[:, 0:9] = left2[...]
-    core = where[1] % 2
+    core = lax.axis_index("col") % 2
     lane_e = lanes_of((8, 128))
     total = jnp.zeros((128, 256), F32)
     also = jnp.zeros((32, 256), F32)
@@ -306,7 +361,7 @@
             total = total + product_terms(left, jnp.concatenate([right[part, :], spread[part, :]], 0))
             e = x[64:72]
             left = jnp.concatenate([jnp.where(lane_e < 64, e, 0.0), jnp.where(lane_e >= 64, e, 0.0)], 0)
-            v = spread[pl.ds(pl.multiple_of(EXT + c * 64, 64), 64), :]
+            v = later[pl.ds(pl.multiple_of(c * 64, 64), 64), :]
             also = also + product_terms(left, jnp.concatenate([v, v], 0))
     out = folded(total)
     g1 = out[:32]
@@ -355,9 +410,8 @@
     return exchanged(jnp.broadcast_to(near, (4, *near.shape)), "row", X_GROUPS)
 
 
-def along_cols(x):
-    mine = exchanged(x, "col", Z_GROUPS)
-    return mine, lax.ppermute(mine, "col", [(c, c ^ 1) for c in range(16)])
+def swapped(x):
+    return lax.ppermute(x, "col", [(c, c ^ 1) for c in range(16)])
 
 
 def transposed(x, turn):
@@ -366,55 +420,59 @@
 
 
 def on_device(ancestor, inverse_first, panel_first, structure_first, inverse_second, panel_second, structure_second):
-    where = jnp.stack([lax.axis_index("row"), lax.axis_index("col")]).astype(jnp.int32)
     panel, mixed = kernel(
         lay_body,
         (VMEM, VMEM, VMEM),
-        (((8, 48, 128), F32), ((8, 40, 128), F32)),
+        (((8, 40, 128), F32), ((8, 40, 128), F32)),
         (pltpu.VMEM((128, 128), F32),),
     )(panel_first.transpose(1, 2, 0), panel_second.transpose(1, 2, 0), inverse_first)
-    packed, slot1, slot2, table = kernel(
+    packed, slot1, slot2, table, later = kernel(
         rank_body,
-        (SMEM, VMEM, VMEM, VMEM),
-        (((TALL, 256), F32), ((12, 128), jnp.int32), ((12, 128), jnp.int32), ((384, 256), BF16)),
+        (VMEM, VMEM, VMEM),
+        (((TALL, 256), F32), ((12, 128), jnp.int32), ((12, 128), jnp.int32), ((384, 256), BF16), ((2, 384), jnp.int32)),
         (pltpu.VMEM((3 * TALL, 1152), BF16), pltpu.VMEM((1152, 256), BF16), pltpu.VMEM((TALL, 128), F32)),
-    )(where, structure_first.reshape(12, 128), structure_second.reshape(12, 128), ancestor)
+    )(structure_first.reshape(12, 128), structure_second.reshape(12, 128), ancestor)
     blocks = lax.all_gather(packed, "col")
+    mine = exchanged(mixed, "col", Z_GROUPS)
+    other = swapped(mine)
     panels = along_rows(panel)
-    mine, other = along_cols(mixed)
     slot1, slot2 = slot1.reshape(1536), slot2.reshape(1536)
     rows = pltpu.VMEM((1536, 128), F32)
-    spread, fold, extra = kernel(
+    second, fold, extra = kernel(
         second_body,
-        (SMEM, SMEM, VMEM, VMEM, VMEM),
-        (((EXT + 1024, 128), F32), ((32, 16, 128), F32), ((32, 128), F32)),
+        (SMEM, VMEM, VMEM, VMEM),
+        (((1032, 128), F32), ((32, 16, 128), F32), ((32, 128), F32)),
         (rows,),
-    )(where, slot2, panels, mine, other)
+    )(later, panels, mine, other)
     folds = lax.all_to_all(fold, "row", 0, 0, tiled=True)
-    (own,) = kernel(first_body, (SMEM, VMEM), (((EXT, 128), F32),), (rows,))(slot1, panels)
+    own, spread = kernel(
+        first_body, (SMEM, SMEM, VMEM), (((EXT, 128), F32), ((EXT + 8, 128), F32)), (rows, rows)
+    )(slot1, slot2, panels)
     right, send0, send1 = kernel(
         image_body,
-        (SMEM, SMEM, VMEM, VMEM, VMEM, ANY, VMEM, VMEM),
+        (SMEM, VMEM, VMEM, VMEM, ANY, VMEM, VMEM),
         (((EXT, 128), F32), ((64, 128), F32), ((64, 128), F32)),
         (rows, pltpu.VMEM((16, TALL, 256), F32), pltpu.SemaphoreType.DMA),
-    )(where, slot1, folds, own, spread, blocks, extra, jnp.asarray(column_choice(), BF16))
+    )(slot1, folds, own, spread, blocks, extra, jnp.asarray(column_choice(), BF16))
     got0, got1 = transposed(send0, 0), transposed(send1, 1)
     left1, left2, share, own = kernel(
         cross_body,
-        (SMEM, VMEM, VMEM, VMEM, VMEM),
+        (VMEM, VMEM, VMEM, VMEM),
         (((2, 9, 4, 128), F32), ((1, 9, 4, 128), F32), ((8, 72, 128), F32), ((16, 128), F32)),
-    )(where, got0, got1, jnp.asarray(lane_order(), BF16), table)
-    mine, other = along_cols(share)
+    )(got0, got1, jnp.asarray(lane_order(), BF16), table)
+    mine = exchanged(share, "col", Z_GROUPS)
+    other = swapped(mine)
     return kernel(
         diagonal_body,
-        (SMEM,) + (VMEM,) * 9,
+        (VMEM,) * 10,
         (((2, 11, 4, 128), F32), ((1, 12, 4, 128), F32)),
-    )(where, mine, other, right, spread, own, inverse_first, inverse_second, left1, left2)
+    )(mine, other, right, spread, second, own, inverse_first, inverse_second, left1, left2)
 
 
 def solution(mesh):
     tiles = P(None, None, "row", "col")
     panels = P("row", None, "col")
+
     return jax.shard_map(
         on_device,
         mesh=mesh,

time: 152 us -> 150 us (0.987)
  waiting for transfers between devices: 14.9 us -> 13 us
where the time goes in v3:
time: 150 us; the launch traced here: 149 us
  blocking collectives  65 us (43%)
  starting transfers between devices  27.6 us (18%)
  Pallas kernels  25.9 us (17%)
  between operations  14.1 us (9%)
  waiting for transfers between devices  13 us (9%)
  local copies, waits for them, and re-layouts  3.73 us (2%)
    all_to_all x3, blocking collectives, exchanged(): return lax.all_to_all(x, axis, 0, 0, axis_index_groups=groups, tiled=True)  65 us
    ppermute x2, starting transfers between devices, transposed(): return lax.ppermute(x, ('row', 'col'), pairs)  10.5 us
    ppermute x2, starting transfers between devices, swapped(): return lax.ppermute(x, 'col', [(c, c ^ 1) for c in range(16)])  8.33 us
    all_to_all x1, waiting for transfers between devices, on_device(): folds = lax.all_to_all(fold, 'row', 0, 0, tiled=True)  5.55 us
    pallas_call x1, Pallas kernels, on_device(): kernel(image_body, (SMEM, VMEM, VMEM, VMEM, ANY, VMEM, VMEM), (((EXT, 128...  5.52 us
    pallas_call x1, Pallas kernels, on_device(): kernel(first_body, (SMEM, SMEM, VMEM), (((EXT, 128), F32), ((EXT + 8, 128...  4.85 us
    all_to_all x1, starting transfers between devices, on_device(): folds = lax.all_to_all(fold, 'row', 0, 0, tiled=True)  4.8 us
    ppermute x2, waiting for transfers between devices, transposed(): return lax.ppermute(x, ('row', 'col'), pairs)  4.71 us
  transfers between devices with their start and end apart: 7, of which 5 were waited for; matrix products, arithmetic and copies ran while one was open for 1% of the time, Pallas kernels for 7%

profile of v3, /device:TPU:1, one launch (start us, length us, event | category | flops | bytes accessed | tf_op | source)
XLA Modules:
  0.0 149.3 jit_solution(10747015442766851685)
XLA Ops:
  7.2 0.0 all-gather.3.cloned.1.call-start
  7.2 4.4 %shard_map.104 = (f32[144,256]{1,0:T(8,128)}, s32[12,128]{1,0:T(8,128)}, s32[12,128]{1,0:T(8,128)}, bf16[384,256]{1,0:T(8,128)(2,1)}, s32[2,384]{1,0:T(2,128)}) custom-call(s32[12,128]{1,0:T(8,128)} %bitcast.13, s32[12,128]{1,0:T(8,128)} %bitcast.14, f32[9,9,4,128]{3,2,1,0:T(4,128)} %tiles.1), custom_call_target="tpu_custom_call" | custom-call | tf_op jit(solution)/shard_map/pallas_call | solution.py:429
  11.6 0.0 all-gather.3.cloned.1.call-update
  11.6 1.7 %shard_map.105 = (f32[8,40,128]{2,1,0:T(8,128)}, f32[8,40,128]{2,1,0:T(8,128)}) custom-call(f32[2,32,48]{2,1,0:T(8,128)} %bitcast.10, f32[1,32,48]{2,1,0:T(8,128)} %bitcast.11, f32[2,2,4,128]{3,2,1,0:T(4,128)} %d1.3), custom_call_target="tpu_custom_call" | custom-call | tf_op jit(solution)/shard_map/pallas_call | solution.py:423
  13.3 16.0 %all_to_all.25 = f32[8,40,128]{2,1,0:T(8,128)S(1)} all-to-all(f32[8,40,128]{2,1,0:T(8,128)} %get-tuple-element.23), channel_id=1, replica_groups={{0,64,128,192,256,320,384,448},{16,80,144,208,272,336,400,464},{32,96,1..., dimensions={0} | all-to-all | bytes 327680 | tf_op jit(solution)/shard_map/all_to_all | solution.py:405
  29.3 19.8 %all_to_all.26.mine = f32[8,40,128]{2,1,0:T(8,128)S(1)} all-to-all(f32[8,40,128]{2,1,0:T(8,128)} %get-tuple-element.24), channel_id=1, replica_groups={{0,2,4,6,8,10,12,14},{1,3,5,7,9,11,13,15},{16,18,20,22,24,26,28,30},{17..., dimensions={0} | all-to-all | bytes 327680 | tf_op jit(solution)/shard_map/all_to_all | solution.py:405
  49.0 0.0 copy-start.3
  49.1 0.9 broadcast_in_dim.3
  49.9 3.9 %all-to-all-start.1 = ((f32[4,8,40,128]{3,2,1,0:T(8,128)}), f32[4,8,40,128]{3,2,1,0:T(8,128)S(1)}, u32[]{:S(2)}, u32[]{:S(2)}) async-start(f32[4,8,40,128]{3,2,1,0:T(8,128)} %broadcast_in_dim.3), calls=%async_computation.1 | async-start | bytes 1310720 | tf_op jit(solution)/shard_map/all_to_all | solution.py:405
  53.8 6.0 %collective-permute-start = (f32[8,40,128]{2,1,0:T(8,128)S(1)}, f32[8,40,128]{2,1,0:T(8,128)S(1)}, u32[]{:S(2)}, u32[]{:S(2)}) collective-permute-start(f32[8,40,128]{2,1,0:T(8,128)S(1)} %all_to_all.26.mine), channel_id=1, source_target_pairs={{0,1},{1,0},{2,3},{3,2},{4,5},{5,4},{6,7},{7,6},{8,9},{9,8},{10,11... | collective-permute-start | bytes 491528 | tf_op jit(solution)/shard_map/ppermute | solution.py:414
  59.9 1.0 collective-permute-done.other
  60.9 0.0 copy-start.5
  60.9 0.6 all-to-all-done.1.panels
  61.5 0.0 copy-start
  61.5 0.0 copy-done.3
  61.5 0.1 copy-done.5
  61.6 0.7 copy-done
  62.3 3.9 %shard_map.106 = (f32[1032,128]{1,0:T(8,128)}, f32[32,16,128]{2,1,0:T(8,128)}, f32[32,128]{1,0:T(8,128)}) custom-call(s32[2,384]{1,0:T(2,128)} %get-tuple-element.22.later, f32[4,8,40,128]{3,2,1,0:T(8,128)} %copy-done, f32[8,40,128]{2,1,0:T(8,128)} %copy-done.3, f32[8,40,128]{2,1,0:T(8,128)} %copy-done.5), custom_call_target="tpu_custom_call" | custom-call | tf_op jit(solution)/shard_map/pallas_call | solution.py:441
  66.2 4.8 %all-to-all-start.3 = ((f32[32,16,128]{2,1,0:T(8,128)}), f32[32,16,128]{2,1,0:T(8,128)S(1)}, u32[]{:S(2)}, u32[]{:S(2)}) async-start(f32[32,16,128]{2,1,0:T(8,128)} %get-tuple-element.25), calls=%async_computation.3 | async-start | bytes 524288 | tf_op jit(solution)/shard_map/all_to_all | solution.py:447
  71.0 4.8 %shard_map.107 = (f32[2048,128]{1,0:T(8,128)}, f32[2056,128]{1,0:T(8,128)}) custom-call(s32[1536]{0:T(1024)} %bitcast.8, s32[1536]{0:T(1024)} %bitcast.12, f32[4,8,40,128]{3,2,1,0:T(8,128)} %copy-done), custom_call_target="tpu_custom_call" | custom-call | tf_op jit(solution)/shard_map/pallas_call | solution.py:448
  75.9 5.6 %all-to-all-done.3.fold = f32[32,16,128]{2,1,0:T(8,128)S(1)} async-done(((f32[32,16,128]{2,1,0:T(8,128)}), f32[32,16,128]{2,1,0:T(8,128)S(1)}, u32[]{:S(2)}, u32[]{:S(2)}) %all-to-all-start.3) | async-done | bytes 262176 | tf_op jit(solution)/shard_map/all_to_all | solution.py:447
  81.4 0.0 copy-start.2
  81.4 0.0 all-gather.3.cloned.1.call-done
  81.4 0.7 copy-done.2
  82.1 5.5 %shard_map.108 = (f32[2048,128]{1,0:T(8,128)}, f32[64,128]{1,0:T(8,128)}, f32[64,128]{1,0:T(8,128)}) custom-call(s32[1536]{0:T(1024)} %bitcast.9, f32[32,16,128]{2,1,0:T(8,128)} %copy-done.2, f32[2048,128]{1,0:T(8,128)} %get-tuple-element.27.own, f32[2056,128]{1,0:T(8,128)} %get-tuple-element.28.second.spread, f32[16,144,256]{2,1,0:T(8,128)} %bitcast.7, ...), custom_call_target="tpu_custom_call" | custom-call | tf_op jit(solution)/shard_map/pallas_call | solution.py:451
  87.7 8.6 %collective-permute-start.1 = (f32[64,128]{1,0:T(8,128)}, f32[64,128]{1,0:T(8,128)S(1)}, u32[]{:S(2)}, u32[]{:S(2)}) collective-permute-start(f32[64,128]{1,0:T(8,128)} %get-tuple-element.31), channel_id=1, source_target_pairs={{0,0},{1,32},{2,64},{3,96},{4,128},{5,160},{6,192},{7,224},{8,256}... | collective-permute-start | bytes 98312 | tf_op jit(solution)/shard_map/ppermute | solution.py:419
  96.2 1.9 %collective-permute-start.2 = (f32[64,128]{1,0:T(8,128)}, f32[64,128]{1,0:T(8,128)S(1)}, u32[]{:S(2)}, u32[]{:S(2)}) collective-permute-start(f32[64,128]{1,0:T(8,128)} %get-tuple-element.32), channel_id=1, source_target_pairs={{0,16},{1,48},{2,80},{3,112},{4,144},{5,176},{6,208},{7,240},{8,27... | collective-permute-start | bytes 98312 | tf_op jit(solution)/shard_map/ppermute | solution.py:419
  98.2 0.0 collective-permute-done.1.got0
  98.2 0.0 copy-start.6
  98.2 4.7 %collective-permute-done.2.got1 = f32[64,128]{1,0:T(8,128)S(1)} collective-permute-done((f32[64,128]{1,0:T(8,128)}, f32[64,128]{1,0:T(8,128)S(1)}, u32[]{:S(2)}, u32[]{:S(2)}) %collective-permute-start.2) | collective-permute-done | bytes 32800 | tf_op jit(solution)/shard_map/ppermute | solution.py:419
  102.9 0.0 copy-start.7
  102.9 0.0 copy-done.6
  102.9 0.6 copy-done.7
  103.5 2.3 %shard_map.109 = (f32[2,9,4,128]{3,2,1,0:T(4,128)}, f32[1,9,4,128]{3,2,1,0:T(4,128)}, f32[8,72,128]{2,1,0:T(8,128)}, f32[16,128]{1,0:T(8,128)}) custom-call(f32[64,128]{1,0:T(8,128)} %copy-done.6, f32[64,128]{1,0:T(8,128)} %copy-done.7, bf16[512,512]{1,0:T(8,128)(2,1)} %constant.5.clone.order, bf16[384,256]{1,0:T(8,128)(2,1)} %get-tuple-element.33.table), custom_call_target="tpu_custom_call" | custom-call | tf_op jit(solution)/shard_map/pallas_call | solution.py:458
  105.8 29.2 %all_to_all.27.mine = f32[8,72,128]{2,1,0:T(8,128)S(1)} all-to-all(f32[8,72,128]{2,1,0:T(8,128)} %get-tuple-element.34), channel_id=1, replica_groups={{0,2,4,6,8,10,12,14},{1,3,5,7,9,11,13,15},{16,18,20,22,24,26,28,30},{17..., dimensions={0} | all-to-all | bytes 589824 | tf_op jit(solution)/shard_map/all_to_all | solution.py:405
  135.0 0.0 copy-start.1
  135.0 2.3 %collective-permute-start.3 = (f32[8,72,128]{2,1,0:T(8,128)S(1)}, f32[8,72,128]{2,1,0:T(8,128)S(1)}, u32[]{:S(2)}, u32[]{:S(2)}) collective-permute-start(f32[8,72,128]{2,1,0:T(8,128)S(1)} %all_to_all.27.mine), channel_id=1, source_target_pairs={{0,1},{1,0},{2,3},{3,2},{4,5},{5,4},{6,7},{7,6},{8,9},{9,8},{10,11... | collective-permute-start | bytes 884744 | tf_op jit(solution)/shard_map/ppermute | solution.py:414
  137.3 1.2 collective-permute-done.3.other
  138.5 0.0 copy-start.4
  138.5 0.0 copy-done.1
  138.5 0.7 copy-done.4
  139.2 3.2 %shard_map.110 = (f32[2,11,4,128]{3,2,1,0:T(4,128)}, f32[1,12,4,128]{3,2,1,0:T(4,128)}) custom-call(f32[8,72,128]{2,1,0:T(8,128)} %copy-done.1, f32[8,72,128]{2,1,0:T(8,128)} %copy-done.4, f32[2048,128]{1,0:T(8,128)} %get-tuple-element.35.right, f32[2056,128]{1,0:T(8,128)} %get-tuple-element.28.second.spread, f32[1032,128]{1,0:T(8,128)} %get-tuple-element.36.later, ...), custom_call_target="tpu_custom_call" | custom-call | tf_op jit(solution)/shard_map/pallas_call | solution.py:465
Async XLA Ops:
  7.2 74.3 %all-gather.3.cloned.1.call-start = ((), (), s32[]{:S(2)}) async-start(), calls=%async_computation.5 | async-start | bytes 2506752 | tf_op jit(solution)/shard_map/all_gather | solution.py:435
  49.0 12.4 %copy-start.3 = (f32[8,40,128]{2,1,0:T(8,128)}, f32[8,40,128]{2,1,0:T(8,128)S(1)}, u32[]{:S(2)}) copy-start(f32[8,40,128]{2,1,0:T(8,128)S(1)} %all_to_all.26.mine) | copy-start | bytes 491524
  49.9 11.5 %all-to-all-start.1 = ((f32[4,8,40,128]{3,2,1,0:T(8,128)}), f32[4,8,40,128]{3,2,1,0:T(8,128)S(1)}, u32[]{:S(2)}, u32[]{:S(2)}) async-start(f32[4,8,40,128]{3,2,1,0:T(8,128)} %broadcast_in_dim.3), calls=%async_computation.1 | async-start | bytes 1310720 | tf_op jit(solution)/shard_map/all_to_all | solution.py:405
  53.8 7.1 %collective-permute-start = (f32[8,40,128]{2,1,0:T(8,128)S(1)}, f32[8,40,128]{2,1,0:T(8,128)S(1)}, u32[]{:S(2)}, u32[]{:S(2)}) collective-permute-start(f32[8,40,128]{2,1,0:T(8,128)S(1)} %all_to_all.26.mine), channel_id=1, source_target_pairs={{0,1},{1,0},{2,3},{3,2},{4,5},{5,4},{6,7},{7,6},{8,9},{9,8},{10,11... | collective-permute-start | bytes 491528 | tf_op jit(solution)/shard_map/ppermute | solution.py:414
  60.9 0.7 copy-start.5
  61.5 0.8 copy-start
  66.2 15.2 %all-to-all-start.3 = ((f32[32,16,128]{2,1,0:T(8,128)}), f32[32,16,128]{2,1,0:T(8,128)S(1)}, u32[]{:S(2)}, u32[]{:S(2)}) async-start(f32[32,16,128]{2,1,0:T(8,128)} %get-tuple-element.25), calls=%async_computation.3 | async-start | bytes 524288 | tf_op jit(solution)/shard_map/all_to_all | solution.py:447
  81.4 0.7 copy-start.2
  87.7 10.5 %collective-permute-start.1 = (f32[64,128]{1,0:T(8,128)}, f32[64,128]{1,0:T(8,128)S(1)}, u32[]{:S(2)}, u32[]{:S(2)}) collective-permute-start(f32[64,128]{1,0:T(8,128)} %get-tuple-element.31), channel_id=1, source_target_pairs={{0,0},{1,32},{2,64},{3,96},{4,128},{5,160},{6,192},{7,224},{8,256}... | collective-permute-start | bytes 98312 | tf_op jit(solution)/shard_map/ppermute | solution.py:419
  96.2 6.7 %collective-permute-start.2 = (f32[64,128]{1,0:T(8,128)}, f32[64,128]{1,0:T(8,128)S(1)}, u32[]{:S(2)}, u32[]{:S(2)}) collective-permute-start(f32[64,128]{1,0:T(8,128)} %get-tuple-element.32), channel_id=1, source_target_pairs={{0,16},{1,48},{2,80},{3,112},{4,144},{5,176},{6,208},{7,240},{8,27... | collective-permute-start | bytes 98312 | tf_op jit(solution)/shard_map/ppermute | solution.py:419
  98.2 4.7 %copy-start.6 = (f32[64,128]{1,0:T(8,128)}, f32[64,128]{1,0:T(8,128)S(1)}, u32[]{:S(2)}) copy-start(f32[64,128]{1,0:T(8,128)S(1)} %collective-permute-done.1.got0) | copy-start | bytes 98308
  102.9 0.6 copy-start.7
  135.0 3.5 %copy-start.1 = (f32[8,72,128]{2,1,0:T(8,128)}, f32[8,72,128]{2,1,0:T(8,128)S(1)}, u32[]{:S(2)}) copy-start(f32[8,72,128]{2,1,0:T(8,128)S(1)} %all_to_all.27.mine) | copy-start | bytes 884740
  135.0 3.5 %collective-permute-start.3 = (f32[8,72,128]{2,1,0:T(8,128)S(1)}, f32[8,72,128]{2,1,0:T(8,128)S(1)}, u32[]{:S(2)}, u32[]{:S(2)}) collective-permute-start(f32[8,72,128]{2,1,0:T(8,128)S(1)} %all_to_all.27.mine), channel_id=1, source_target_pairs={{0,1},{1,0},{2,3},{3,2},{4,5},{5,4},{6,7},{7,6},{8,9},{9,8},{10,11... | collective-permute-start | bytes 884744 | tf_op jit(solution)/shard_map/ppermute | solution.py:414
  138.5 0.7 copy-start.4
Sparse Core Ops, SparseCore 0:
  11.7 50.1 all-gather.2

commit v4 on v3

--- a/solution.py
+++ b/solution.py
@@ -149,18 +149,20 @@
     packed[...] = out[:TALL] + (out[TALL : 2 * TALL] + out[2 * TALL :])
 
 
-def lay_body(p1, p2, d1, panel, mixed, tall):
+def lay_body(p1, p2, d1, panel, near, mixed, tall):
     tall[...] = jnp.zeros((128, 128), F32)
     tall[0:32, 0:48] = p1[0]
     tall[32:64, 0:48] = p1[1]
     tall[64:96, 0:48] = p2[0]
     both = tall[...].T[:48]
-    lane = lanes_of((8, 128))
-    spare = [jnp.where(lane < 96, 0.0, pltpu.roll(both[40:48], 96 - 32 * g, 1)) for g in range(3)]
-    lane = lanes_of((40, 128))
-    value = jnp.where(lane < 96, both[:40], jnp.concatenate([*spare, jnp.zeros((16, 128), F32)], 0))
-    for n in range(8):
+    lane = lanes_of((16, 128))
+    value = jnp.zeros((16, 128), F32)
+    for h in range(3):
+        moved = pltpu.roll(both[16 * h : 16 * (h + 1)], (32 * h - 64) % 128, 1)
+        value = jnp.where(lane // 32 == h, moved, value)
+    for n in range(32):
         panel[n] = value
+    near[...] = jnp.where(lanes_of((24, 128)) < 64, both[:24], pltpu.roll(both[24:], 64, 1))
     lane = lanes_of((4, 128))
     tall[0:48, :] = both
     for al in range(4):
@@ -189,25 +191,17 @@
     return ((step % 8) * 4 + step // 8) * 48
 
 
-def opened(panels, step):
-    piece = panels[step // 8, step % 8]
-    lane = lanes_of((8, 128))
-    tail = pltpu.roll(piece[16:24], 96, 1)
-    tail = jnp.where(lane < 64, pltpu.roll(piece[8:16], 64, 1), tail)
-    tail = jnp.where(lane < 32, pltpu.roll(piece[0:8], 32, 1), tail)
-    return jnp.concatenate([piece, tail], 0)
-
-
-def second_body(later, panels, mine, other, spread, fold, extra, rows):
-    lane = lanes_of((48, 128))
-    keep = (lane >= 64) & (lane < 96)
-
-    def copy(step):
-        rows[pl.ds(in_order(step), 48), :] = jnp.where(keep, opened(panels, step), 0.0)
-        return 0
-
-    for step in range(32):
-        copy(step)
+def unfold(folds, rows):
+    keep = lanes_of((16, 128))
+    keep = (keep >= 64) & (keep < 96)
+    for r in range(32):
+        for h in range(3):
+            moved = pltpu.roll(folds[r], (64 - 32 * h) % 128, 1)
+            rows[r * 48 + 16 * h : r * 48 + 16 * (h + 1), :] = jnp.where(keep, moved, 0.0)
+
+
+def second_body(later, panels, near, mine, other, spread, fold, extra, rows):
+    unfold(panels, rows)
     spread[...] = jnp.zeros(spread.shape, F32)
 
     def place(step, _):
@@ -232,55 +226,37 @@
     for h in range(3):
         moved = pltpu.roll(out[16 * h : 16 * (h + 1), :], (32 * h - 64) % 128, 1)
         value = jnp.where(lane_f // 32 == h, moved, value)
-    for n in range(32):
+    value = jnp.concatenate([value, near[...]], 0)
+    for n in range(8):
         fold[n] = value
     extra[...] = out[48:80, :]
 
 
-def first_body(slot1, slot2, panels, own, spread, rows1, rows2):
-    lane = lanes_of((48, 128))
-
-    def copy(step):
-        value = opened(panels, step)
-        rows1[pl.ds(in_order(step), 48), :] = jnp.where(lane < 64, value, 0.0)
-        rows2[pl.ds(in_order(step), 48), :] = jnp.where((lane >= 64) & (lane < 96), value, 0.0)
-        return 0
-
+def first_body(slot2, panels, spread, rows):
+    unfold(panels, rows)
+    spread[...] = jnp.zeros(spread.shape, F32)
+    scatter_rows(slot2, rows, spread)
+
+
+def image_body(slot1, folds, second_hbm, blocks, extra, choice, out, send0, send1, rows, held, second, right, done):
+    send = (send0, send1)
+    third = pltpu.make_async_copy(second_hbm.at[pl.ds(0, EXT)], second, done.at[0])
+    arrival = pltpu.make_async_copy(blocks, held, done.at[1])
+    leaving = pltpu.make_async_copy(right, out, done.at[2])
+    third.start()
+    arrival.start()
+    lane = lanes_of((16, 128))
     for step in range(32):
-        copy(step)
-    own[...] = jnp.zeros(own.shape, F32)
-    spread[...] = jnp.zeros(spread.shape, F32)
-
-    def place(step, _):
-        base = pl.multiple_of(step * 48, 16)
-        for u in range(48):
-            own[pl.ds(slot1[base + u], 1), :] = rows1[pl.ds(base + u, 1), :]
-            spread[pl.ds(slot2[base + u], 1), :] = rows2[pl.ds(base + u, 1), :]
-        return 0
-
-    lax.fori_loop(0, 32, place, 0)
-
-
-def image_body(slot1, fold, own, second, blocks, extra, choice, right, send0, send1, rows, held, done):
-    send = (send0, send1)
-    arrival = pltpu.make_async_copy(blocks, held, done)
-    arrival.start()
-    keep = lanes_of((16, 128))
-    keep = (keep >= 64) & (keep < 96)
-
-    def join(step):
-        q = -fold[step]
-        base = step * 48
+        piece = folds[step // 8, step % 8]
+        base = in_order(step)
+        near = jnp.concatenate([piece[16:], pltpu.roll(piece[16:], 64, 1)], 0)
         for h in range(3):
-            moved = pltpu.roll(q, (64 - 32 * h) % 128, 1)
-            rows[pl.ds(base + 16 * h, 16), :] = jnp.where(keep, moved, 0.0)
-        return 0
-
-    for step in range(32):
-        join(step)
+            moved = jnp.where(lane < 96, -pltpu.roll(piece[:16], (64 - 32 * h) % 128, 1), 0.0)
+            rows[base + 16 * h : base + 16 * (h + 1), :] = jnp.where(lane < 64, near[16 * h : 16 * (h + 1)], moved)
     right[...] = jnp.zeros(right.shape, F32)
     scatter_rows(slot1, rows, right)
-    right[...] = right[...] + own[...]
+    leaving.start()
+    third.wait()
     arrival.wait()
     total = jnp.zeros((2 * TALL, 256), F32)
     for c in range(16):
@@ -304,6 +280,8 @@
         def _(h=h):
             send[0][...] = pieces[h]
             send[1][...] = pieces[1 - h]
+
+    leaving.wait()
 
 
 def cross_body(got0, got1, order, table, first, second, share, own):
@@ -391,11 +369,11 @@
 ANY = pl.BlockSpec(memory_space=pl.ANY)
 
 
-def kernel(body, specs, outs, scratch=()):
+def kernel(body, specs, outs, scratch=(), places=None):
     return pl.pallas_call(
         body,
         in_specs=list(specs),
-        out_specs=[VMEM] * len(outs),
+        out_specs=list(places or [VMEM] * len(outs)),
         out_shape=[jax.ShapeDtypeStruct(shape, dtype) for shape, dtype in outs],
         scratch_shapes=list(scratch),
     )
@@ -405,11 +383,6 @@
     return lax.all_to_all(x, axis, 0, 0, axis_index_groups=groups, tiled=True)
 
 
-def along_rows(x):
-    near = exchanged(x, "row", Y_GROUPS)
-    return exchanged(jnp.broadcast_to(near, (4, *near.shape)), "row", X_GROUPS)
-
-
 def swapped(x):
     return lax.ppermute(x, "col", [(c, c ^ 1) for c in range(16)])
 
@@ -420,10 +393,10 @@
 
 
 def on_device(ancestor, inverse_first, panel_first, structure_first, inverse_second, panel_second, structure_second):
-    panel, mixed = kernel(
+    panel, near, mixed = kernel(
         lay_body,
         (VMEM, VMEM, VMEM),
-        (((8, 40, 128), F32), ((8, 40, 128), F32)),
+        (((32, 16, 128), F32), ((24, 128), F32), ((8, 40, 128), F32)),
         (pltpu.VMEM((128, 128), F32),),
     )(panel_first.transpose(1, 2, 0), panel_second.transpose(1, 2, 0), inverse_first)
     packed, slot1, slot2, table, later = kernel(
@@ -435,25 +408,26 @@
     blocks = lax.all_gather(packed, "col")
     mine = exchanged(mixed, "col", Z_GROUPS)
     other = swapped(mine)
-    panels = along_rows(panel)
+    panels = lax.all_to_all(panel, "row", 0, 0, tiled=True)
     slot1, slot2 = slot1.reshape(1536), slot2.reshape(1536)
     rows = pltpu.VMEM((1536, 128), F32)
     second, fold, extra = kernel(
         second_body,
-        (SMEM, VMEM, VMEM, VMEM),
-        (((1032, 128), F32), ((32, 16, 128), F32), ((32, 128), F32)),
+        (SMEM, VMEM, VMEM, VMEM, VMEM),
+        (((1032, 128), F32), ((8, 40, 128), F32), ((32, 128), F32)),
         (rows,),
-    )(later, panels, mine, other)
-    folds = lax.all_to_all(fold, "row", 0, 0, tiled=True)
-    own, spread = kernel(
-        first_body, (SMEM, SMEM, VMEM), (((EXT, 128), F32), ((EXT + 8, 128), F32)), (rows, rows)
-    )(slot1, slot2, panels)
+    )(later, panels, near, mine, other)
+    folds = exchanged(fold, "row", Y_GROUPS)
+    folds = exchanged(jnp.broadcast_to(folds, (4, *folds.shape)), "row", X_GROUPS)
+    (spread,) = kernel(first_body, (SMEM, VMEM), (((EXT + 8, 128), F32),), (rows,))(slot2, panels)
+    big = pltpu.VMEM((EXT, 128), F32)
     right, send0, send1 = kernel(
         image_body,
-        (SMEM, VMEM, VMEM, VMEM, ANY, VMEM, VMEM),
+        (SMEM, VMEM, ANY, ANY, VMEM, VMEM),
         (((EXT, 128), F32), ((64, 128), F32), ((64, 128), F32)),
-        (rows, pltpu.VMEM((16, TALL, 256), F32), pltpu.SemaphoreType.DMA),
-    )(slot1, folds, own, spread, blocks, extra, jnp.asarray(column_choice(), BF16))
+        (rows, pltpu.VMEM((16, TALL, 256), F32), big, big, pltpu.SemaphoreType.DMA((3,))),
+        (ANY, VMEM, VMEM),
+    )(slot1, folds, spread, blocks, extra, jnp.asarray(column_choice(), BF16))
     got0, got1 = transposed(send0, 0), transposed(send1, 1)
     left1, left2, share, own = kernel(
         cross_body,

time: 150 us -> 149 us (level)
  blocking collectives: 65 us -> 59.3 us
  starting transfers between devices: 27.6 us -> 31.5 us
  waiting for transfers between devices: 13 us -> 15.2 us
  Pallas kernels: 25.9 us -> 23.9 us
    all_to_all x3, blocking collectives: 65 us -> 59.3 us  [exchanged(): return lax.all_to_all(x, axis, 0, 0, axis_index_groups=groups, tiled=True)]
    all_to_all x1, starting transfers between devices: 4.8 us -> 9.69 us  [on_device(): panels = lax.all_to_all(panel, 'row', 0, 0, tiled=True)]
    all_to_all x1, waiting for transfers between devices: 0.58 us -> 4.11 us  [exchanged(): return lax.all_to_all(x, axis, 0, 0, axis_index_groups=groups, tiled=True)]
    pallas_call x4, Pallas kernels: 16 us -> 14 us  [the longest x1 4.94 us: on_device(): kernel(image_body, (SMEM, VMEM, ANY, ANY, VMEM, VMEM), (((EXT, 128), F32)...]
  transfers between devices with their start and end apart: 7 -> 7, of which waited for: 5 -> 5; matrix products, arithmetic and copies ran while one was open for 1% -> 1% of each run, Pallas kernels for 7% -> 6%
where the time goes in v4:
time: 149 us; the launch traced here: 148 us
  blocking collectives  59.3 us (40%)
  starting transfers between devices  31.5 us (21%)
  Pallas kernels  23.9 us (16%)
  waiting for transfers between devices  15.2 us (10%)
  between operations  14.1 us (9%)
  local copies, waits for them, and re-layouts  3.8 us (3%)
    all_to_all x3, blocking collectives, exchanged(): return lax.all_to_all(x, axis, 0, 0, axis_index_groups=groups, tiled=True)  59.3 us
    ppermute x2, starting transfers between devices, transposed(): return lax.ppermute(x, ('row', 'col'), pairs)  10.9 us
    all_to_all x1, starting transfers between devices, on_device(): panels = lax.all_to_all(panel, 'row', 0, 0, tiled=True)  9.69 us
    ppermute x2, starting transfers between devices, swapped(): return lax.ppermute(x, 'col', [(c, c ^ 1) for c in range(16)])  7.41 us
    pallas_call x1, Pallas kernels, on_device(): kernel(image_body, (SMEM, VMEM, ANY, ANY, VMEM, VMEM), (((EXT, 128), F32)...  4.94 us
    all_to_all x1, waiting for transfers between devices, on_device(): panels = lax.all_to_all(panel, 'row', 0, 0, tiled=True)  4.77 us
    pallas_call x1, Pallas kernels, on_device(): kernel(rank_body, (VMEM, VMEM, VMEM), (((TALL, 256), F32), ((12, 128), jn...  4.37 us
    all_to_all x1, waiting for transfers between devices, exchanged(): return lax.all_to_all(x, axis, 0, 0, axis_index_groups=groups, tiled=True)  4.11 us
  transfers between devices with their start and end apart: 7, of which 5 were waited for; matrix products, arithmetic and copies ran while one was open for 1% of the time, Pallas kernels for 6%

profile of v4, /device:TPU:1, one launch (start us, length us, event | category | flops | bytes accessed | tf_op | source)
XLA Modules:
  0.0 147.8 jit_solution(880926181470395198)
XLA Ops:
  7.2 0.0 all-gather.3.cloned.1.call-start
  7.2 4.4 %shard_map.104 = (f32[144,256]{1,0:T(8,128)}, s32[12,128]{1,0:T(8,128)}, s32[12,128]{1,0:T(8,128)}, bf16[384,256]{1,0:T(8,128)(2,1)}, s32[2,384]{1,0:T(2,128)}) custom-call(s32[12,128]{1,0:T(8,128)} %bitcast.12, s32[12,128]{1,0:T(8,128)} %bitcast.13, f32[9,9,4,128]{3,2,1,0:T(4,128)} %tiles.1), custom_call_target="tpu_custom_call" | custom-call | tf_op jit(solution)/shard_map/pallas_call | solution.py:402
  11.6 0.0 all-gather.3.cloned.1.call-update
  11.6 1.7 %shard_map.105 = (f32[32,16,128]{2,1,0:T(8,128)}, f32[24,128]{1,0:T(8,128)}, f32[8,40,128]{2,1,0:T(8,128)}) custom-call(f32[2,32,48]{2,1,0:T(8,128)} %bitcast.8, f32[1,32,48]{2,1,0:T(8,128)} %bitcast.9, f32[2,2,4,128]{3,2,1,0:T(4,128)} %d1.3), custom_call_target="tpu_custom_call" | custom-call | tf_op jit(solution)/shard_map/pallas_call | solution.py:396
  13.3 19.1 %all_to_all.25.mine = f32[8,40,128]{2,1,0:T(8,128)S(1)} all-to-all(f32[8,40,128]{2,1,0:T(8,128)} %get-tuple-element.24), channel_id=1, replica_groups={{0,2,4,6,8,10,12,14},{1,3,5,7,9,11,13,15},{16,18,20,22,24,26,28,30},{17..., dimensions={0} | all-to-all | bytes 327680 | tf_op jit(solution)/shard_map/all_to_all | solution.py:383
  32.4 0.0 copy-start.3
  32.4 9.7 %all-to-all-start = ((f32[32,16,128]{2,1,0:T(8,128)}), f32[32,16,128]{2,1,0:T(8,128)S(1)}, u32[]{:S(2)}, u32[]{:S(2)}) async-start(f32[32,16,128]{2,1,0:T(8,128)} %get-tuple-element.22), calls=%async_computation | async-start | bytes 524288 | tf_op jit(solution)/shard_map/all_to_all | solution.py:411
  42.1 4.7 %collective-permute-start = (f32[8,40,128]{2,1,0:T(8,128)S(1)}, f32[8,40,128]{2,1,0:T(8,128)S(1)}, u32[]{:S(2)}, u32[]{:S(2)}) collective-permute-start(f32[8,40,128]{2,1,0:T(8,128)S(1)} %all_to_all.25.mine), channel_id=1, source_target_pairs={{0,1},{1,0},{2,3},{3,2},{4,5},{5,4},{6,7},{7,6},{8,9},{9,8},{10,11... | collective-permute-start | bytes 491528 | tf_op jit(solution)/shard_map/ppermute | solution.py:387
  46.8 1.0 collective-permute-done.other
  47.8 0.0 copy-start.5
  47.8 4.8 %all-to-all-done.panels = f32[32,16,128]{2,1,0:T(8,128)S(1)} async-done(((f32[32,16,128]{2,1,0:T(8,128)}), f32[32,16,128]{2,1,0:T(8,128)S(1)}, u32[]{:S(2)}, u32[]{:S(2)}) %all-to-all-start) | async-done | bytes 262176 | tf_op jit(solution)/shard_map/all_to_all | solution.py:411
  52.6 0.0 copy-start.1
  52.6 0.0 copy-done.3
  52.6 0.0 copy-done.5
  52.6 0.7 copy-done.1
  53.3 3.8 %shard_map.106 = (f32[1032,128]{1,0:T(8,128)}, f32[8,40,128]{2,1,0:T(8,128)}, f32[32,128]{1,0:T(8,128)}) custom-call(s32[2,384]{1,0:T(2,128)} %get-tuple-element.21.later, f32[32,16,128]{2,1,0:T(8,128)} %copy-done.1, f32[24,128]{1,0:T(8,128)} %get-tuple-element.23.near, f32[8,40,128]{2,1,0:T(8,128)} %copy-done.3, f32[8,40,128]{2,1,0:T(8,128)} %copy-done.5), custom_call_target="tpu_custom_call" | custom-call | tf_op jit(solution)/shard_map/pallas_call | solution.py:414
  57.1 11.6 %all_to_all.26 = f32[8,40,128]{2,1,0:T(8,128)S(1)} all-to-all(f32[8,40,128]{2,1,0:T(8,128)} %get-tuple-element.25), channel_id=1, replica_groups={{0,64,128,192,256,320,384,448},{16,80,144,208,272,336,400,464},{32,96,1..., dimensions={0} | all-to-all | bytes 327680 | tf_op jit(solution)/shard_map/all_to_all | solution.py:383
  68.6 0.9 broadcast_in_dim.3
  69.5 3.5 %all-to-all-start.3 = ((f32[4,8,40,128]{3,2,1,0:T(8,128)}), f32[4,8,40,128]{3,2,1,0:T(8,128)S(1)}, u32[]{:S(2)}, u32[]{:S(2)}) async-start(f32[4,8,40,128]{3,2,1,0:T(8,128)} %broadcast_in_dim.3), calls=%async_computation.3 | async-start | bytes 1310720 | tf_op jit(solution)/shard_map/all_to_all | solution.py:383
  73.0 3.5 %shard_map.107.second_hbm.spread = f32[2056,128]{1,0:T(8,128)} custom-call(s32[1536]{0:T(1024)} %bitcast.11, f32[32,16,128]{2,1,0:T(8,128)} %copy-done.1), custom_call_target="tpu_custom_call" | custom-call | tf_op jit(solution)/shard_map/pallas_call | solution.py:422
  76.5 4.1 %all-to-all-done.3.folds = f32[4,8,40,128]{3,2,1,0:T(8,128)S(1)} async-done(((f32[4,8,40,128]{3,2,1,0:T(8,128)}), f32[4,8,40,128]{3,2,1,0:T(8,128)S(1)}, u32[]{:S(2)}, u32[]{:S(2)}) %all-to-all-start.3) | async-done | bytes 655392 | tf_op jit(solution)/shard_map/all_to_all | solution.py:383
  80.6 0.0 copy-start
  80.6 0.0 all-gather.3.cloned.1.call-done
  80.6 0.8 copy-done
  81.5 4.9 %shard_map.108 = (f32[2048,128]{1,0:T(8,128)}, f32[64,128]{1,0:T(8,128)}, f32[64,128]{1,0:T(8,128)}) custom-call(s32[1536]{0:T(1024)} %bitcast.10, f32[4,8,40,128]{3,2,1,0:T(8,128)} %copy-done, f32[2056,128]{1,0:T(8,128)} %shard_map.107.second_hbm.spread, f32[16,144,256]{2,1,0:T(8,128)} %bitcast.7, f32[32,128]{1,0:T(8,128)} %get-tuple-element.28.extra, ...), custom_call_target="tpu_custom_call" | custom-call | tf_op jit(solution)/shard_map/pallas_call | solution.py:424
  86.4 8.4 %collective-permute-start.1 = (f32[64,128]{1,0:T(8,128)}, f32[64,128]{1,0:T(8,128)S(1)}, u32[]{:S(2)}, u32[]{:S(2)}) collective-permute-start(f32[64,128]{1,0:T(8,128)} %get-tuple-element.29), channel_id=1, source_target_pairs={{0,0},{1,32},{2,64},{3,96},{4,128},{5,160},{6,192},{7,224},{8,256}... | collective-permute-start | bytes 98312 | tf_op jit(solution)/shard_map/ppermute | solution.py:392
  94.8 2.5 %collective-permute-start.2 = (f32[64,128]{1,0:T(8,128)}, f32[64,128]{1,0:T(8,128)S(1)}, u32[]{:S(2)}, u32[]{:S(2)}) collective-permute-start(f32[64,128]{1,0:T(8,128)} %get-tuple-element.30), channel_id=1, source_target_pairs={{0,16},{1,48},{2,80},{3,112},{4,144},{5,176},{6,208},{7,240},{8,27... | collective-permute-start | bytes 98312 | tf_op jit(solution)/shard_map/ppermute | solution.py:392
  97.4 0.0 collective-permute-done.1.got0
  97.4 0.0 copy-start.6
  97.4 4.1 %collective-permute-done.2.got1 = f32[64,128]{1,0:T(8,128)S(1)} collective-permute-done((f32[64,128]{1,0:T(8,128)}, f32[64,128]{1,0:T(8,128)S(1)}, u32[]{:S(2)}, u32[]{:S(2)}) %collective-permute-start.2) | collective-permute-done | bytes 32800 | tf_op jit(solution)/shard_map/ppermute | solution.py:392
  101.5 0.0 copy-start.7
  101.5 0.0 copy-done.6
  101.5 0.6 copy-done.7
  102.1 2.3 %shard_map.109 = (f32[2,9,4,128]{3,2,1,0:T(4,128)}, f32[1,9,4,128]{3,2,1,0:T(4,128)}, f32[8,72,128]{2,1,0:T(8,128)}, f32[16,128]{1,0:T(8,128)}) custom-call(f32[64,128]{1,0:T(8,128)} %copy-done.6, f32[64,128]{1,0:T(8,128)} %copy-done.7, bf16[512,512]{1,0:T(8,128)(2,1)} %constant.5.clone.order, bf16[384,256]{1,0:T(8,128)(2,1)} %get-tuple-element.31.table), custom_call_target="tpu_custom_call" | custom-call | tf_op jit(solution)/shard_map/pallas_call | solution.py:432
  104.5 28.7 %all_to_all.27.mine = f32[8,72,128]{2,1,0:T(8,128)S(1)} all-to-all(f32[8,72,128]{2,1,0:T(8,128)} %get-tuple-element.32), channel_id=1, replica_groups={{0,2,4,6,8,10,12,14},{1,3,5,7,9,11,13,15},{16,18,20,22,24,26,28,30},{17..., dimensions={0} | all-to-all | bytes 589824 | tf_op jit(solution)/shard_map/all_to_all | solution.py:383
  133.1 0.0 copy-start.2
  133.1 2.7 %collective-permute-start.3 = (f32[8,72,128]{2,1,0:T(8,128)S(1)}, f32[8,72,128]{2,1,0:T(8,128)S(1)}, u32[]{:S(2)}, u32[]{:S(2)}) collective-permute-start(f32[8,72,128]{2,1,0:T(8,128)S(1)} %all_to_all.27.mine), channel_id=1, source_target_pairs={{0,1},{1,0},{2,3},{3,2},{4,5},{5,4},{6,7},{7,6},{8,9},{9,8},{10,11... | collective-permute-start | bytes 884744 | tf_op jit(solution)/shard_map/ppermute | solution.py:387
  135.9 1.2 collective-permute-done.3.other
  137.1 0.0 copy-start.4
  137.1 0.0 copy-done.2
  137.1 0.7 copy-done.4
  137.8 3.2 %shard_map.110 = (f32[2,11,4,128]{3,2,1,0:T(4,128)}, f32[1,12,4,128]{3,2,1,0:T(4,128)}) custom-call(f32[8,72,128]{2,1,0:T(8,128)} %copy-done.2, f32[8,72,128]{2,1,0:T(8,128)} %copy-done.4, f32[2048,128]{1,0:T(8,128)} %get-tuple-element.33.right, f32[2056,128]{1,0:T(8,128)} %shard_map.107.second_hbm.spread, f32[1032,128]{1,0:T(8,128)} %get-tuple-element.34.later, ...), custom_call_target="tpu_custom_call" | custom-call | tf_op jit(solution)/shard_map/pallas_call | solution.py:439
Async XLA Ops:
  7.2 73.5 %all-gather.3.cloned.1.call-start = ((), (), s32[]{:S(2)}) async-start(), calls=%async_computation.5 | async-start | bytes 2506752 | tf_op jit(solution)/shard_map/all_gather | solution.py:408
  32.4 20.2 %copy-start.3 = (f32[8,40,128]{2,1,0:T(8,128)}, f32[8,40,128]{2,1,0:T(8,128)S(1)}, u32[]{:S(2)}) copy-start(f32[8,40,128]{2,1,0:T(8,128)S(1)} %all_to_all.25.mine) | copy-start | bytes 491524
  32.4 20.2 %all-to-all-start = ((f32[32,16,128]{2,1,0:T(8,128)}), f32[32,16,128]{2,1,0:T(8,128)S(1)}, u32[]{:S(2)}, u32[]{:S(2)}) async-start(f32[32,16,128]{2,1,0:T(8,128)} %get-tuple-element.22), calls=%async_computation | async-start | bytes 524288 | tf_op jit(solution)/shard_map/all_to_all | solution.py:411
  42.1 5.7 %collective-permute-start = (f32[8,40,128]{2,1,0:T(8,128)S(1)}, f32[8,40,128]{2,1,0:T(8,128)S(1)}, u32[]{:S(2)}, u32[]{:S(2)}) collective-permute-start(f32[8,40,128]{2,1,0:T(8,128)S(1)} %all_to_all.25.mine), channel_id=1, source_target_pairs={{0,1},{1,0},{2,3},{3,2},{4,5},{5,4},{6,7},{7,6},{8,9},{9,8},{10,11... | collective-permute-start | bytes 491528 | tf_op jit(solution)/shard_map/ppermute | solution.py:387
  47.8 4.8 %copy-start.5 = (f32[8,40,128]{2,1,0:T(8,128)}, f32[8,40,128]{2,1,0:T(8,128)S(1)}, u32[]{:S(2)}) copy-start(f32[8,40,128]{2,1,0:T(8,128)S(1)} %collective-permute-done.other) | copy-start | bytes 491524
  52.6 0.7 copy-start.1
  69.5 11.1 %all-to-all-start.3 = ((f32[4,8,40,128]{3,2,1,0:T(8,128)}), f32[4,8,40,128]{3,2,1,0:T(8,128)S(1)}, u32[]{:S(2)}, u32[]{:S(2)}) async-start(f32[4,8,40,128]{3,2,1,0:T(8,128)} %broadcast_in_dim.3), calls=%async_computation.3 | async-start | bytes 1310720 | tf_op jit(solution)/shard_map/all_to_all | solution.py:383
  80.6 0.9 copy-start
  86.4 10.9 %collective-permute-start.1 = (f32[64,128]{1,0:T(8,128)}, f32[64,128]{1,0:T(8,128)S(1)}, u32[]{:S(2)}, u32[]{:S(2)}) collective-permute-start(f32[64,128]{1,0:T(8,128)} %get-tuple-element.29), channel_id=1, source_target_pairs={{0,0},{1,32},{2,64},{3,96},{4,128},{5,160},{6,192},{7,224},{8,256}... | collective-permute-start | bytes 98312 | tf_op jit(solution)/shard_map/ppermute | solution.py:392
  94.8 6.7 %collective-permute-start.2 = (f32[64,128]{1,0:T(8,128)}, f32[64,128]{1,0:T(8,128)S(1)}, u32[]{:S(2)}, u32[]{:S(2)}) collective-permute-start(f32[64,128]{1,0:T(8,128)} %get-tuple-element.30), channel_id=1, source_target_pairs={{0,16},{1,48},{2,80},{3,112},{4,144},{5,176},{6,208},{7,240},{8,27... | collective-permute-start | bytes 98312 | tf_op jit(solution)/shard_map/ppermute | solution.py:392
  97.4 4.1 %copy-start.6 = (f32[64,128]{1,0:T(8,128)}, f32[64,128]{1,0:T(8,128)S(1)}, u32[]{:S(2)}) copy-start(f32[64,128]{1,0:T(8,128)S(1)} %collective-permute-done.1.got0) | copy-start | bytes 98308
  101.5 0.6 copy-start.7
  133.1 3.9 %copy-start.2 = (f32[8,72,128]{2,1,0:T(8,128)}, f32[8,72,128]{2,1,0:T(8,128)S(1)}, u32[]{:S(2)}) copy-start(f32[8,72,128]{2,1,0:T(8,128)S(1)} %all_to_all.27.mine) | copy-start | bytes 884740
  133.1 3.9 %collective-permute-start.3 = (f32[8,72,128]{2,1,0:T(8,128)S(1)}, f32[8,72,128]{2,1,0:T(8,128)S(1)}, u32[]{:S(2)}, u32[]{:S(2)}) collective-permute-start(f32[8,72,128]{2,1,0:T(8,128)S(1)} %all_to_all.27.mine), channel_id=1, source_target_pairs={{0,1},{1,0},{2,3},{3,2},{4,5},{5,4},{6,7},{7,6},{8,9},{9,8},{10,11... | collective-permute-start | bytes 884744 | tf_op jit(solution)/shard_map/ppermute | solution.py:387
  137.1 0.7 copy-start.4
Sparse Core Ops, SparseCore 0:
  11.7 49.0 all-gather.2

commit v5 on v4

--- a/solution.py
+++ b/solution.py
@@ -78,17 +78,13 @@
     return lax.broadcasted_iota(jnp.int32, shape, len(shape) - 1)
 
 
-def rank_body(s1, s2, tiles, packed, slot1, slot2, table, later, lhs, rhs, stage):
+def rank_body(s1, s2, tiles, packed, slot1, slot2, table, lhs, rhs, stage):
     col = lax.axis_index("col")
     upper = (
         lax.broadcasted_iota(jnp.int32, (128, 128), 0) < lax.broadcasted_iota(jnp.int32, (128, 128), 1)
     ).astype(BF16)
     groups = lax.broadcasted_iota(jnp.int32, (16, 128), 0)
     ranks = []
-    count = jnp.zeros((8, 1), F32)
-    listed = jnp.zeros((8, 384), F32)
-    spot = lax.broadcasted_iota(jnp.int32, (384, 128), 0).astype(F32)
-    kind = lax.broadcasted_iota(jnp.int32, (8, 128), 0)
     for which, (source, target) in enumerate(((s1, slot1), (s2, slot2))):
         carry = jnp.zeros((16, 1), F32)
         rank = []
@@ -103,27 +99,9 @@
             rank.append(t + 1.0)
             place = group * SLOTS + t.astype(jnp.int32)
             if which:
-                high = lax.shift_right_logical(row - 4608, 9)
-                other = group * 64 + high * 32 + jnp.bitwise_and(row, 31)
                 place = jnp.where(inside, place, EXT)
-                mark = jnp.broadcast_to(jnp.where(inside, 0.0, 1.0), (8, 128))
-                order = dot(mark.astype(BF16), upper) + count
-                count = count + jnp.sum(mark, axis=1, keepdims=True)
-                order = jnp.where(mark[0:1] > 0, order[0:1], -1.0)
-                index = lanes_of((1, 128)) + m * 128
-                value = jnp.where(kind == 0, lax.shift_right_logical(index, 6), jnp.bitwise_and(index, 63))
-                value = jnp.where(kind == 2, lax.shift_right_logical(other, 6), value)
-                value = jnp.where(kind == 3, jnp.bitwise_and(other, 63), value)
-                value = jnp.where(kind == 4, 1, value)
-                match = (order == spot).astype(BF16)
-                listed = listed + lax.dot_general(
-                    value.astype(F32).astype(BF16), match, (((1,), (1,)), ((), ())), preferred_element_type=F32
-                )
             target[m : m + 1, :] = place
         ranks.append(rank)
-    source_row = listed[0:1] * 64.0 + listed[1:2]
-    target_row = jnp.where(listed[4:5] > 0.5, listed[2:3] * 64.0 + listed[3:4], 1024.0)
-    later[...] = jnp.concatenate([source_row, target_row], 0).astype(jnp.int32)
     slots = lanes_of((32, 128)).astype(F32)
     table[288:, :] = jnp.zeros((96, 256), BF16)
     for j in range(9):
@@ -147,6 +125,41 @@
             lhs[part * TALL : (part + 1) * TALL, j * 128 : (j + 1) * 128] = value
     out = dot(lhs[...], rhs[...])
     packed[...] = out[:TALL] + (out[TALL : 2 * TALL] + out[2 * TALL :])
+
+
+def list_body(s2, later):
+    upper = (
+        lax.broadcasted_iota(jnp.int32, (128, 128), 0) < lax.broadcasted_iota(jnp.int32, (128, 128), 1)
+    ).astype(BF16)
+    row = s2[...]
+    group = jnp.bitwise_and(lax.shift_right_logical(row, 5), 15)
+    high = lax.shift_right_logical(row - 4608, 9)
+    other = group * 64 + high * 32 + jnp.bitwise_and(row, 31)
+    mark = jnp.where(row < 4608, 0.0, 1.0)
+    order = dot(jnp.concatenate([mark, mark[:4]], 0).astype(BF16), upper)[:12]
+    total = jnp.sum(mark, axis=1, keepdims=True)
+    count = jnp.zeros((1, 1), F32)
+    spot = lax.broadcasted_iota(jnp.int32, (384, 128), 0).astype(F32)
+    kind = lax.broadcasted_iota(jnp.int32, (8, 128), 0)
+    matches, values = [], []
+    for m in range(12):
+        place = jnp.where(mark[m : m + 1] > 0, order[m : m + 1] + count, -1.0)
+        count = count + total[m : m + 1]
+        index = lanes_of((1, 128)) + m * 128
+        value = jnp.where(kind == 0, lax.shift_right_logical(index, 6), jnp.bitwise_and(index, 63))
+        value = jnp.where(kind == 2, lax.shift_right_logical(other[m : m + 1], 6), value)
+        value = jnp.where(kind == 3, jnp.bitwise_and(other[m : m + 1], 63), value)
+        values.append(jnp.where(kind == 4, 1, value).astype(F32).astype(BF16))
+        matches.append((place == spot).astype(BF16))
+    listed = lax.dot_general(
+        jnp.concatenate(values, 1),
+        jnp.concatenate(matches, 1),
+        (((1,), (1,)), ((), ())),
+        preferred_element_type=F32,
+    )
+    source_row = listed[0:1] * 64.0 + listed[1:2]
+    target_row = jnp.where(listed[4:5] > 0.5, listed[2:3] * 64.0 + listed[3:4], 1024.0)
+    later[...] = jnp.concatenate([source_row, target_row], 0).astype(jnp.int32)
 
 
 def lay_body(p1, p2, d1, panel, near, mixed, tall):
@@ -215,11 +228,12 @@
     half = lanes_of((40, 128)) < 64
     total = jnp.zeros((160, 256), F32)
     for z in range(8):
+        left, right = [], []
         for source, k in ((mine, core), (other, 1 - core)):
             x = source[z]
-            left = jnp.concatenate([jnp.where(half, x, 0.0), jnp.where(half, 0.0, x)], 0)
-            right = spread[pl.ds(pl.multiple_of((2 * z + k) * 64, 64), 64), :]
-            total = total + product_terms(left, jnp.concatenate([right, right], 0))
+            left.append(jnp.concatenate([jnp.where(half, x, 0.0), jnp.where(half, 0.0, x)], 0))
+            right += 2 * [spread[pl.ds(pl.multiple_of((2 * z + k) * 64, 64), 64), :]]
+        total = total + product_terms(jnp.concatenate(left, 1), jnp.concatenate(right, 0))
     out = folded(total)
     lane_f = lanes_of((16, 128))
     value = jnp.zeros((16, 128), F32)
@@ -255,14 +269,19 @@
             rows[base + 16 * h : base + 16 * (h + 1), :] = jnp.where(lane < 64, near[16 * h : 16 * (h + 1)], moved)
     right[...] = jnp.zeros(right.shape, F32)
     scatter_rows(slot1, rows, right)
+    third.wait()
+    right[...] = right[...] + pltpu.roll(second[...], 32, 1)
     leaving.start()
-    third.wait()
     arrival.wait()
-    total = jnp.zeros((2 * TALL, 256), F32)
-    for c in range(16):
-        part = slice(c * SLOTS, (c + 1) * SLOTS)
-        total = total + product_terms(held[c], jnp.concatenate([right[part, :], second[part, :]], 0))
-    image = jnp.concatenate([folded(total), extra[...]], 0)
+    total = jnp.zeros((4 * TALL, 256), F32)
+    for c in range(0, 16, 2):
+        left = [jnp.concatenate([held[c, :, n : n + 128], held[c + 1, :, n : n + 128]], 1) for n in (0, 128)]
+        total = total + product_terms(jnp.concatenate(left, 0), right[c * SLOTS : (c + 2) * SLOTS, :])
+    out_terms = folded(total)
+    image = out_terms[:TALL]
+    late = lanes_of((TALL, 128))
+    image = jnp.where((late >= 64) & (late < 96), image + pltpu.roll(out_terms[TALL:], 96, 1), image)
+    image = jnp.concatenate([image, extra[...]], 0)
     sent = jnp.zeros((96, TALL + 32), F32)
     for part in thirds(image):
         sent = sent + lax.dot_general(choice[...], part, (((1,), (1,)), ((), ())), preferred_element_type=F32)
@@ -284,7 +303,7 @@
     leaving.wait()
 
 
-def cross_body(got0, got1, order, table, first, second, share, own):
+def cross_body(got0, got1, order, table, whole, share, own):
     parity = lax.axis_index("row") % 2
     a, b = got0[...], got1[...]
     even = jnp.where(parity == 0, a, b)
@@ -303,6 +322,12 @@
     e = jnp.concatenate([close[:, :128], close[32:48, 128:], e], 0)
     for n in range(8):
         share[n] = e
+    whole[...] = y[:, :384]
+
+
+def pack_body(whole, first, second):
+    y = whole[...]
+    lane = lanes_of((8, 128))
     lane2 = lanes_of((4, 128))
     for i in range(9):
         chunk = (i // 4) * 128
@@ -320,7 +345,7 @@
         second[0, i] = -two
 
 
-def diagonal_body(mine, other, right, spread, later, own, d1, d2, left1, left2, first, second):
+def diagonal_body(mine, other, right, later, own, d1, d2, left1, left2, first, second):
     first[:, 0:9] = left1[...]
     second[:, 0:9] = left2[...]
     core = lax.axis_index("col") % 2
@@ -328,23 +353,21 @@
     total = jnp.zeros((128, 256), F32)
     also = jnp.zeros((32, 256), F32)
     for z in range(8):
+        left, wide, extra, late = [], [], [], []
         for source, k in ((mine, core), (other, 1 - core)):
             c = 2 * z + k
             x = source[z]
-            part = pl.ds(pl.multiple_of(c * SLOTS, SLOTS), SLOTS)
-            zero = jnp.zeros((48, 128), F32)
-            left = jnp.concatenate(
-                [jnp.concatenate([x[:48], zero], 1), jnp.concatenate([zero[:16], x[48:64]], 1)], 0
-            )
-            total = total + product_terms(left, jnp.concatenate([right[part, :], spread[part, :]], 0))
+            left.append(x[:64])
+            wide.append(right[pl.ds(pl.multiple_of(c * SLOTS, SLOTS), SLOTS), :])
             e = x[64:72]
-            left = jnp.concatenate([jnp.where(lane_e < 64, e, 0.0), jnp.where(lane_e >= 64, e, 0.0)], 0)
-            v = later[pl.ds(pl.multiple_of(c * 64, 64), 64), :]
-            also = also + product_terms(left, jnp.concatenate([v, v], 0))
+            extra.append(jnp.concatenate([jnp.where(lane_e < 64, e, 0.0), jnp.where(lane_e >= 64, e, 0.0)], 0))
+            late += 2 * [later[pl.ds(pl.multiple_of(c * 64, 64), 64), :]]
+        total = total + product_terms(jnp.concatenate(left, 1), jnp.concatenate(wide, 0))
+        also = also + product_terms(jnp.concatenate(extra, 1), jnp.concatenate(late, 0))
     out = folded(total)
     g1 = out[:32]
     bottom = own[...] - out[32:48]
-    g2 = out[32:48] + out[48:64] + folded(also)
+    g2 = out[32:48] + pltpu.roll(out[48:64], 96, 1) + folded(also)
     lane = lanes_of((8, 128))
     lane2 = lanes_of((4, 128))
     for k in range(2):
@@ -399,16 +422,22 @@
         (((32, 16, 128), F32), ((24, 128), F32), ((8, 40, 128), F32)),
         (pltpu.VMEM((128, 128), F32),),
     )(panel_first.transpose(1, 2, 0), panel_second.transpose(1, 2, 0), inverse_first)
-    packed, slot1, slot2, table, later = kernel(
+    packed, slot1, slot2, table = kernel(
         rank_body,
         (VMEM, VMEM, VMEM),
-        (((TALL, 256), F32), ((12, 128), jnp.int32), ((12, 128), jnp.int32), ((384, 256), BF16), ((2, 384), jnp.int32)),
+        (
+            ((TALL, 256), F32),
+            ((12, 128), jnp.int32),
+            ((12, 128), jnp.int32),
+            ((384, 256), BF16),
+        ),
         (pltpu.VMEM((3 * TALL, 1152), BF16), pltpu.VMEM((1152, 256), BF16), pltpu.VMEM((TALL, 128), F32)),
     )(structure_first.reshape(12, 128), structure_second.reshape(12, 128), ancestor)
     blocks = lax.all_gather(packed, "col")
     mine = exchanged(mixed, "col", Z_GROUPS)
     other = swapped(mine)
     panels = lax.all_to_all(panel, "row", 0, 0, tiled=True)
+    (later,) = kernel(list_body, (VMEM,), (((2, 384), jnp.int32),))(structure_second.reshape(12, 128))
     slot1, slot2 = slot1.reshape(1536), slot2.reshape(1536)
     rows = pltpu.VMEM((1536, 128), F32)
     second, fold, extra = kernel(
@@ -429,18 +458,19 @@
         (ANY, VMEM, VMEM),
     )(slot1, folds, spread, blocks, extra, jnp.asarray(column_choice(), BF16))
     got0, got1 = transposed(send0, 0), transposed(send1, 1)
-    left1, left2, share, own = kernel(
+    whole, share, own = kernel(
         cross_body,
         (VMEM, VMEM, VMEM, VMEM),
-        (((2, 9, 4, 128), F32), ((1, 9, 4, 128), F32), ((8, 72, 128), F32), ((16, 128), F32)),
+        (((48, 384), F32), ((8, 72, 128), F32), ((16, 128), F32)),
     )(got0, got1, jnp.asarray(lane_order(), BF16), table)
     mine = exchanged(share, "col", Z_GROUPS)
+    left1, left2 = kernel(pack_body, (VMEM,), (((2, 9, 4, 128), F32), ((1, 9, 4, 128), F32)))(whole)
     other = swapped(mine)
     return kernel(
         diagonal_body,
-        (VMEM,) * 10,
+        (VMEM,) * 9,
         (((2, 11, 4, 128), F32), ((1, 12, 4, 128), F32)),
-    )(mine, other, right, spread, second, own, inverse_first, inverse_second, left1, left2)
+    )(mine, other, right, second, own, inverse_first, inverse_second, left1, left2)
 
 
 def solution(mesh):

time: 149 us -> 147 us (0.987)
  waiting for transfers between devices: 15.2 us -> 12.1 us
  Pallas kernels: 23.9 us -> 25.5 us
    pallas_call x2 -> x4, Pallas kernels: 5.55 us -> 8.68 us  [the longest x1 2.79 us: on_device(): kernel(diagonal_body, (VMEM,) * 9, (((2, 11, 4, 128), F32), ((1, 12, 4, 1...]
    ppermute x2, waiting for transfers between devices: 2.19 us -> 0.01 us  [swapped(): return lax.ppermute(x, 'col', [(c, c ^ 1) for c in range(16)])]
  transfers between devices with their start and end apart: 7 -> 7, of which waited for: 5 -> 3; matrix products, arithmetic and copies ran while one was open for 1% -> 1% of each run, Pallas kernels for 6% -> 9%
where the time goes in v5:
time: 147 us; the launch traced here: 146 us
  blocking collectives  59.3 us (40%)
  starting transfers between devices  31.5 us (21%)
  Pallas kernels  25.5 us (17%)
  between operations  14.1 us (10%)
  waiting for transfers between devices  12.1 us (8%)
  local copies, waits for them, and re-layouts  3.77 us (3%)
    all_to_all x3, blocking collectives, exchanged(): return lax.all_to_all(x, axis, 0, 0, axis_index_groups=groups, tiled=True)  59.3 us
    ppermute x2, starting transfers between devices, transposed(): return lax.ppermute(x, ('row', 'col'), pairs)  10.7 us
    all_to_all x1, starting transfers between devices, on_device(): panels = lax.all_to_all(panel, 'row', 0, 0, tiled=True)  9.67 us
    ppermute x2, starting transfers between devices, swapped(): return lax.ppermute(x, 'col', [(c, c ^ 1) for c in range(16)])  7.41 us
    pallas_call x1, Pallas kernels, on_device(): kernel(image_body, (SMEM, VMEM, ANY, ANY, VMEM, VMEM), (((EXT, 128), F32)...  5.01 us
    all_to_all x1, waiting for transfers between devices, exchanged(): return lax.all_to_all(x, axis, 0, 0, axis_index_groups=groups, tiled=True)  4.13 us
    ppermute x2, waiting for transfers between devices, transposed(): return lax.ppermute(x, ('row', 'col'), pairs)  4.1 us
    all_to_all x1, waiting for transfers between devices, on_device(): panels = lax.all_to_all(panel, 'row', 0, 0, tiled=True)  3.85 us
  transfers between devices with their start and end apart: 7, of which 3 were waited for; matrix products, arithmetic and copies ran while one was open for 1% of the time, Pallas kernels for 9%

profile of v5, /device:TPU:1, one launch (start us, length us, event | category | flops | bytes accessed | tf_op | source)
XLA Modules:
  0.0 146.3 jit_solution(11223311758887345328)
XLA Ops:
  7.2 0.0 all-gather.3.cloned.1.call-start
  7.2 2.9 %shard_map.104 = (f32[144,256]{1,0:T(8,128)}, s32[12,128]{1,0:T(8,128)}, s32[12,128]{1,0:T(8,128)}, bf16[384,256]{1,0:T(8,128)(2,1)}) custom-call(s32[12,128]{1,0:T(8,128)} %bitcast.14, s32[12,128]{1,0:T(8,128)} %bitcast.9, f32[9,9,4,128]{3,2,1,0:T(4,128)} %tiles.1), custom_call_target="tpu_custom_call" | custom-call | tf_op jit(solution)/shard_map/pallas_call | solution.py:425
  10.2 0.0 all-gather.3.cloned.1.call-update
  10.2 1.7 %shard_map.106 = (f32[32,16,128]{2,1,0:T(8,128)}, f32[24,128]{1,0:T(8,128)}, f32[8,40,128]{2,1,0:T(8,128)}) custom-call(f32[2,32,48]{2,1,0:T(8,128)} %bitcast.8, f32[1,32,48]{2,1,0:T(8,128)} %bitcast.11, f32[2,2,4,128]{3,2,1,0:T(4,128)} %d1.3), custom_call_target="tpu_custom_call" | custom-call | tf_op jit(solution)/shard_map/pallas_call | solution.py:419
  11.9 19.1 %all_to_all.25.mine = f32[8,40,128]{2,1,0:T(8,128)S(1)} all-to-all(f32[8,40,128]{2,1,0:T(8,128)} %get-tuple-element.23), channel_id=1, replica_groups={{0,2,4,6,8,10,12,14},{1,3,5,7,9,11,13,15},{16,18,20,22,24,26,28,30},{17..., dimensions={0} | all-to-all | bytes 327680 | tf_op jit(solution)/shard_map/all_to_all | solution.py:406
  31.0 0.0 copy-start.3
  31.0 9.7 %all-to-all-start = ((f32[32,16,128]{2,1,0:T(8,128)}), f32[32,16,128]{2,1,0:T(8,128)S(1)}, u32[]{:S(2)}, u32[]{:S(2)}) async-start(f32[32,16,128]{2,1,0:T(8,128)} %get-tuple-element.21), calls=%async_computation | async-start | bytes 524288 | tf_op jit(solution)/shard_map/all_to_all | solution.py:439
  40.7 4.7 %collective-permute-start = (f32[8,40,128]{2,1,0:T(8,128)S(1)}, f32[8,40,128]{2,1,0:T(8,128)S(1)}, u32[]{:S(2)}, u32[]{:S(2)}) collective-permute-start(f32[8,40,128]{2,1,0:T(8,128)S(1)} %all_to_all.25.mine), channel_id=1, source_target_pairs={{0,1},{1,0},{2,3},{3,2},{4,5},{5,4},{6,7},{7,6},{8,9},{9,8},{10,11... | collective-permute-start | bytes 491528 | tf_op jit(solution)/shard_map/ppermute | solution.py:410
  45.4 1.9 %shard_map.105.later = s32[2,384]{1,0:T(2,128)} custom-call(s32[12,128]{1,0:T(8,128)} %bitcast.10), custom_call_target="tpu_custom_call" | custom-call | tf_op jit(solution)/shard_map/pallas_call | solution.py:440
  47.3 0.0 collective-permute-done.other
  47.3 0.0 copy-start.5
  47.3 3.8 %all-to-all-done.panels = f32[32,16,128]{2,1,0:T(8,128)S(1)} async-done(((f32[32,16,128]{2,1,0:T(8,128)}), f32[32,16,128]{2,1,0:T(8,128)S(1)}, u32[]{:S(2)}, u32[]{:S(2)}) %all-to-all-start) | async-done | bytes 262176 | tf_op jit(solution)/shard_map/all_to_all | solution.py:439
  51.1 0.0 copy-start.1
  51.2 0.0 copy-done.3
  51.2 0.0 copy-done.5
  51.2 0.7 copy-done.1
  51.8 3.6 %shard_map.107 = (f32[1032,128]{1,0:T(8,128)}, f32[8,40,128]{2,1,0:T(8,128)}, f32[32,128]{1,0:T(8,128)}) custom-call(s32[2,384]{1,0:T(2,128)} %shard_map.105.later, f32[32,16,128]{2,1,0:T(8,128)} %copy-done.1, f32[24,128]{1,0:T(8,128)} %get-tuple-element.22.near, f32[8,40,128]{2,1,0:T(8,128)} %copy-done.3, f32[8,40,128]{2,1,0:T(8,128)} %copy-done.5), custom_call_target="tpu_custom_call" | custom-call | tf_op jit(solution)/shard_map/pallas_call | solution.py:443
  55.5 11.6 %all_to_all.26 = f32[8,40,128]{2,1,0:T(8,128)S(1)} all-to-all(f32[8,40,128]{2,1,0:T(8,128)} %get-tuple-element.24), channel_id=1, replica_groups={{0,64,128,192,256,320,384,448},{16,80,144,208,272,336,400,464},{32,96,1..., dimensions={0} | all-to-all | bytes 327680 | tf_op jit(solution)/shard_map/all_to_all | solution.py:406
  67.0 0.9 broadcast_in_dim.3
  67.9 3.7 %all-to-all-start.3 = ((f32[4,8,40,128]{3,2,1,0:T(8,128)}), f32[4,8,40,128]{3,2,1,0:T(8,128)S(1)}, u32[]{:S(2)}, u32[]{:S(2)}) async-start(f32[4,8,40,128]{3,2,1,0:T(8,128)} %broadcast_in_dim.3), calls=%async_computation.3 | async-start | bytes 1310720 | tf_op jit(solution)/shard_map/all_to_all | solution.py:406
  71.6 3.5 %shard_map.108.second_hbm = f32[2056,128]{1,0:T(8,128)} custom-call(s32[1536]{0:T(1024)} %bitcast.13, f32[32,16,128]{2,1,0:T(8,128)} %copy-done.1), custom_call_target="tpu_custom_call" | custom-call | tf_op jit(solution)/shard_map/pallas_call | solution.py:451
  75.1 4.1 %all-to-all-done.3.folds = f32[4,8,40,128]{3,2,1,0:T(8,128)S(1)} async-done(((f32[4,8,40,128]{3,2,1,0:T(8,128)}), f32[4,8,40,128]{3,2,1,0:T(8,128)S(1)}, u32[]{:S(2)}, u32[]{:S(2)}) %all-to-all-start.3) | async-done | bytes 655392 | tf_op jit(solution)/shard_map/all_to_all | solution.py:406
  79.3 0.0 copy-start
  79.3 0.0 all-gather.3.cloned.1.call-done
  79.3 0.9 copy-done
  80.1 5.0 %shard_map.109 = (f32[2048,128]{1,0:T(8,128)}, f32[64,128]{1,0:T(8,128)}, f32[64,128]{1,0:T(8,128)}) custom-call(s32[1536]{0:T(1024)} %bitcast.12, f32[4,8,40,128]{3,2,1,0:T(8,128)} %copy-done, f32[2056,128]{1,0:T(8,128)} %shard_map.108.second_hbm, f32[16,144,256]{2,1,0:T(8,128)} %bitcast.7, f32[32,128]{1,0:T(8,128)} %get-tuple-element.27.extra, ...), custom_call_target="tpu_custom_call" | custom-call | tf_op jit(solution)/shard_map/pallas_call | solution.py:453
  85.1 8.2 %collective-permute-start.1 = (f32[64,128]{1,0:T(8,128)}, f32[64,128]{1,0:T(8,128)S(1)}, u32[]{:S(2)}, u32[]{:S(2)}) collective-permute-start(f32[64,128]{1,0:T(8,128)} %get-tuple-element.28), channel_id=1, source_target_pairs={{0,0},{1,32},{2,64},{3,96},{4,128},{5,160},{6,192},{7,224},{8,256}... | collective-permute-start | bytes 98312 | tf_op jit(solution)/shard_map/ppermute | solution.py:415
  93.3 2.5 %collective-permute-start.2 = (f32[64,128]{1,0:T(8,128)}, f32[64,128]{1,0:T(8,128)S(1)}, u32[]{:S(2)}, u32[]{:S(2)}) collective-permute-start(f32[64,128]{1,0:T(8,128)} %get-tuple-element.29), channel_id=1, source_target_pairs={{0,16},{1,48},{2,80},{3,112},{4,144},{5,176},{6,208},{7,240},{8,27... | collective-permute-start | bytes 98312 | tf_op jit(solution)/shard_map/ppermute | solution.py:415
  95.9 0.0 collective-permute-done.1.got0
  95.9 0.0 copy-start.6
  95.9 4.1 %collective-permute-done.2.got1 = f32[64,128]{1,0:T(8,128)S(1)} collective-permute-done((f32[64,128]{1,0:T(8,128)}, f32[64,128]{1,0:T(8,128)S(1)}, u32[]{:S(2)}, u32[]{:S(2)}) %collective-permute-start.2) | collective-permute-done | bytes 32800 | tf_op jit(solution)/shard_map/ppermute | solution.py:415
  100.0 0.0 copy-start.7
  100.0 0.0 copy-done.6
  100.0 0.6 copy-done.7
  100.6 2.3 %shard_map.110 = (f32[48,384]{1,0:T(8,128)}, f32[8,72,128]{2,1,0:T(8,128)}, f32[16,128]{1,0:T(8,128)}) custom-call(f32[64,128]{1,0:T(8,128)} %copy-done.6, f32[64,128]{1,0:T(8,128)} %copy-done.7, bf16[512,512]{1,0:T(8,128)(2,1)} %constant.5.clone.order, bf16[384,256]{1,0:T(8,128)(2,1)} %get-tuple-element.30.table), custom_call_target="tpu_custom_call" | custom-call | tf_op jit(solution)/shard_map/pallas_call | solution.py:461
  102.9 28.7 %all_to_all.27.mine = f32[8,72,128]{2,1,0:T(8,128)S(1)} all-to-all(f32[8,72,128]{2,1,0:T(8,128)} %get-tuple-element.31), channel_id=1, replica_groups={{0,2,4,6,8,10,12,14},{1,3,5,7,9,11,13,15},{16,18,20,22,24,26,28,30},{17..., dimensions={0} | all-to-all | bytes 589824 | tf_op jit(solution)/shard_map/all_to_all | solution.py:406
  131.6 0.0 copy-start.2
  131.6 2.7 %collective-permute-start.3 = (f32[8,72,128]{2,1,0:T(8,128)S(1)}, f32[8,72,128]{2,1,0:T(8,128)S(1)}, u32[]{:S(2)}, u32[]{:S(2)}) collective-permute-start(f32[8,72,128]{2,1,0:T(8,128)S(1)} %all_to_all.27.mine), channel_id=1, source_target_pairs={{0,1},{1,0},{2,3},{3,2},{4,5},{5,4},{6,7},{7,6},{8,9},{9,8},{10,11... | collective-permute-start | bytes 884744 | tf_op jit(solution)/shard_map/ppermute | solution.py:410
  134.3 1.6 %shard_map.111 = (f32[2,9,4,128]{3,2,1,0:T(4,128)}, f32[1,9,4,128]{3,2,1,0:T(4,128)}) custom-call(f32[48,384]{1,0:T(8,128)} %get-tuple-element.35.whole), custom_call_target="tpu_custom_call" | custom-call | tf_op jit(solution)/shard_map/pallas_call | solution.py:467
  135.9 0.0 collective-permute-done.3.other
  135.9 0.0 copy-start.4
  135.9 0.0 copy-done.2
  136.0 0.7 copy-done.4
  136.7 2.8 %shard_map.112 = (f32[2,11,4,128]{3,2,1,0:T(4,128)}, f32[1,12,4,128]{3,2,1,0:T(4,128)}) custom-call(f32[8,72,128]{2,1,0:T(8,128)} %copy-done.2, f32[8,72,128]{2,1,0:T(8,128)} %copy-done.4, f32[2048,128]{1,0:T(8,128)} %get-tuple-element.32.right, f32[1032,128]{1,0:T(8,128)} %get-tuple-element.33.later, f32[16,128]{1,0:T(8,128)} %get-tuple-element.34.own, ...), custom_call_target="tpu_custom_call" | custom-call | tf_op jit(solution)/shard_map/pallas_call | solution.py:469
Async XLA Ops:
  7.2 72.1 %all-gather.3.cloned.1.call-start = ((), (), s32[]{:S(2)}) async-start(), calls=%async_computation.5 | async-start | bytes 2506752 | tf_op jit(solution)/shard_map/all_gather | solution.py:436
  31.0 20.2 %copy-start.3 = (f32[8,40,128]{2,1,0:T(8,128)}, f32[8,40,128]{2,1,0:T(8,128)S(1)}, u32[]{:S(2)}) copy-start(f32[8,40,128]{2,1,0:T(8,128)S(1)} %all_to_all.25.mine) | copy-start | bytes 491524
  31.0 20.2 %all-to-all-start = ((f32[32,16,128]{2,1,0:T(8,128)}), f32[32,16,128]{2,1,0:T(8,128)S(1)}, u32[]{:S(2)}, u32[]{:S(2)}) async-start(f32[32,16,128]{2,1,0:T(8,128)} %get-tuple-element.21), calls=%async_computation | async-start | bytes 524288 | tf_op jit(solution)/shard_map/all_to_all | solution.py:439
  40.7 6.6 %collective-permute-start = (f32[8,40,128]{2,1,0:T(8,128)S(1)}, f32[8,40,128]{2,1,0:T(8,128)S(1)}, u32[]{:S(2)}, u32[]{:S(2)}) collective-permute-start(f32[8,40,128]{2,1,0:T(8,128)S(1)} %all_to_all.25.mine), channel_id=1, source_target_pairs={{0,1},{1,0},{2,3},{3,2},{4,5},{5,4},{6,7},{7,6},{8,9},{9,8},{10,11... | collective-permute-start | bytes 491528 | tf_op jit(solution)/shard_map/ppermute | solution.py:410
  47.3 3.9 %copy-start.5 = (f32[8,40,128]{2,1,0:T(8,128)}, f32[8,40,128]{2,1,0:T(8,128)S(1)}, u32[]{:S(2)}) copy-start(f32[8,40,128]{2,1,0:T(8,128)S(1)} %collective-permute-done.other) | copy-start | bytes 491524
  51.1 0.7 copy-start.1
  67.9 11.3 %all-to-all-start.3 = ((f32[4,8,40,128]{3,2,1,0:T(8,128)}), f32[4,8,40,128]{3,2,1,0:T(8,128)S(1)}, u32[]{:S(2)}, u32[]{:S(2)}) async-start(f32[4,8,40,128]{3,2,1,0:T(8,128)} %broadcast_in_dim.3), calls=%async_computation.3 | async-start | bytes 1310720 | tf_op jit(solution)/shard_map/all_to_all | solution.py:406
  79.3 0.9 copy-start
  85.1 10.7 %collective-permute-start.1 = (f32[64,128]{1,0:T(8,128)}, f32[64,128]{1,0:T(8,128)S(1)}, u32[]{:S(2)}, u32[]{:S(2)}) collective-permute-start(f32[64,128]{1,0:T(8,128)} %get-tuple-element.28), channel_id=1, source_target_pairs={{0,0},{1,32},{2,64},{3,96},{4,128},{5,160},{6,192},{7,224},{8,256}... | collective-permute-start | bytes 98312 | tf_op jit(solution)/shard_map/ppermute | solution.py:415
  93.3 6.7 %collective-permute-start.2 = (f32[64,128]{1,0:T(8,128)}, f32[64,128]{1,0:T(8,128)S(1)}, u32[]{:S(2)}, u32[]{:S(2)}) collective-permute-start(f32[64,128]{1,0:T(8,128)} %get-tuple-element.29), channel_id=1, source_target_pairs={{0,16},{1,48},{2,80},{3,112},{4,144},{5,176},{6,208},{7,240},{8,27... | collective-permute-start | bytes 98312 | tf_op jit(solution)/shard_map/ppermute | solution.py:415
  95.9 4.1 %copy-start.6 = (f32[64,128]{1,0:T(8,128)}, f32[64,128]{1,0:T(8,128)S(1)}, u32[]{:S(2)}) copy-start(f32[64,128]{1,0:T(8,128)S(1)} %collective-permute-done.1.got0) | copy-start | bytes 98308
  100.0 0.6 copy-start.7
  131.6 4.4 %copy-start.2 = (f32[8,72,128]{2,1,0:T(8,128)}, f32[8,72,128]{2,1,0:T(8,128)S(1)}, u32[]{:S(2)}) copy-start(f32[8,72,128]{2,1,0:T(8,128)S(1)} %all_to_all.27.mine) | copy-start | bytes 884740
  131.6 4.4 %collective-permute-start.3 = (f32[8,72,128]{2,1,0:T(8,128)S(1)}, f32[8,72,128]{2,1,0:T(8,128)S(1)}, u32[]{:S(2)}, u32[]{:S(2)}) collective-permute-start(f32[8,72,128]{2,1,0:T(8,128)S(1)} %all_to_all.27.mine), channel_id=1, source_target_pairs={{0,1},{1,0},{2,3},{3,2},{4,5},{5,4},{6,7},{7,6},{8,9},{9,8},{10,11... | collective-permute-start | bytes 884744 | tf_op jit(solution)/shard_map/ppermute | solution.py:410
  135.9 0.7 copy-start.4
Sparse Core Ops, SparseCore 0:
  10.3 49.0 all-gather.2

commit v6 on v5

--- a/solution.py
+++ b/solution.py
@@ -252,8 +252,7 @@
     scatter_rows(slot2, rows, spread)
 
 
-def image_body(slot1, folds, second_hbm, blocks, extra, choice, out, send0, send1, rows, held, second, right, done):
-    send = (send0, send1)
+def image_body(slot1, folds, second_hbm, blocks, extra, choice, out, send, rows, held, second, right, done):
     third = pltpu.make_async_copy(second_hbm.at[pl.ds(0, EXT)], second, done.at[0])
     arrival = pltpu.make_async_copy(blocks, held, done.at[1])
     leaving = pltpu.make_async_copy(right, out, done.at[2])
@@ -292,26 +291,20 @@
         tail = jnp.where(lane < 16, rest[0:16], pltpu.roll(rest[16:32], 16, 1))
         tail = jnp.where(lane < 32, tail, pltpu.roll(rest[32:48], 32, 1))
         pieces.append(jnp.concatenate([sent[h * 48 : (h + 1) * 48, :128], tail], 0))
-    parity = lax.axis_index("row") % 2
+    place = mirror_place()
+    send[...] = jnp.zeros(send.shape, F32)
     for h in range(2):
-
-        @pl.when(parity == h)
-        def _(h=h):
-            send[0][...] = pieces[h]
-            send[1][...] = pieces[1 - h]
-
+        send[pl.ds(place + h, 1)] = pieces[h][None]
     leaving.wait()
 
 
-def cross_body(got0, got1, order, table, whole, share, own):
-    parity = lax.axis_index("row") % 2
-    a, b = got0[...], got1[...]
-    even = jnp.where(parity == 0, a, b)
-    odd = jnp.where(parity == 0, b, a)
+def cross_body(got, order, table, whole, share, own):
+    place = mirror_place()
     parts = []
-    for got in (even, odd):
-        tail = got[48:64]
-        parts.append(got[:48])
+    for g in range(2):
+        piece = got[pl.ds(place + g, 1)][0]
+        tail = piece[48:64]
+        parts.append(piece[:48])
         parts.append(jnp.concatenate([tail, pltpu.roll(tail, 112, 1), pltpu.roll(tail, 96, 1)], 0))
     y = chosen(jnp.concatenate(parts, 1), order[...])
     close = chosen(y[:, :384], table[...])
@@ -410,9 +403,17 @@
     return lax.ppermute(x, "col", [(c, c ^ 1) for c in range(16)])
 
 
-def transposed(x, turn):
-    pairs = [(r * 16 + c, (2 * c + (r + turn) % 2) * 16 + r // 2) for r in range(32) for c in range(16)]
-    return lax.ppermute(x, ("row", "col"), pairs)
+def mirror_groups():
+    def pair(u, v):
+        return [(2 * u) * 16 + v, (2 * u + 1) * 16 + v]
+
+    groups = [pair(u, v) + pair(v, u) for u in range(16) for v in range(u + 1, 16)]
+    return groups + [pair(u, u) + pair(u + 1, u + 1) for u in range(0, 16, 2)]
+
+
+def mirror_place():
+    u, v = lax.axis_index("row") // 2, lax.axis_index("col")
+    return jnp.where(u == v, (u % 2) * 2, jnp.where(u < v, 2, 0))
 
 
 def on_device(ancestor, inverse_first, panel_first, structure_first, inverse_second, panel_second, structure_second):
@@ -450,19 +451,19 @@
     folds = exchanged(jnp.broadcast_to(folds, (4, *folds.shape)), "row", X_GROUPS)
     (spread,) = kernel(first_body, (SMEM, VMEM), (((EXT + 8, 128), F32),), (rows,))(slot2, panels)
     big = pltpu.VMEM((EXT, 128), F32)
-    right, send0, send1 = kernel(
+    right, send = kernel(
         image_body,
         (SMEM, VMEM, ANY, ANY, VMEM, VMEM),
-        (((EXT, 128), F32), ((64, 128), F32), ((64, 128), F32)),
+        (((EXT, 128), F32), ((4, 64, 128), F32)),
         (rows, pltpu.VMEM((16, TALL, 256), F32), big, big, pltpu.SemaphoreType.DMA((3,))),
-        (ANY, VMEM, VMEM),
+        (ANY, VMEM),
     )(slot1, folds, spread, blocks, extra, jnp.asarray(column_choice(), BF16))
-    got0, got1 = transposed(send0, 0), transposed(send1, 1)
+    got = exchanged(send, ("row", "col"), mirror_groups())
     whole, share, own = kernel(
         cross_body,
-        (VMEM, VMEM, VMEM, VMEM),
+        (VMEM, VMEM, VMEM),
         (((48, 384), F32), ((8, 72, 128), F32), ((16, 128), F32)),
-    )(got0, got1, jnp.asarray(lane_order(), BF16), table)
+    )(got, jnp.asarray(lane_order(), BF16), table)
     mine = exchanged(share, "col", Z_GROUPS)
     left1, left2 = kernel(pack_body, (VMEM,), (((2, 9, 4, 128), F32), ((1, 9, 4, 128), F32)))(whole)
     other = swapped(mine)

time: 147 us -> 144 us (0.980)
  blocking collectives: 59.3 us -> 72.3 us
  starting transfers between devices: 31.5 us -> 20 us
  waiting for transfers between devices: 12.1 us -> 8.02 us
    all_to_all x3 -> x4, blocking collectives: 59.3 us -> 72.3 us  [exchanged(): return lax.all_to_all(x, axis, 0, 0, axis_index_groups=groups, tiled=True)]
    ppermute x2 -> x0, starting transfers between devices: 10.7 us -> none  [transposed(): return lax.ppermute(x, ('row', 'col'), pairs)]
    ppermute x2 -> x0, waiting for transfers between devices: 4.1 us -> none  [transposed(): return lax.ppermute(x, ('row', 'col'), pairs)]
  transfers between devices with their start and end apart: 7 -> 5, of which waited for: 3 -> 2; matrix products, arithmetic and copies ran while one was open for 1% -> 1% of each run, Pallas kernels for 9% -> 9%
where the time goes in v6:
time: 144 us; the launch traced here: 143 us
  blocking collectives  72.3 us (50%)
  Pallas kernels  25.5 us (18%)
  starting transfers between devices  20 us (14%)
  between operations  14.1 us (10%)
  waiting for transfers between devices  8.02 us (6%)
  local copies, waits for them, and re-layouts  3.18 us (2%)
    all_to_all x4, blocking collectives, exchanged(): return lax.all_to_all(x, axis, 0, 0, axis_index_groups=groups, tiled=True)  72.3 us
    all_to_all x1, starting transfers between devices, on_device(): panels = lax.all_to_all(panel, 'row', 0, 0, tiled=True)  9.67 us
    ppermute x2, starting transfers between devices, swapped(): return lax.ppermute(x, 'col', [(c, c ^ 1) for c in range(16)])  6.6 us
    pallas_call x1, Pallas kernels, on_device(): kernel(image_body, (SMEM, VMEM, ANY, ANY, VMEM, VMEM), (((EXT, 128), F32)...  5.05 us
    all_to_all x1, waiting for transfers between devices, exchanged(): return lax.all_to_all(x, axis, 0, 0, axis_index_groups=groups, tiled=True)  4.15 us
    all_to_all x1, waiting for transfers between devices, on_device(): panels = lax.all_to_all(panel, 'row', 0, 0, tiled=True)  3.85 us
    all_to_all x1, starting transfers between devices, exchanged(): return lax.all_to_all(x, axis, 0, 0, axis_index_groups=groups, tiled=True)  3.69 us
    pallas_call x1, Pallas kernels, on_device(): kernel(second_body, (SMEM, VMEM, VMEM, VMEM, VMEM), (((1032, 128), F32),...  3.63 us
  transfers between devices with their start and end apart: 5, of which 2 were waited for; matrix products, arithmetic and copies ran while one was open for 1% of the time, Pallas kernels for 9%

profile of v6, /device:TPU:1, one launch (start us, length us, event | category | flops | bytes accessed | tf_op | source)
XLA Modules:
  0.0 143.2 jit_solution(4235191724013202689)
XLA Ops:
  7.2 0.0 all-gather.3.cloned.1.call-start
  7.2 3.0 %shard_map.104 = (f32[144,256]{1,0:T(8,128)}, s32[12,128]{1,0:T(8,128)}, s32[12,128]{1,0:T(8,128)}, bf16[384,256]{1,0:T(8,128)(2,1)}) custom-call(s32[12,128]{1,0:T(8,128)} %bitcast.14, s32[12,128]{1,0:T(8,128)} %bitcast.9, f32[9,9,4,128]{3,2,1,0:T(4,128)} %tiles.1), custom_call_target="tpu_custom_call" | custom-call | tf_op jit(solution)/shard_map/pallas_call | solution.py:426
  10.2 0.0 all-gather.3.cloned.1.call-update
  10.2 1.7 %shard_map.106 = (f32[32,16,128]{2,1,0:T(8,128)}, f32[24,128]{1,0:T(8,128)}, f32[8,40,128]{2,1,0:T(8,128)}) custom-call(f32[2,32,48]{2,1,0:T(8,128)} %bitcast.8, f32[1,32,48]{2,1,0:T(8,128)} %bitcast.11, f32[2,2,4,128]{3,2,1,0:T(4,128)} %d1.3), custom_call_target="tpu_custom_call" | custom-call | tf_op jit(solution)/shard_map/pallas_call | solution.py:420
  11.9 19.1 %all_to_all.30.mine = f32[8,40,128]{2,1,0:T(8,128)S(1)} all-to-all(f32[8,40,128]{2,1,0:T(8,128)} %get-tuple-element.22), channel_id=1, replica_groups={{0,2,4,6,8,10,12,14},{1,3,5,7,9,11,13,15},{16,18,20,22,24,26,28,30},{17..., dimensions={0} | all-to-all | bytes 327680 | tf_op jit(solution)/shard_map/all_to_all | solution.py:399
  31.0 0.0 copy-start.3
  31.0 9.7 %all-to-all-start = ((f32[32,16,128]{2,1,0:T(8,128)}), f32[32,16,128]{2,1,0:T(8,128)S(1)}, u32[]{:S(2)}, u32[]{:S(2)}) async-start(f32[32,16,128]{2,1,0:T(8,128)} %get-tuple-element.20), calls=%async_computation | async-start | bytes 524288 | tf_op jit(solution)/shard_map/all_to_all | solution.py:440
  40.7 4.7 %collective-permute-start = (f32[8,40,128]{2,1,0:T(8,128)S(1)}, f32[8,40,128]{2,1,0:T(8,128)S(1)}, u32[]{:S(2)}, u32[]{:S(2)}) collective-permute-start(f32[8,40,128]{2,1,0:T(8,128)S(1)} %all_to_all.30.mine), channel_id=1, source_target_pairs={{0,1},{1,0},{2,3},{3,2},{4,5},{5,4},{6,7},{7,6},{8,9},{9,8},{10,11... | collective-permute-start | bytes 491528 | tf_op jit(solution)/shard_map/ppermute | solution.py:403
  45.4 1.9 %shard_map.105.later = s32[2,384]{1,0:T(2,128)} custom-call(s32[12,128]{1,0:T(8,128)} %bitcast.10), custom_call_target="tpu_custom_call" | custom-call | tf_op jit(solution)/shard_map/pallas_call | solution.py:441
  47.3 0.0 collective-permute-done.other
  47.3 0.0 copy-start.5
  47.3 3.9 %all-to-all-done.panels = f32[32,16,128]{2,1,0:T(8,128)S(1)} async-done(((f32[32,16,128]{2,1,0:T(8,128)}), f32[32,16,128]{2,1,0:T(8,128)S(1)}, u32[]{:S(2)}, u32[]{:S(2)}) %all-to-all-start) | async-done | bytes 262176 | tf_op jit(solution)/shard_map/all_to_all | solution.py:440
  51.2 0.0 copy-start.1
  51.2 0.0 copy-done.3
  51.2 0.0 copy-done.5
  51.2 0.7 copy-done.1
  51.9 3.6 %shard_map.107 = (f32[1032,128]{1,0:T(8,128)}, f32[8,40,128]{2,1,0:T(8,128)}, f32[32,128]{1,0:T(8,128)}) custom-call(s32[2,384]{1,0:T(2,128)} %shard_map.105.later, f32[32,16,128]{2,1,0:T(8,128)} %copy-done.1, f32[24,128]{1,0:T(8,128)} %get-tuple-element.21.near, f32[8,40,128]{2,1,0:T(8,128)} %copy-done.3, f32[8,40,128]{2,1,0:T(8,128)} %copy-done.5), custom_call_target="tpu_custom_call" | custom-call | tf_op jit(solution)/shard_map/pallas_call | solution.py:444
  55.5 11.6 %all_to_all.31 = f32[8,40,128]{2,1,0:T(8,128)S(1)} all-to-all(f32[8,40,128]{2,1,0:T(8,128)} %get-tuple-element.23), channel_id=1, replica_groups={{0,64,128,192,256,320,384,448},{16,80,144,208,272,336,400,464},{32,96,1..., dimensions={0} | all-to-all | bytes 327680 | tf_op jit(solution)/shard_map/all_to_all | solution.py:399
  67.1 0.9 broadcast_in_dim.3
  68.0 3.7 %all-to-all-start.3 = ((f32[4,8,40,128]{3,2,1,0:T(8,128)}), f32[4,8,40,128]{3,2,1,0:T(8,128)S(1)}, u32[]{:S(2)}, u32[]{:S(2)}) async-start(f32[4,8,40,128]{3,2,1,0:T(8,128)} %broadcast_in_dim.3), calls=%async_computation.3 | async-start | bytes 1310720 | tf_op jit(solution)/shard_map/all_to_all | solution.py:399
  71.7 3.5 %shard_map.108.second_hbm = f32[2056,128]{1,0:T(8,128)} custom-call(s32[1536]{0:T(1024)} %bitcast.13, f32[32,16,128]{2,1,0:T(8,128)} %copy-done.1), custom_call_target="tpu_custom_call" | custom-call | tf_op jit(solution)/shard_map/pallas_call | solution.py:452
  75.1 4.1 %all-to-all-done.3.folds = f32[4,8,40,128]{3,2,1,0:T(8,128)S(1)} async-done(((f32[4,8,40,128]{3,2,1,0:T(8,128)}), f32[4,8,40,128]{3,2,1,0:T(8,128)S(1)}, u32[]{:S(2)}, u32[]{:S(2)}) %all-to-all-start.3) | async-done | bytes 655392 | tf_op jit(solution)/shard_map/all_to_all | solution.py:399
  79.3 0.0 copy-start
  79.3 0.0 all-gather.3.cloned.1.call-done
  79.3 0.9 copy-done
  80.2 5.1 %shard_map.109 = (f32[2048,128]{1,0:T(8,128)}, f32[4,64,128]{2,1,0:T(8,128)}) custom-call(s32[1536]{0:T(1024)} %bitcast.12, f32[4,8,40,128]{3,2,1,0:T(8,128)} %copy-done, f32[2056,128]{1,0:T(8,128)} %shard_map.108.second_hbm, f32[16,144,256]{2,1,0:T(8,128)} %bitcast.7, f32[32,128]{1,0:T(8,128)} %get-tuple-element.26.extra, bf16[96,128]{1,0:T(8,128)(2,1)} %constant.4.clone.choice), custom_call_target="tpu_custom_call" | custom-call | tf_op jit(solution)/shard_map/pallas_call | solution.py:454
  85.2 13.7 %all_to_all.32.got = f32[4,64,128]{2,1,0:T(8,128)} all-to-all(f32[4,64,128]{2,1,0:T(8,128)} %get-tuple-element.27), channel_id=1, replica_groups={{1,17,32,48},{2,18,64,80},{3,19,96,112},{4,20,128,144},{5,21,160,176},{..., dimensions={0} | all-to-all | bytes 262144 | tf_op jit(solution)/shard_map/all_to_all | solution.py:399
  98.9 2.3 %shard_map.110 = (f32[48,384]{1,0:T(8,128)}, f32[8,72,128]{2,1,0:T(8,128)}, f32[16,128]{1,0:T(8,128)}) custom-call(f32[4,64,128]{2,1,0:T(8,128)} %all_to_all.32.got, bf16[512,512]{1,0:T(8,128)(2,1)} %constant.5.clone.order, bf16[384,256]{1,0:T(8,128)(2,1)} %get-tuple-element.28.table), custom_call_target="tpu_custom_call" | custom-call | tf_op jit(solution)/shard_map/pallas_call | solution.py:462
  101.2 28.1 %all_to_all.33.mine = f32[8,72,128]{2,1,0:T(8,128)S(1)} all-to-all(f32[8,72,128]{2,1,0:T(8,128)} %get-tuple-element.29), channel_id=1, replica_groups={{0,2,4,6,8,10,12,14},{1,3,5,7,9,11,13,15},{16,18,20,22,24,26,28,30},{17..., dimensions={0} | all-to-all | bytes 589824 | tf_op jit(solution)/shard_map/all_to_all | solution.py:399
  129.2 0.0 copy-start.2
  129.3 1.9 %collective-permute-start.1 = (f32[8,72,128]{2,1,0:T(8,128)S(1)}, f32[8,72,128]{2,1,0:T(8,128)S(1)}, u32[]{:S(2)}, u32[]{:S(2)}) collective-permute-start(f32[8,72,128]{2,1,0:T(8,128)S(1)} %all_to_all.33.mine), channel_id=1, source_target_pairs={{0,1},{1,0},{2,3},{3,2},{4,5},{5,4},{6,7},{7,6},{8,9},{9,8},{10,11... | collective-permute-start | bytes 884744 | tf_op jit(solution)/shard_map/ppermute | solution.py:403
  131.2 1.6 %shard_map.111 = (f32[2,9,4,128]{3,2,1,0:T(4,128)}, f32[1,9,4,128]{3,2,1,0:T(4,128)}) custom-call(f32[48,384]{1,0:T(8,128)} %get-tuple-element.33.whole), custom_call_target="tpu_custom_call" | custom-call | tf_op jit(solution)/shard_map/pallas_call | solution.py:468
  132.8 0.0 collective-permute-done.1.other
  132.8 0.0 copy-start.4
  132.8 0.0 copy-done.2
  132.8 0.7 copy-done.4
  133.5 2.8 %shard_map.112 = (f32[2,11,4,128]{3,2,1,0:T(4,128)}, f32[1,12,4,128]{3,2,1,0:T(4,128)}) custom-call(f32[8,72,128]{2,1,0:T(8,128)} %copy-done.2, f32[8,72,128]{2,1,0:T(8,128)} %copy-done.4, f32[2048,128]{1,0:T(8,128)} %get-tuple-element.30.right, f32[1032,128]{1,0:T(8,128)} %get-tuple-element.31.later, f32[16,128]{1,0:T(8,128)} %get-tuple-element.32.own, ...), custom_call_target="tpu_custom_call" | custom-call | tf_op jit(solution)/shard_map/pallas_call | solution.py:470
Async XLA Ops:
  7.2 72.1 %all-gather.3.cloned.1.call-start = ((), (), s32[]{:S(2)}) async-start(), calls=%async_computation.6 | async-start | bytes 2506752 | tf_op jit(solution)/shard_map/all_gather | solution.py:437
  31.0 20.2 %copy-start.3 = (f32[8,40,128]{2,1,0:T(8,128)}, f32[8,40,128]{2,1,0:T(8,128)S(1)}, u32[]{:S(2)}) copy-start(f32[8,40,128]{2,1,0:T(8,128)S(1)} %all_to_all.30.mine) | copy-start | bytes 491524
  31.0 20.2 %all-to-all-start = ((f32[32,16,128]{2,1,0:T(8,128)}), f32[32,16,128]{2,1,0:T(8,128)S(1)}, u32[]{:S(2)}, u32[]{:S(2)}) async-start(f32[32,16,128]{2,1,0:T(8,128)} %get-tuple-element.20), calls=%async_computation | async-start | bytes 524288 | tf_op jit(solution)/shard_map/all_to_all | solution.py:440
  40.7 6.6 %collective-permute-start = (f32[8,40,128]{2,1,0:T(8,128)S(1)}, f32[8,40,128]{2,1,0:T(8,128)S(1)}, u32[]{:S(2)}, u32[]{:S(2)}) collective-permute-start(f32[8,40,128]{2,1,0:T(8,128)S(1)} %all_to_all.30.mine), channel_id=1, source_target_pairs={{0,1},{1,0},{2,3},{3,2},{4,5},{5,4},{6,7},{7,6},{8,9},{9,8},{10,11... | collective-permute-start | bytes 491528 | tf_op jit(solution)/shard_map/ppermute | solution.py:403
  47.3 3.9 %copy-start.5 = (f32[8,40,128]{2,1,0:T(8,128)}, f32[8,40,128]{2,1,0:T(8,128)S(1)}, u32[]{:S(2)}) copy-start(f32[8,40,128]{2,1,0:T(8,128)S(1)} %collective-permute-done.other) | copy-start | bytes 491524
  51.2 0.7 copy-start.1
  68.0 11.3 %all-to-all-start.3 = ((f32[4,8,40,128]{3,2,1,0:T(8,128)}), f32[4,8,40,128]{3,2,1,0:T(8,128)S(1)}, u32[]{:S(2)}, u32[]{:S(2)}) async-start(f32[4,8,40,128]{3,2,1,0:T(8,128)} %broadcast_in_dim.3), calls=%async_computation.3 | async-start | bytes 1310720 | tf_op jit(solution)/shard_map/all_to_all | solution.py:399
  79.3 0.9 copy-start
  129.2 3.5 %copy-start.2 = (f32[8,72,128]{2,1,0:T(8,128)}, f32[8,72,128]{2,1,0:T(8,128)S(1)}, u32[]{:S(2)}) copy-start(f32[8,72,128]{2,1,0:T(8,128)S(1)} %all_to_all.33.mine) | copy-start | bytes 884740
  129.3 3.5 %collective-permute-start.1 = (f32[8,72,128]{2,1,0:T(8,128)S(1)}, f32[8,72,128]{2,1,0:T(8,128)S(1)}, u32[]{:S(2)}, u32[]{:S(2)}) collective-permute-start(f32[8,72,128]{2,1,0:T(8,128)S(1)} %all_to_all.33.mine), channel_id=1, source_target_pairs={{0,1},{1,0},{2,3},{3,2},{4,5},{5,4},{6,7},{7,6},{8,9},{9,8},{10,11... | collective-permute-start | bytes 884744 | tf_op jit(solution)/shard_map/ppermute | solution.py:403
  132.8 0.7 copy-start.4
Sparse Core Ops, SparseCore 0:
  10.3 49.0 all-gather.2

commit v7 on v6

--- a/solution.py
+++ b/solution.py
@@ -204,17 +204,17 @@
     return ((step % 8) * 4 + step // 8) * 48
 
 
-def unfold(folds, rows):
+def unfold(folds, rows, low):
     keep = lanes_of((16, 128))
-    keep = (keep >= 64) & (keep < 96)
+    keep = (keep >= low) & (keep < low + 32)
     for r in range(32):
         for h in range(3):
-            moved = pltpu.roll(folds[r], (64 - 32 * h) % 128, 1)
+            moved = pltpu.roll(folds[r], (low - 32 * h) % 128, 1)
             rows[r * 48 + 16 * h : r * 48 + 16 * (h + 1), :] = jnp.where(keep, moved, 0.0)
 
 
 def second_body(later, panels, near, mine, other, spread, fold, extra, rows):
-    unfold(panels, rows)
+    unfold(panels, rows, 64)
     spread[...] = jnp.zeros(spread.shape, F32)
 
     def place(step, _):
@@ -247,7 +247,7 @@
 
 
 def first_body(slot2, panels, spread, rows):
-    unfold(panels, rows)
+    unfold(panels, rows, 96)
     spread[...] = jnp.zeros(spread.shape, F32)
     scatter_rows(slot2, rows, spread)
 
@@ -269,7 +269,7 @@
     right[...] = jnp.zeros(right.shape, F32)
     scatter_rows(slot1, rows, right)
     third.wait()
-    right[...] = right[...] + pltpu.roll(second[...], 32, 1)
+    right[...] = right[...] + second[...]
     leaving.start()
     arrival.wait()
     total = jnp.zeros((4 * TALL, 256), F32)

time: 144 us -> 144 us (level)
  no operation moved by 1% of the time
where the time goes in v7:
time: 144 us; the launch traced here: 143 us
  blocking collectives  72.4 us (50%)
  Pallas kernels  25.6 us (18%)
  starting transfers between devices  20 us (14%)
  between operations  14.1 us (10%)
  waiting for transfers between devices  7.97 us (6%)
  local copies, waits for them, and re-layouts  3.18 us (2%)
    all_to_all x4, blocking collectives, exchanged(): return lax.all_to_all(x, axis, 0, 0, axis_index_groups=groups, tiled=True)  72.4 us
    all_to_all x1, starting transfers between devices, on_device(): panels = lax.all_to_all(panel, 'row', 0, 0, tiled=True)  9.67 us
    ppermute x2, starting transfers between devices, swapped(): return lax.ppermute(x, 'col', [(c, c ^ 1) for c in range(16)])  6.6 us
    pallas_call x1, Pallas kernels, on_device(): kernel(image_body, (SMEM, VMEM, ANY, ANY, VMEM, VMEM), (((EXT, 128), F32)...  5.03 us
    all_to_all x1, waiting for transfers between devices, exchanged(): return lax.all_to_all(x, axis, 0, 0, axis_index_groups=groups, tiled=True)  4.1 us
    all_to_all x1, waiting for transfers between devices, on_device(): panels = lax.all_to_all(panel, 'row', 0, 0, tiled=True)  3.85 us
    all_to_all x1, starting transfers between devices, exchanged(): return lax.all_to_all(x, axis, 0, 0, axis_index_groups=groups, tiled=True)  3.69 us
    pallas_call x1, Pallas kernels, on_device(): kernel(second_body, (SMEM, VMEM, VMEM, VMEM, VMEM), (((1032, 128), F32),...  3.63 us
  transfers between devices with their start and end apart: 5, of which 2 were waited for; matrix products, arithmetic and copies ran while one was open for 1% of the time, Pallas kernels for 9%

profile of v7, /device:TPU:1, one launch (start us, length us, event | category | flops | bytes accessed | tf_op | source)
XLA Modules:
  0.0 143.1 jit_solution(12921356191728280284)
XLA Ops:
  7.2 0.0 all-gather.3.cloned.1.call-start
  7.2 3.0 %shard_map.104 = (f32[144,256]{1,0:T(8,128)}, s32[12,128]{1,0:T(8,128)}, s32[12,128]{1,0:T(8,128)}, bf16[384,256]{1,0:T(8,128)(2,1)}) custom-call(s32[12,128]{1,0:T(8,128)} %bitcast.14, s32[12,128]{1,0:T(8,128)} %bitcast.9, f32[9,9,4,128]{3,2,1,0:T(4,128)} %tiles.1), custom_call_target="tpu_custom_call" | custom-call | tf_op jit(solution)/shard_map/pallas_call | solution.py:426
  10.2 0.0 all-gather.3.cloned.1.call-update
  10.2 1.7 %shard_map.106 = (f32[32,16,128]{2,1,0:T(8,128)}, f32[24,128]{1,0:T(8,128)}, f32[8,40,128]{2,1,0:T(8,128)}) custom-call(f32[2,32,48]{2,1,0:T(8,128)} %bitcast.8, f32[1,32,48]{2,1,0:T(8,128)} %bitcast.11, f32[2,2,4,128]{3,2,1,0:T(4,128)} %d1.3), custom_call_target="tpu_custom_call" | custom-call | tf_op jit(solution)/shard_map/pallas_call | solution.py:420
  11.9 19.1 %all_to_all.30.mine = f32[8,40,128]{2,1,0:T(8,128)S(1)} all-to-all(f32[8,40,128]{2,1,0:T(8,128)} %get-tuple-element.22), channel_id=1, replica_groups={{0,2,4,6,8,10,12,14},{1,3,5,7,9,11,13,15},{16,18,20,22,24,26,28,30},{17..., dimensions={0} | all-to-all | bytes 327680 | tf_op jit(solution)/shard_map/all_to_all | solution.py:399
  31.0 0.0 copy-start.3
  31.0 9.7 %all-to-all-start = ((f32[32,16,128]{2,1,0:T(8,128)}), f32[32,16,128]{2,1,0:T(8,128)S(1)}, u32[]{:S(2)}, u32[]{:S(2)}) async-start(f32[32,16,128]{2,1,0:T(8,128)} %get-tuple-element.20), calls=%async_computation | async-start | bytes 524288 | tf_op jit(solution)/shard_map/all_to_all | solution.py:440
  40.7 4.7 %collective-permute-start = (f32[8,40,128]{2,1,0:T(8,128)S(1)}, f32[8,40,128]{2,1,0:T(8,128)S(1)}, u32[]{:S(2)}, u32[]{:S(2)}) collective-permute-start(f32[8,40,128]{2,1,0:T(8,128)S(1)} %all_to_all.30.mine), channel_id=1, source_target_pairs={{0,1},{1,0},{2,3},{3,2},{4,5},{5,4},{6,7},{7,6},{8,9},{9,8},{10,11... | collective-permute-start | bytes 491528 | tf_op jit(solution)/shard_map/ppermute | solution.py:403
  45.4 1.9 %shard_map.105.later = s32[2,384]{1,0:T(2,128)} custom-call(s32[12,128]{1,0:T(8,128)} %bitcast.10), custom_call_target="tpu_custom_call" | custom-call | tf_op jit(solution)/shard_map/pallas_call | solution.py:441
  47.3 0.0 collective-permute-done.other
  47.3 0.0 copy-start.5
  47.3 3.9 %all-to-all-done.panels = f32[32,16,128]{2,1,0:T(8,128)S(1)} async-done(((f32[32,16,128]{2,1,0:T(8,128)}), f32[32,16,128]{2,1,0:T(8,128)S(1)}, u32[]{:S(2)}, u32[]{:S(2)}) %all-to-all-start) | async-done | bytes 262176 | tf_op jit(solution)/shard_map/all_to_all | solution.py:440
  51.2 0.0 copy-start.1
  51.2 0.0 copy-done.3
  51.2 0.0 copy-done.5
  51.2 0.7 copy-done.1
  51.9 3.6 %shard_map.107 = (f32[1032,128]{1,0:T(8,128)}, f32[8,40,128]{2,1,0:T(8,128)}, f32[32,128]{1,0:T(8,128)}) custom-call(s32[2,384]{1,0:T(2,128)} %shard_map.105.later, f32[32,16,128]{2,1,0:T(8,128)} %copy-done.1, f32[24,128]{1,0:T(8,128)} %get-tuple-element.21.near, f32[8,40,128]{2,1,0:T(8,128)} %copy-done.3, f32[8,40,128]{2,1,0:T(8,128)} %copy-done.5), custom_call_target="tpu_custom_call" | custom-call | tf_op jit(solution)/shard_map/pallas_call | solution.py:444
  55.5 11.6 %all_to_all.31 = f32[8,40,128]{2,1,0:T(8,128)S(1)} all-to-all(f32[8,40,128]{2,1,0:T(8,128)} %get-tuple-element.23), channel_id=1, replica_groups={{0,64,128,192,256,320,384,448},{16,80,144,208,272,336,400,464},{32,96,1..., dimensions={0} | all-to-all | bytes 327680 | tf_op jit(solution)/shard_map/all_to_all | solution.py:399
  67.1 0.9 broadcast_in_dim.3
  68.0 3.7 %all-to-all-start.3 = ((f32[4,8,40,128]{3,2,1,0:T(8,128)}), f32[4,8,40,128]{3,2,1,0:T(8,128)S(1)}, u32[]{:S(2)}, u32[]{:S(2)}) async-start(f32[4,8,40,128]{3,2,1,0:T(8,128)} %broadcast_in_dim.3), calls=%async_computation.3 | async-start | bytes 1310720 | tf_op jit(solution)/shard_map/all_to_all | solution.py:399
  71.7 3.5 %shard_map.108.second_hbm = f32[2056,128]{1,0:T(8,128)} custom-call(s32[1536]{0:T(1024)} %bitcast.13, f32[32,16,128]{2,1,0:T(8,128)} %copy-done.1), custom_call_target="tpu_custom_call" | custom-call | tf_op jit(solution)/shard_map/pallas_call | solution.py:452
  75.2 4.1 %all-to-all-done.3.folds = f32[4,8,40,128]{3,2,1,0:T(8,128)S(1)} async-done(((f32[4,8,40,128]{3,2,1,0:T(8,128)}), f32[4,8,40,128]{3,2,1,0:T(8,128)S(1)}, u32[]{:S(2)}, u32[]{:S(2)}) %all-to-all-start.3) | async-done | bytes 655392 | tf_op jit(solution)/shard_map/all_to_all | solution.py:399
  79.3 0.0 copy-start
  79.3 0.0 all-gather.3.cloned.1.call-done
  79.3 0.9 copy-done
  80.2 5.0 %shard_map.109 = (f32[2048,128]{1,0:T(8,128)}, f32[4,64,128]{2,1,0:T(8,128)}) custom-call(s32[1536]{0:T(1024)} %bitcast.12, f32[4,8,40,128]{3,2,1,0:T(8,128)} %copy-done, f32[2056,128]{1,0:T(8,128)} %shard_map.108.second_hbm, f32[16,144,256]{2,1,0:T(8,128)} %bitcast.7, f32[32,128]{1,0:T(8,128)} %get-tuple-element.26.extra, bf16[96,128]{1,0:T(8,128)(2,1)} %constant.4.clone.choice), custom_call_target="tpu_custom_call" | custom-call | tf_op jit(solution)/shard_map/pallas_call | solution.py:454
  85.2 13.7 %all_to_all.32.got = f32[4,64,128]{2,1,0:T(8,128)} all-to-all(f32[4,64,128]{2,1,0:T(8,128)} %get-tuple-element.27), channel_id=1, replica_groups={{1,17,32,48},{2,18,64,80},{3,19,96,112},{4,20,128,144},{5,21,160,176},{..., dimensions={0} | all-to-all | bytes 262144 | tf_op jit(solution)/shard_map/all_to_all | solution.py:399
  98.9 2.3 %shard_map.110 = (f32[48,384]{1,0:T(8,128)}, f32[8,72,128]{2,1,0:T(8,128)}, f32[16,128]{1,0:T(8,128)}) custom-call(f32[4,64,128]{2,1,0:T(8,128)} %all_to_all.32.got, bf16[512,512]{1,0:T(8,128)(2,1)} %constant.5.clone.order, bf16[384,256]{1,0:T(8,128)(2,1)} %get-tuple-element.28.table), custom_call_target="tpu_custom_call" | custom-call | tf_op jit(solution)/shard_map/pallas_call | solution.py:462
  101.2 28.1 %all_to_all.33.mine = f32[8,72,128]{2,1,0:T(8,128)S(1)} all-to-all(f32[8,72,128]{2,1,0:T(8,128)} %get-tuple-element.29), channel_id=1, replica_groups={{0,2,4,6,8,10,12,14},{1,3,5,7,9,11,13,15},{16,18,20,22,24,26,28,30},{17..., dimensions={0} | all-to-all | bytes 589824 | tf_op jit(solution)/shard_map/all_to_all | solution.py:399
  129.2 0.0 copy-start.2
  129.2 1.9 %collective-permute-start.1 = (f32[8,72,128]{2,1,0:T(8,128)S(1)}, f32[8,72,128]{2,1,0:T(8,128)S(1)}, u32[]{:S(2)}, u32[]{:S(2)}) collective-permute-start(f32[8,72,128]{2,1,0:T(8,128)S(1)} %all_to_all.33.mine), channel_id=1, source_target_pairs={{0,1},{1,0},{2,3},{3,2},{4,5},{5,4},{6,7},{7,6},{8,9},{9,8},{10,11... | collective-permute-start | bytes 884744 | tf_op jit(solution)/shard_map/ppermute | solution.py:403
  131.2 1.6 %shard_map.111 = (f32[2,9,4,128]{3,2,1,0:T(4,128)}, f32[1,9,4,128]{3,2,1,0:T(4,128)}) custom-call(f32[48,384]{1,0:T(8,128)} %get-tuple-element.33.whole), custom_call_target="tpu_custom_call" | custom-call | tf_op jit(solution)/shard_map/pallas_call | solution.py:468
  132.8 0.0 collective-permute-done.1.other
  132.8 0.0 copy-start.4
  132.8 0.0 copy-done.2
  132.8 0.7 copy-done.4
  133.5 2.8 %shard_map.112 = (f32[2,11,4,128]{3,2,1,0:T(4,128)}, f32[1,12,4,128]{3,2,1,0:T(4,128)}) custom-call(f32[8,72,128]{2,1,0:T(8,128)} %copy-done.2, f32[8,72,128]{2,1,0:T(8,128)} %copy-done.4, f32[2048,128]{1,0:T(8,128)} %get-tuple-element.30.right, f32[1032,128]{1,0:T(8,128)} %get-tuple-element.31.later, f32[16,128]{1,0:T(8,128)} %get-tuple-element.32.own, ...), custom_call_target="tpu_custom_call" | custom-call | tf_op jit(solution)/shard_map/pallas_call | solution.py:470
Async XLA Ops:
  7.2 72.1 %all-gather.3.cloned.1.call-start = ((), (), s32[]{:S(2)}) async-start(), calls=%async_computation.6 | async-start | bytes 2506752 | tf_op jit(solution)/shard_map/all_gather | solution.py:437
  31.0 20.2 %copy-start.3 = (f32[8,40,128]{2,1,0:T(8,128)}, f32[8,40,128]{2,1,0:T(8,128)S(1)}, u32[]{:S(2)}) copy-start(f32[8,40,128]{2,1,0:T(8,128)S(1)} %all_to_all.30.mine) | copy-start | bytes 491524
  31.0 20.2 %all-to-all-start = ((f32[32,16,128]{2,1,0:T(8,128)}), f32[32,16,128]{2,1,0:T(8,128)S(1)}, u32[]{:S(2)}, u32[]{:S(2)}) async-start(f32[32,16,128]{2,1,0:T(8,128)} %get-tuple-element.20), calls=%async_computation | async-start | bytes 524288 | tf_op jit(solution)/shard_map/all_to_all | solution.py:440
  40.7 6.6 %collective-permute-start = (f32[8,40,128]{2,1,0:T(8,128)S(1)}, f32[8,40,128]{2,1,0:T(8,128)S(1)}, u32[]{:S(2)}, u32[]{:S(2)}) collective-permute-start(f32[8,40,128]{2,1,0:T(8,128)S(1)} %all_to_all.30.mine), channel_id=1, source_target_pairs={{0,1},{1,0},{2,3},{3,2},{4,5},{5,4},{6,7},{7,6},{8,9},{9,8},{10,11... | collective-permute-start | bytes 491528 | tf_op jit(solution)/shard_map/ppermute | solution.py:403
  47.3 3.9 %copy-start.5 = (f32[8,40,128]{2,1,0:T(8,128)}, f32[8,40,128]{2,1,0:T(8,128)S(1)}, u32[]{:S(2)}) copy-start(f32[8,40,128]{2,1,0:T(8,128)S(1)} %collective-permute-done.other) | copy-start | bytes 491524
  51.2 0.7 copy-start.1
  68.0 11.3 %all-to-all-start.3 = ((f32[4,8,40,128]{3,2,1,0:T(8,128)}), f32[4,8,40,128]{3,2,1,0:T(8,128)S(1)}, u32[]{:S(2)}, u32[]{:S(2)}) async-start(f32[4,8,40,128]{3,2,1,0:T(8,128)} %broadcast_in_dim.3), calls=%async_computation.3 | async-start | bytes 1310720 | tf_op jit(solution)/shard_map/all_to_all | solution.py:399
  79.3 0.9 copy-start
  129.2 3.5 %copy-start.2 = (f32[8,72,128]{2,1,0:T(8,128)}, f32[8,72,128]{2,1,0:T(8,128)S(1)}, u32[]{:S(2)}) copy-start(f32[8,72,128]{2,1,0:T(8,128)S(1)} %all_to_all.33.mine) | copy-start | bytes 884740
  129.2 3.5 %collective-permute-start.1 = (f32[8,72,128]{2,1,0:T(8,128)S(1)}, f32[8,72,128]{2,1,0:T(8,128)S(1)}, u32[]{:S(2)}, u32[]{:S(2)}) collective-permute-start(f32[8,72,128]{2,1,0:T(8,128)S(1)} %all_to_all.33.mine), channel_id=1, source_target_pairs={{0,1},{1,0},{2,3},{3,2},{4,5},{5,4},{6,7},{7,6},{8,9},{9,8},{10,11... | collective-permute-start | bytes 884744 | tf_op jit(solution)/shard_map/ppermute | solution.py:403
  132.8 0.7 copy-start.4
Sparse Core Ops, SparseCore 0:
  10.3 49.0 all-gather.2

commit v8 on v7

--- a/solution.py
+++ b/solution.py
@@ -192,12 +192,12 @@
 
 def scatter_rows(slots, source, target):
     def place(step, _):
-        base = pl.multiple_of(step * 48, 16)
-        for u in range(48):
+        base = pl.multiple_of(step * 96, 32)
+        for u in range(96):
             target[pl.ds(slots[base + u], 1), :] = source[pl.ds(base + u, 1), :]
         return 0
 
-    lax.fori_loop(0, 32, place, 0)
+    lax.fori_loop(0, 16, place, 0)
 
 
 def in_order(step):

time: 144 us -> 144 us (level)
  no operation moved by 1% of the time
where the time goes in v8:
time: 144 us; the launch traced here: 143 us
  blocking collectives  72.4 us (50%)
  Pallas kernels  25.5 us (18%)
  starting transfers between devices  20 us (14%)
  between operations  14.1 us (10%)
  waiting for transfers between devices  8.03 us (6%)
  local copies, waits for them, and re-layouts  3.18 us (2%)
    all_to_all x4, blocking collectives, exchanged(): return lax.all_to_all(x, axis, 0, 0, axis_index_groups=groups, tiled=True)  72.4 us
    all_to_all x1, starting transfers between devices, on_device(): panels = lax.all_to_all(panel, 'row', 0, 0, tiled=True)  9.67 us
    ppermute x2, starting transfers between devices, swapped(): return lax.ppermute(x, 'col', [(c, c ^ 1) for c in range(16)])  6.6 us
    pallas_call x1, Pallas kernels, on_device(): kernel(image_body, (SMEM, VMEM, ANY, ANY, VMEM, VMEM), (((EXT, 128), F32)...  5.03 us
    all_to_all x1, waiting for transfers between devices, exchanged(): return lax.all_to_all(x, axis, 0, 0, axis_index_groups=groups, tiled=True)  4.16 us
    all_to_all x1, waiting for transfers between devices, on_device(): panels = lax.all_to_all(panel, 'row', 0, 0, tiled=True)  3.85 us
    all_to_all x1, starting transfers between devices, exchanged(): return lax.all_to_all(x, axis, 0, 0, axis_index_groups=groups, tiled=True)  3.69 us
    pallas_call x1, Pallas kernels, on_device(): kernel(second_body, (SMEM, VMEM, VMEM, VMEM, VMEM), (((1032, 128), F32),...  3.63 us
  transfers between devices with their start and end apart: 5, of which 2 were waited for; matrix products, arithmetic and copies ran while one was open for 1% of the time, Pallas kernels for 9%

profile of v8, /device:TPU:1, one launch (start us, length us, event | category | flops | bytes accessed | tf_op | source)
XLA Modules:
  0.0 143.1 jit_solution(9587941467889038999)
XLA Ops:
  7.2 0.0 all-gather.3.cloned.1.call-start
  7.2 3.0 %shard_map.104 = (f32[144,256]{1,0:T(8,128)}, s32[12,128]{1,0:T(8,128)}, s32[12,128]{1,0:T(8,128)}, bf16[384,256]{1,0:T(8,128)(2,1)}) custom-call(s32[12,128]{1,0:T(8,128)} %bitcast.14, s32[12,128]{1,0:T(8,128)} %bitcast.9, f32[9,9,4,128]{3,2,1,0:T(4,128)} %tiles.1), custom_call_target="tpu_custom_call" | custom-call | tf_op jit(solution)/shard_map/pallas_call | solution.py:426
  10.2 0.0 all-gather.3.cloned.1.call-update
  10.2 1.7 %shard_map.106 = (f32[32,16,128]{2,1,0:T(8,128)}, f32[24,128]{1,0:T(8,128)}, f32[8,40,128]{2,1,0:T(8,128)}) custom-call(f32[2,32,48]{2,1,0:T(8,128)} %bitcast.8, f32[1,32,48]{2,1,0:T(8,128)} %bitcast.11, f32[2,2,4,128]{3,2,1,0:T(4,128)} %d1.3), custom_call_target="tpu_custom_call" | custom-call | tf_op jit(solution)/shard_map/pallas_call | solution.py:420
  11.9 19.1 %all_to_all.30.mine = f32[8,40,128]{2,1,0:T(8,128)S(1)} all-to-all(f32[8,40,128]{2,1,0:T(8,128)} %get-tuple-element.22), channel_id=1, replica_groups={{0,2,4,6,8,10,12,14},{1,3,5,7,9,11,13,15},{16,18,20,22,24,26,28,30},{17..., dimensions={0} | all-to-all | bytes 327680 | tf_op jit(solution)/shard_map/all_to_all | solution.py:399
  31.0 0.0 copy-start.3
  31.0 9.7 %all-to-all-start = ((f32[32,16,128]{2,1,0:T(8,128)}), f32[32,16,128]{2,1,0:T(8,128)S(1)}, u32[]{:S(2)}, u32[]{:S(2)}) async-start(f32[32,16,128]{2,1,0:T(8,128)} %get-tuple-element.20), calls=%async_computation | async-start | bytes 524288 | tf_op jit(solution)/shard_map/all_to_all | solution.py:440
  40.7 4.7 %collective-permute-start = (f32[8,40,128]{2,1,0:T(8,128)S(1)}, f32[8,40,128]{2,1,0:T(8,128)S(1)}, u32[]{:S(2)}, u32[]{:S(2)}) collective-permute-start(f32[8,40,128]{2,1,0:T(8,128)S(1)} %all_to_all.30.mine), channel_id=1, source_target_pairs={{0,1},{1,0},{2,3},{3,2},{4,5},{5,4},{6,7},{7,6},{8,9},{9,8},{10,11... | collective-permute-start | bytes 491528 | tf_op jit(solution)/shard_map/ppermute | solution.py:403
  45.4 1.9 %shard_map.105.later = s32[2,384]{1,0:T(2,128)} custom-call(s32[12,128]{1,0:T(8,128)} %bitcast.10), custom_call_target="tpu_custom_call" | custom-call | tf_op jit(solution)/shard_map/pallas_call | solution.py:441
  47.3 0.0 collective-permute-done.other
  47.3 0.0 copy-start.5
  47.3 3.9 %all-to-all-done.panels = f32[32,16,128]{2,1,0:T(8,128)S(1)} async-done(((f32[32,16,128]{2,1,0:T(8,128)}), f32[32,16,128]{2,1,0:T(8,128)S(1)}, u32[]{:S(2)}, u32[]{:S(2)}) %all-to-all-start) | async-done | bytes 262176 | tf_op jit(solution)/shard_map/all_to_all | solution.py:440
  51.2 0.0 copy-start.1
  51.2 0.0 copy-done.3
  51.2 0.0 copy-done.5
  51.2 0.7 copy-done.1
  51.9 3.6 %shard_map.107 = (f32[1032,128]{1,0:T(8,128)}, f32[8,40,128]{2,1,0:T(8,128)}, f32[32,128]{1,0:T(8,128)}) custom-call(s32[2,384]{1,0:T(2,128)} %shard_map.105.later, f32[32,16,128]{2,1,0:T(8,128)} %copy-done.1, f32[24,128]{1,0:T(8,128)} %get-tuple-element.21.near, f32[8,40,128]{2,1,0:T(8,128)} %copy-done.3, f32[8,40,128]{2,1,0:T(8,128)} %copy-done.5), custom_call_target="tpu_custom_call" | custom-call | tf_op jit(solution)/shard_map/pallas_call | solution.py:444
  55.5 11.6 %all_to_all.31 = f32[8,40,128]{2,1,0:T(8,128)S(1)} all-to-all(f32[8,40,128]{2,1,0:T(8,128)} %get-tuple-element.23), channel_id=1, replica_groups={{0,64,128,192,256,320,384,448},{16,80,144,208,272,336,400,464},{32,96,1..., dimensions={0} | all-to-all | bytes 327680 | tf_op jit(solution)/shard_map/all_to_all | solution.py:399
  67.1 0.9 broadcast_in_dim.3
  68.0 3.7 %all-to-all-start.3 = ((f32[4,8,40,128]{3,2,1,0:T(8,128)}), f32[4,8,40,128]{3,2,1,0:T(8,128)S(1)}, u32[]{:S(2)}, u32[]{:S(2)}) async-start(f32[4,8,40,128]{3,2,1,0:T(8,128)} %broadcast_in_dim.3), calls=%async_computation.3 | async-start | bytes 1310720 | tf_op jit(solution)/shard_map/all_to_all | solution.py:399
  71.7 3.5 %shard_map.108.second_hbm = f32[2056,128]{1,0:T(8,128)} custom-call(s32[1536]{0:T(1024)} %bitcast.13, f32[32,16,128]{2,1,0:T(8,128)} %copy-done.1), custom_call_target="tpu_custom_call" | custom-call | tf_op jit(solution)/shard_map/pallas_call | solution.py:452
  75.1 4.2 %all-to-all-done.3.folds = f32[4,8,40,128]{3,2,1,0:T(8,128)S(1)} async-done(((f32[4,8,40,128]{3,2,1,0:T(8,128)}), f32[4,8,40,128]{3,2,1,0:T(8,128)S(1)}, u32[]{:S(2)}, u32[]{:S(2)}) %all-to-all-start.3) | async-done | bytes 655392 | tf_op jit(solution)/shard_map/all_to_all | solution.py:399
  79.3 0.0 copy-start
  79.3 0.0 all-gather.3.cloned.1.call-done
  79.3 0.9 copy-done
  80.2 5.0 %shard_map.109 = (f32[2048,128]{1,0:T(8,128)}, f32[4,64,128]{2,1,0:T(8,128)}) custom-call(s32[1536]{0:T(1024)} %bitcast.12, f32[4,8,40,128]{3,2,1,0:T(8,128)} %copy-done, f32[2056,128]{1,0:T(8,128)} %shard_map.108.second_hbm, f32[16,144,256]{2,1,0:T(8,128)} %bitcast.7, f32[32,128]{1,0:T(8,128)} %get-tuple-element.26.extra, bf16[96,128]{1,0:T(8,128)(2,1)} %constant.4.clone.choice), custom_call_target="tpu_custom_call" | custom-call | tf_op jit(solution)/shard_map/pallas_call | solution.py:454
  85.2 13.7 %all_to_all.32.got = f32[4,64,128]{2,1,0:T(8,128)} all-to-all(f32[4,64,128]{2,1,0:T(8,128)} %get-tuple-element.27), channel_id=1, replica_groups={{1,17,32,48},{2,18,64,80},{3,19,96,112},{4,20,128,144},{5,21,160,176},{..., dimensions={0} | all-to-all | bytes 262144 | tf_op jit(solution)/shard_map/all_to_all | solution.py:399
  98.9 2.3 %shard_map.110 = (f32[48,384]{1,0:T(8,128)}, f32[8,72,128]{2,1,0:T(8,128)}, f32[16,128]{1,0:T(8,128)}) custom-call(f32[4,64,128]{2,1,0:T(8,128)} %all_to_all.32.got, bf16[512,512]{1,0:T(8,128)(2,1)} %constant.5.clone.order, bf16[384,256]{1,0:T(8,128)(2,1)} %get-tuple-element.28.table), custom_call_target="tpu_custom_call" | custom-call | tf_op jit(solution)/shard_map/pallas_call | solution.py:462
  101.2 28.1 %all_to_all.33.mine = f32[8,72,128]{2,1,0:T(8,128)S(1)} all-to-all(f32[8,72,128]{2,1,0:T(8,128)} %get-tuple-element.29), channel_id=1, replica_groups={{0,2,4,6,8,10,12,14},{1,3,5,7,9,11,13,15},{16,18,20,22,24,26,28,30},{17..., dimensions={0} | all-to-all | bytes 589824 | tf_op jit(solution)/shard_map/all_to_all | solution.py:399
  129.2 0.0 copy-start.2
  129.2 1.9 %collective-permute-start.1 = (f32[8,72,128]{2,1,0:T(8,128)S(1)}, f32[8,72,128]{2,1,0:T(8,128)S(1)}, u32[]{:S(2)}, u32[]{:S(2)}) collective-permute-start(f32[8,72,128]{2,1,0:T(8,128)S(1)} %all_to_all.33.mine), channel_id=1, source_target_pairs={{0,1},{1,0},{2,3},{3,2},{4,5},{5,4},{6,7},{7,6},{8,9},{9,8},{10,11... | collective-permute-start | bytes 884744 | tf_op jit(solution)/shard_map/ppermute | solution.py:403
  131.2 1.6 %shard_map.111 = (f32[2,9,4,128]{3,2,1,0:T(4,128)}, f32[1,9,4,128]{3,2,1,0:T(4,128)}) custom-call(f32[48,384]{1,0:T(8,128)} %get-tuple-element.33.whole), custom_call_target="tpu_custom_call" | custom-call | tf_op jit(solution)/shard_map/pallas_call | solution.py:468
  132.8 0.0 collective-permute-done.1.other
  132.8 0.0 copy-start.4
  132.8 0.0 copy-done.2
  132.8 0.7 copy-done.4
  133.5 2.8 %shard_map.112 = (f32[2,11,4,128]{3,2,1,0:T(4,128)}, f32[1,12,4,128]{3,2,1,0:T(4,128)}) custom-call(f32[8,72,128]{2,1,0:T(8,128)} %copy-done.2, f32[8,72,128]{2,1,0:T(8,128)} %copy-done.4, f32[2048,128]{1,0:T(8,128)} %get-tuple-element.30.right, f32[1032,128]{1,0:T(8,128)} %get-tuple-element.31.later, f32[16,128]{1,0:T(8,128)} %get-tuple-element.32.own, ...), custom_call_target="tpu_custom_call" | custom-call | tf_op jit(solution)/shard_map/pallas_call | solution.py:470
Async XLA Ops:
  7.2 72.1 %all-gather.3.cloned.1.call-start = ((), (), s32[]{:S(2)}) async-start(), calls=%async_computation.6 | async-start | bytes 2506752 | tf_op jit(solution)/shard_map/all_gather | solution.py:437
  31.0 20.2 %copy-start.3 = (f32[8,40,128]{2,1,0:T(8,128)}, f32[8,40,128]{2,1,0:T(8,128)S(1)}, u32[]{:S(2)}) copy-start(f32[8,40,128]{2,1,0:T(8,128)S(1)} %all_to_all.30.mine) | copy-start | bytes 491524
  31.0 20.2 %all-to-all-start = ((f32[32,16,128]{2,1,0:T(8,128)}), f32[32,16,128]{2,1,0:T(8,128)S(1)}, u32[]{:S(2)}, u32[]{:S(2)}) async-start(f32[32,16,128]{2,1,0:T(8,128)} %get-tuple-element.20), calls=%async_computation | async-start | bytes 524288 | tf_op jit(solution)/shard_map/all_to_all | solution.py:440
  40.7 6.6 %collective-permute-start = (f32[8,40,128]{2,1,0:T(8,128)S(1)}, f32[8,40,128]{2,1,0:T(8,128)S(1)}, u32[]{:S(2)}, u32[]{:S(2)}) collective-permute-start(f32[8,40,128]{2,1,0:T(8,128)S(1)} %all_to_all.30.mine), channel_id=1, source_target_pairs={{0,1},{1,0},{2,3},{3,2},{4,5},{5,4},{6,7},{7,6},{8,9},{9,8},{10,11... | collective-permute-start | bytes 491528 | tf_op jit(solution)/shard_map/ppermute | solution.py:403
  47.3 3.9 %copy-start.5 = (f32[8,40,128]{2,1,0:T(8,128)}, f32[8,40,128]{2,1,0:T(8,128)S(1)}, u32[]{:S(2)}) copy-start(f32[8,40,128]{2,1,0:T(8,128)S(1)} %collective-permute-done.other) | copy-start | bytes 491524
  51.2 0.7 copy-start.1
  68.0 11.3 %all-to-all-start.3 = ((f32[4,8,40,128]{3,2,1,0:T(8,128)}), f32[4,8,40,128]{3,2,1,0:T(8,128)S(1)}, u32[]{:S(2)}, u32[]{:S(2)}) async-start(f32[4,8,40,128]{3,2,1,0:T(8,128)} %broadcast_in_dim.3), calls=%async_computation.3 | async-start | bytes 1310720 | tf_op jit(solution)/shard_map/all_to_all | solution.py:399
  79.3 0.9 copy-start
  129.2 3.5 %copy-start.2 = (f32[8,72,128]{2,1,0:T(8,128)}, f32[8,72,128]{2,1,0:T(8,128)S(1)}, u32[]{:S(2)}) copy-start(f32[8,72,128]{2,1,0:T(8,128)S(1)} %all_to_all.33.mine) | copy-start | bytes 884740
  129.2 3.5 %collective-permute-start.1 = (f32[8,72,128]{2,1,0:T(8,128)S(1)}, f32[8,72,128]{2,1,0:T(8,128)S(1)}, u32[]{:S(2)}, u32[]{:S(2)}) collective-permute-start(f32[8,72,128]{2,1,0:T(8,128)S(1)} %all_to_all.33.mine), channel_id=1, source_target_pairs={{0,1},{1,0},{2,3},{3,2},{4,5},{5,4},{6,7},{7,6},{8,9},{9,8},{10,11... | collective-permute-start | bytes 884744 | tf_op jit(solution)/shard_map/ppermute | solution.py:403
  132.8 0.7 copy-start.4
Sparse Core Ops, SparseCore 0:
  10.3 49.0 all-gather.2
